TPU v7x, 16 devices: a 4x2x1 block of a 4x4x8 slice. The times are simulated.
16 devices in a mesh: dp: 2 (over y, z), tp: 8 (over x, core).
Axes of the slice: x: 4, y: 2, z: 1, core: 2. Of those that a mesh axis runs over, the one named last changes fastest.
The devices are a block of a 4x4x8 slice.
Arguments:
- x_steps: bfloat16 [3, 256, 4096], P(None, 'dp'), parts along dimension 1
- seq_lens: int32 [256], P(('dp', 'tp')), parts along dimension 0
- k_cache: bfloat16 [256, 3072, 128], P(('dp', 'tp')), parts along dimension 0
- v_cache: bfloat16 [256, 3072, 128], P(('dp', 'tp')), parts along dimension 0
- ln_gain: bfloat16 [4096], replicated
- ln_bias: bfloat16 [4096], replicated
- w_q: bfloat16 [4096, 4096], P(None, 'tp')
- b_q: bfloat16 [4096], P('tp')
- w_kv: bfloat16 [4096, 256], replicated
- b_kv: bfloat16 [256], replicated
- w_out: bfloat16 [4096, 4096], P('tp')
- b_out: bfloat16 [4096], replicated
Outputs:
- output 1: bfloat16 [3, 256, 4096], P(None, 'dp'), parts along dimension 1
- output 2: bfloat16 [256, 3072, 128], P(('dp', 'tp')), parts along dimension 0
- output 3: bfloat16 [256, 3072, 128], P(('dp', 'tp')), parts along dimension 0
There are 2 independent parts. A program takes and returns all parts, laid end to end along the dimension named above; an argument that names none is the same for every part.
All inputs are finite; a program needn't handle non-finite values.
Results may differ from a plain program's by a relative error of at most 0.00996645.
Values are sent between devices in bfloat16 or wider.
A program may use at most 768 MiB of HBM per device.

v0:
```python
import functools
import math

import jax
import jax.numpy as jnp
from jax import lax
from jax.experimental import pallas as pl
from jax.experimental.pallas import tpu as pltpu
from jax.sharding import PartitionSpec as P

LN_EPS = 1e-5
KEY_TILE = 256
FRESH_ROWS = 16
VMEM_LIMIT = 60 * 1024 * 1024


def layer_norm(x_rows, ln_gain, ln_bias):
    x_float = x_rows.astype(jnp.float32)
    row_mean = jnp.mean(x_float, axis=-1, keepdims=True)
    centered = x_float - row_mean
    row_var = jnp.mean(centered * centered, axis=-1, keepdims=True)
    scaled = centered * lax.rsqrt(row_var + LN_EPS)
    return (scaled * ln_gain.astype(jnp.float32) + ln_bias.astype(jnp.float32)).astype(jnp.bfloat16)


def attend_one(q_rows, k_ref, v_ref, score_ref, seq_len, fresh_k, fresh_v, fresh_mask):
    rows, depth = q_rows.shape
    length = k_ref.shape[0]
    to_log2 = depth ** -0.5 * math.log2(math.e)
    contract_last = (((1,), (1,)), ((), ()))
    new_scores = lax.dot_general(q_rows, fresh_k, contract_last, preferred_element_type=jnp.float32)
    new_scores = jnp.where(fresh_mask, new_scores, -jnp.inf)
    best = None
    lane = lax.broadcasted_iota(jnp.int32, (rows, KEY_TILE), 1)
    for start in range(0, length, KEY_TILE):
        tile = lax.dot_general(q_rows, k_ref[start:start + KEY_TILE, :], contract_last, preferred_element_type=jnp.float32)
        tile = jnp.where(lane < seq_len - start, tile, -jnp.inf)
        score_ref[:, start:start + KEY_TILE] = tile
        best = tile if best is None else jnp.maximum(best, tile)
    top = jnp.maximum(jnp.max(best, axis=-1, keepdims=True), jnp.max(new_scores, axis=-1, keepdims=True))
    new_weights = jnp.exp2((new_scores - top) * to_log2)
    numerator = jnp.dot(new_weights.astype(jnp.bfloat16), fresh_v, preferred_element_type=jnp.float32)
    total = None
    for start in range(0, length, KEY_TILE):
        weights = jnp.exp2((score_ref[:, start:start + KEY_TILE] - top) * to_log2)
        total = weights if total is None else total + weights
        numerator = numerator + jnp.dot(weights.astype(jnp.bfloat16), v_ref[start:start + KEY_TILE, :], preferred_element_type=jnp.float32)
    denominator = jnp.sum(total, axis=-1, keepdims=True) + jnp.sum(new_weights, axis=-1, keepdims=True)
    return numerator / denominator


def attention_kernel(n_steps, len_ref, q_ref, fk_ref, fv_ref, k_hbm, v_hbm, out_ref, k_out, v_out, k_buf, v_buf, score_buf, sems, out_sems):
    n_seqs, rows, depth = q_ref.shape
    length = k_buf.shape[1]

    def fetch(b):
        return (pltpu.make_async_copy(k_hbm.at[b], k_buf.at[b], sems.at[0, b]),
                pltpu.make_async_copy(v_hbm.at[b], v_buf.at[b], sems.at[1, b]))

    def store(b):
        return (pltpu.make_async_copy(k_buf.at[b], k_out.at[b], out_sems.at[0, b]),
                pltpu.make_async_copy(v_buf.at[b], v_out.at[b], out_sems.at[1, b]))

    def patch(b, buf, fresh):
        start = pl.multiple_of(jnp.minimum(len_ref[b] // 8 * 8, length - WINDOW), 8)
        offset = len_ref[b] - start
        row = lax.broadcasted_iota(jnp.int32, (WINDOW, depth), 0)
        window = buf[b, pl.ds(start, WINDOW), :].astype(jnp.float32)
        for s in range(n_steps):
            window = jnp.where(row == offset + s, fresh[b, s:s + 1, :].astype(jnp.float32), window)
        buf[b, pl.ds(start, WINDOW), :] = window.astype(buf.dtype)

    for b in range(n_seqs):
        for copy in fetch(b):
            copy.start()
    shape = (rows, FRESH_ROWS)
    step_of_row = lax.broadcasted_iota(jnp.int32, shape, 0) // (rows // n_steps)
    fresh_mask = lax.broadcasted_iota(jnp.int32, shape, 1) <= step_of_row

    def body(i, carry):
        for j in range(2):
            b = 2 * i + j
            for copy in fetch(b):
                copy.wait()
            patch(b, k_buf, fk_ref)
            patch(b, v_buf, fv_ref)
            for copy in store(b):
                copy.start()
        for j in range(2):
            b = 2 * i + j
            out = attend_one(q_ref[b], k_buf.at[b], v_buf.at[b], score_buf.at[j], len_ref[b], fk_ref[b], fv_ref[b], fresh_mask)
            out_ref[b] = out.astype(out_ref.dtype)
        return carry

    lax.fori_loop(0, n_seqs // 2, body, 0)
    for b in range(n_seqs):
        for copy in store(b):
            copy.wait()


WINDOW = 16


def attention(q_rows, seq_lens, k_cache, v_cache, fresh_k, fresh_v, n_steps):
    n_seqs, rows, depth = q_rows.shape
    length = k_cache.shape[1]
    pad = ((0, 0), (0, FRESH_ROWS - n_steps), (0, 0))
    vmem = pl.BlockSpec(memory_space=pltpu.VMEM)
    hbm = pl.BlockSpec(memory_space=pl.ANY)
    return pl.pallas_call(
        functools.partial(attention_kernel, n_steps),
        out_shape=[jax.ShapeDtypeStruct(q_rows.shape, jnp.bfloat16), jax.ShapeDtypeStruct(k_cache.shape, k_cache.dtype), jax.ShapeDtypeStruct(v_cache.shape, v_cache.dtype)],
        in_specs=[pl.BlockSpec(memory_space=pltpu.SMEM), vmem, vmem, vmem, hbm, hbm],
        out_specs=[vmem, hbm, hbm],
        scratch_shapes=[
            pltpu.VMEM((n_seqs, length, depth), jnp.bfloat16),
            pltpu.VMEM((n_seqs, length, depth), jnp.bfloat16),
            pltpu.VMEM((2, rows, length), jnp.float32),
            pltpu.SemaphoreType.DMA((2, n_seqs)),
            pltpu.SemaphoreType.DMA((2, n_seqs)),
        ],
        compiler_params=pltpu.CompilerParams(vmem_limit_bytes=VMEM_LIMIT),
        cost_estimate=pl.CostEstimate(flops=4 * n_seqs * rows * length * depth, bytes_accessed=8 * n_seqs * length * depth, transcendentals=n_seqs * rows * length),
    )(seq_lens, q_rows, jnp.pad(fresh_k, pad), jnp.pad(fresh_v, pad), k_cache, v_cache)


def solution(mesh):
    tp_size = mesh.shape['tp']

    def local_block(x_steps, seq_lens, k_cache, v_cache, ln_gain, ln_bias, w_q, b_q, w_kv, b_kv, w_out, b_out):
        n_steps, group_rows, width = x_steps.shape
        local_rows, _, head_dim = k_cache.shape
        q_part_width = w_q.shape[1]
        n_heads = q_part_width * tp_size // head_dim
        row_start = lax.axis_index('tp') * local_rows
        normed = layer_norm(x_steps, ln_gain, ln_bias)
        q_part = (jnp.einsum('sbk,kn->sbn', normed, w_q, preferred_element_type=jnp.float32) + b_q.astype(jnp.float32)).astype(jnp.bfloat16)
        q_local = lax.all_to_all(q_part, 'tp', 1, 2, tiled=True)
        own_normed = lax.dynamic_slice_in_dim(normed, row_start, local_rows, axis=1)
        kv_rows = (jnp.einsum('sbk,kn->bsn', own_normed, w_kv, preferred_element_type=jnp.float32) + b_kv.astype(jnp.float32)).astype(jnp.bfloat16)
        fresh_k, fresh_v = kv_rows[:, :, :head_dim], kv_rows[:, :, head_dim:]
        q_rows = q_local.reshape(n_steps, local_rows, n_heads, head_dim).transpose(1, 0, 2, 3).reshape(local_rows, n_steps * n_heads, head_dim)
        attn, k_out, v_out = attention(q_rows, seq_lens, k_cache, v_cache, fresh_k, fresh_v, n_steps)
        attn = attn.reshape(local_rows, n_steps, n_heads * head_dim).transpose(1, 0, 2)
        attn_heads = lax.all_to_all(attn, 'tp', 2, 1, tiled=True)
        proj_part = jnp.einsum('sbk,kn->sbn', attn_heads, w_out, preferred_element_type=jnp.float32).astype(jnp.bfloat16)
        proj_sum = lax.psum(proj_part, 'tp')
        y_steps = (x_steps.astype(jnp.float32) + proj_sum.astype(jnp.float32) + b_out.astype(jnp.float32)).astype(jnp.bfloat16)
        return y_steps, k_out, v_out

    row_spec = P(('dp', 'tp'), None, None)
    return jax.shard_map(
        local_block,
        mesh=mesh,
        in_specs=(P(None, 'dp', None), P(('dp', 'tp')), row_spec, row_spec, P(None), P(None), P(None, 'tp'), P('tp'), P(None, None), P(None), P('tp', None), P(None)),
        out_specs=(P(None, 'dp', None), row_spec, row_spec),
        check_vma=False,
    )
```

profile of v0, /device:TPU:113, one launch (start us, length us, event | category | flops | bytes accessed | tf_op | source)
XLA Modules:
  0.0 165.4 jit_solution(8248135891208577523)
XLA Ops:
  7.2 0.0 copy-start
  7.2 0.0 copy-start.2
  7.2 0.0 copy-start.4
  7.2 0.0 copy-start.5
  7.2 0.0 copy-start.7
  7.2 2.5 %convert_reduce_fusion = f32[3,128]{1,0:T(4,128)S(1)} fusion(bf16[3,128,4096]{2,1,0:T(8,128)(2,1)} %param.12), kind=kLoop, calls=%fused_computation.2 | loop fusion | flops 3145344 | bytes 3147264 | tf_op jit(solution)/shard_map/reduce_sum | solution.py:19
  9.8 0.4 copy-done.2
  10.2 0.0 copy-start.8
  10.2 1.0 fusion.2
  11.2 0.0 copy-done.4
  11.2 0.0 copy-done.5
  11.2 0.0 copy-done.7
  11.2 1.6 fusion.5
  12.9 0.0 copy-done.8
  12.9 0.0 copy-start.3
  12.9 0.0 copy-start.9
  12.9 1.8 %fusion.16 = bf16[3,128,512]{2,1,0:T(8,128)(2,1)S(1)} fusion(bf16[3,128,4096]{2,1,0:T(8,128)(2,1)S(1)} %fusion.5, bf16[4096,512]{1,0:T(8,128)(2,1)S(1)} %copy-done.8, f32[512]{0:T(512)S(1)} %convert_element_type.47), kind=kOutput, calls=%fused_computation.18 | convolution fusion | flops 1611005952 | bytes 7735296 | tf_op jit(solution)/shard_map/sbk,kn->sbn/dot_general | solution.py:137
  14.7 0.0 copy-done.3
  14.8 1.1 copy.34
  15.9 6.0 %all-to-all-start = ((bf16[3,128,512]{2,0,1:T(4,128)(2,1)}), bf16[3,128,512]{2,0,1:T(4,128)(2,1)S(1)}, u32[]{:S(2)}, u32[]{:S(2)}) async-start(bf16[3,128,512]{2,0,1:T(4,128)(2,1)} %copy.34), calls=%async_computation | async-start | bytes 1048576 | tf_op jit(solution)/shard_map/all_to_all | solution.py:138
  21.9 0.0 all-reduce.4.cloned.1.call-start
  21.9 0.0 copy-done.9
  21.9 0.0 copy-done
  21.9 1.5 fusion.11
  23.5 0.7 pad.7.fk_ref
  24.1 0.6 pad.8.fv_ref
  24.8 6.3 %all-to-all-done = bf16[3,128,512]{2,0,1:T(4,128)(2,1)S(1)} async-done(((bf16[3,128,512]{2,0,1:T(4,128)(2,1)}), bf16[3,128,512]{2,0,1:T(4,128)(2,1)S(1)}, u32[]{:S(2)}, u32[]{:S(2)}) %all-to-all-start) | async-done | bytes 393248 | tf_op jit(solution)/shard_map/all_to_all | solution.py:138
  31.0 0.3 copy.35
  31.3 1.0 reshape.33
  32.3 20.2 %shard_map.139 = (bf16[16,96,128]{2,1,0:T(8,128)(2,1)}, bf16[16,3072,128]{2,1,0:T(8,128)(2,1)}, bf16[16,3072,128]{2,1,0:T(8,128)(2,1)}) custom-call(s32[16]{0:T(128)} %len_ref.1, bf16[16,96,128]{2,1,0:T(8,128)(2,1)} %bitcast.39, bf16[16,16,128]{2,1,0:T(8,128)(2,1)} %pad.7.fk_ref, bf16[16,16,128]{2,1,0:T(8,128)(2,1)} %pad.8.fv_ref, ...), custom_call_target="tpu_custom_call" | custom-call | flops 2415919104 | bytes 50331648 | tf_op jit(solution)/shard_map/pallas_call | solution.py:110
  52.5 1.4 reshape.35
  53.9 4.7 %copy.38 = bf16[3,16,4096]{1,0,2:T(4,128)(2,1)} copy(bf16[3,16,4096]{2,0,1:T(4,128)(2,1)S(1)} %bitcast.37) | data formatting | bytes 786432 | tf_op jit(solution)/shard_map/transpose | solution.py:144
  58.6 6.6 %reshape.39 = bf16[8,2,12288]{2,1,0:T(2,128)(2,1)S(1)} reshape(bf16[4096,3,16]{2,1,0:T(4,128)(2,1)} %bitcast.35) | data formatting | bytes 786432
  65.2 11.7 %all_to_all.33 = bf16[8,2,12288]{2,1,0:T(2,128)(2,1)S(1)} all-to-all(bf16[8,2,12288]{2,1,0:T(2,128)(2,1)S(1)} %reshape.39), channel_id=1, replica_groups=mesh['dp'=2,'tp'=8] {'tp'}, dimensions={0} | all-to-all | bytes 786432 | tf_op jit(solution)/shard_map/all_to_all | solution.py:145
  76.9 5.6 %reshape.40 = bf16[4096,3,16]{2,1,0:T(4,128)(2,1)} reshape(bf16[8,2,12288]{2,1,0:T(2,128)(2,1)S(1)} %all_to_all.33) | data formatting | bytes 786432
  82.5 5.3 %copy.42 = bf16[3,16,8,512]{3,1,2,0:T(8,128)(2,1)S(1)} copy(bf16[3,16,8,512]{1,0,3,2:T(4,128)(2,1)} %bitcast.36) | data formatting | bytes 786432 | tf_op jit(solution)/shard_map/all_to_all | solution.py:145
  87.8 0.0 copy-start.6
  87.8 5.7 %convolution_convert_fusion = bf16[3,128,4096]{2,1,0:T(8,128)(2,1)} fusion(bf16[3,128,512]{2,1,0:T(8,128)(2,1)S(1)} %bitcast.40, bf16[512,4096]{1,0:T(8,128)(2,1)} %param.22), kind=kOutput, calls=%fused_computation.11 | convolution fusion | flops 1612185600 | bytes 7733248 | tf_op jit(solution)/shard_map/sbk,kn->sbn/dot_general | solution.py:146
  93.5 0.1 all-reduce.4.cloned.1.call-update
  93.6 0.0 copy-done.6
  93.6 0.0 copy-start.1
  93.6 59.1 %all-reduce.4.cloned.1.call-done = bf16[3,128,4096]{2,1,0:T(8,128)(2,1)} async-done(((bf16[3,128,4096]{2,1,0:T(8,128)(2,1)}), bf16[3,128,4096]{2,1,0:T(8,128)(2,1)}) %all-reduce.4.cloned.1.call-update) | async-done | bytes 3145744 | tf_op jit(solution)/shard_map/psum | solution.py:147
  152.7 5.8 %fusion.7 = bf16[3,128,4096]{2,1,0:T(8,128)(2,1)} fusion(bf16[3,128,4096]{2,1,0:T(8,128)(2,1)} %param.12, bf16[3,128,4096]{2,1,0:T(8,128)(2,1)} %all-reduce.4.cloned.1.call-done, f32[4096]{0:T(1024)S(1)} %convert_element_type.54), kind=kLoop, calls=%fused_computation.10 | loop fusion | flops 7864320 | bytes 9453568 | tf_op jit(solution)/shard_map/convert_element_type | solution.py:148
  158.5 0.0 copy-done.1
  (9 shorter events, 0.1 us)
Async XLA Ops:
  7.2 14.7 %copy-start = (bf16[4096,256]{1,0:T(8,128)(2,1)S(1)}, bf16[4096,256]{1,0:T(8,128)(2,1)}, u32[]{:S(2)}) copy-start(bf16[4096,256]{1,0:T(8,128)(2,1)} %param.20) | copy-start | bytes 6291460
  7.2 3.0 %copy-start.2 = (bf16[3,128,4096]{2,1,0:T(8,128)(2,1)S(1)}, bf16[3,128,4096]{2,1,0:T(8,128)(2,1)}, u32[]{:S(2)}) copy-start(bf16[3,128,4096]{2,1,0:T(8,128)(2,1)} %param.12) | copy-start | bytes 9437188
  7.2 3.9 %copy-start.4 = (bf16[4096]{0:T(1024)(128)(2,1)S(1)}, bf16[4096]{0:T(1024)(128)(2,1)}, u32[]{:S(2)}) copy-start(bf16[4096]{0:T(1024)(128)(2,1)} %param.16) | copy-start | bytes 24580
  7.2 4.0 %copy-start.5 = (bf16[4096]{0:T(1024)(128)(2,1)S(1)}, bf16[4096]{0:T(1024)(128)(2,1)}, u32[]{:S(2)}) copy-start(bf16[4096]{0:T(1024)(128)(2,1)} %param.17) | copy-start | bytes 24580
  7.2 4.0 %copy-start.7 = (bf16[512]{0:T(512)(128)(2,1)S(1)}, bf16[512]{0:T(512)(128)(2,1)}, u32[]{:S(2)}) copy-start(bf16[512]{0:T(512)(128)(2,1)} %param.19) | copy-start | bytes 3076
  10.2 2.7 %copy-start.8 = (bf16[4096,512]{1,0:T(8,128)(2,1)S(1)}, bf16[4096,512]{1,0:T(8,128)(2,1)}, u32[]{:S(2)}) copy-start(bf16[4096,512]{1,0:T(8,128)(2,1)} %param.18) | copy-start | bytes 12582916
  12.9 1.9 %copy-start.3 = (bf16[3,128,4096]{2,1,0:T(8,128)(2,1)}, bf16[3,128,4096]{2,1,0:T(8,128)(2,1)S(1)}, u32[]{:S(2)}) copy-start(bf16[3,128,4096]{2,1,0:T(8,128)(2,1)S(1)} %fusion.5) | copy-start | bytes 9437188
  12.9 9.0 %copy-start.9 = (bf16[256]{0:T(256)(128)(2,1)S(1)}, bf16[256]{0:T(256)(128)(2,1)}, u32[]{:S(2)}) copy-start(bf16[256]{0:T(256)(128)(2,1)} %param.21) | copy-start | bytes 1540
  15.9 15.2 %all-to-all-start = ((bf16[3,128,512]{2,0,1:T(4,128)(2,1)}), bf16[3,128,512]{2,0,1:T(4,128)(2,1)S(1)}, u32[]{:S(2)}, u32[]{:S(2)}) async-start(bf16[3,128,512]{2,0,1:T(4,128)(2,1)} %copy.34), calls=%async_computation | async-start | bytes 1048576 | tf_op jit(solution)/shard_map/all_to_all | solution.py:138
  21.9 130.8 %all-reduce.4.cloned.1.call-start = ((), (), s32[]{:S(2)}) async-start(), calls=%async_computation.2 | async-start | bytes 6291456 | tf_op jit(solution)/shard_map/psum | solution.py:147
  87.8 5.7 %copy-start.6 = (bf16[4096]{0:T(1024)(128)(2,1)S(1)}, bf16[4096]{0:T(1024)(128)(2,1)}, u32[]{:S(2)}) copy-start(bf16[4096]{0:T(1024)(128)(2,1)} %param.23) | copy-start | bytes 24580
  93.6 65.0 %copy-start.1 = (bf16[4096,256]{1,0:T(8,128)(2,1)S(1)}, bf16[4096,256]{1,0:T(8,128)(2,1)}, u32[]{:S(2)}) copy-start(bf16[4096,256]{1,0:T(8,128)(2,1)} %param.20) | copy-start | bytes 6291460
Sparse Core Ops, SparseCore 0:
  93.7 58.9 all-reduce.3
where the time goes:
time: 168 us; the launch traced here: 165 us
  waiting for transfers between devices  65.4 us (39%)
  local copies, waits for them, and re-layouts  27.8 us (17%)
  Pallas kernels  20.2 us (12%)
  between operations  14.3 us (9%)
  blocking collectives  11.7 us (7%)
  other arithmetic  11 us (7%)
  matrix products  8.97 us (5%)
  starting transfers between devices  6.02 us (4%)
    psum x1, waiting for transfers between devices, local_block(): proj_sum = lax.psum(proj_part, 'tp')  59.1 us
    pallas_call x1, Pallas kernels, attention(): pl.pallas_call(functools.partial(attention_kernel, n_steps), out_shape=[j...  20.2 us
    unnamed x22, local copies, waits for them, and re-layouts  12.7 us
    all_to_all x1, blocking collectives, local_block(): attn_heads = lax.all_to_all(attn, 'tp', 2, 1, tiled=True)  11.7 us
    all_to_all x1, waiting for transfers between devices, local_block(): q_local = lax.all_to_all(q_part, 'tp', 1, 2, tiled=True)  6.27 us
    all_to_all x1, starting transfers between devices, local_block(): q_local = lax.all_to_all(q_part, 'tp', 1, 2, tiled=True)  6.02 us
    convert_element_type x1, other arithmetic, local_block(): (x_steps.astype(jnp.float32) + proj_sum.astype(jnp.float32) + b_out.astyp...  5.82 us
    dot_general x1, matrix products, local_block(): jnp.einsum('sbk,kn->sbn', attn_heads, w_out, preferred_element_type=jnp.f...  5.66 us
  transfers between devices with their start and end apart: 2, of which 2 were waited for; matrix products, arithmetic and copies ran while one was open for 2% of the time, Pallas kernels for 0%

commit v1 on v0

--- a/solution.py
+++ b/solution.py
@@ -49,7 +49,7 @@
     return numerator / denominator
 
 
-def attention_kernel(n_steps, len_ref, q_ref, fk_ref, fv_ref, k_hbm, v_hbm, out_ref, k_out, v_out, k_buf, v_buf, score_buf, sems, out_sems):
+def attention_kernel(n_steps, len_ref, q_ref, fk_ref, fv_ref, k_hbm, v_hbm, out_ref, k_out, v_out, k_buf, v_buf, score_buf, head_buf, sems, out_sems):
     n_seqs, rows, depth = q_ref.shape
     length = k_buf.shape[1]
 
@@ -89,10 +89,17 @@
         for j in range(2):
             b = 2 * i + j
             out = attend_one(q_ref[b], k_buf.at[b], v_buf.at[b], score_buf.at[j], len_ref[b], fk_ref[b], fv_ref[b], fresh_mask)
-            out_ref[b] = out.astype(out_ref.dtype)
+            head_buf[pl.ds(b, rows, stride=n_seqs), :] = out
         return carry
 
     lax.fori_loop(0, n_seqs // 2, body, 0)
+    n_chips, _, _, chip_width = out_ref.shape
+    chip_heads = chip_width // depth
+    for chip in range(n_chips):
+        for s in range(n_steps):
+            for h in range(chip_heads):
+                first = ((s * n_chips + chip) * chip_heads + h) * n_seqs
+                out_ref[chip, s, :, h * depth:(h + 1) * depth] = head_buf[first:first + n_seqs, :].astype(out_ref.dtype)
     for b in range(n_seqs):
         for copy in store(b):
             copy.wait()
@@ -101,7 +108,7 @@
 WINDOW = 16
 
 
-def attention(q_rows, seq_lens, k_cache, v_cache, fresh_k, fresh_v, n_steps):
+def attention(q_rows, seq_lens, k_cache, v_cache, fresh_k, fresh_v, n_steps, n_chips):
     n_seqs, rows, depth = q_rows.shape
     length = k_cache.shape[1]
     pad = ((0, 0), (0, FRESH_ROWS - n_steps), (0, 0))
@@ -109,19 +116,212 @@
     hbm = pl.BlockSpec(memory_space=pl.ANY)
     return pl.pallas_call(
         functools.partial(attention_kernel, n_steps),
-        out_shape=[jax.ShapeDtypeStruct(q_rows.shape, jnp.bfloat16), jax.ShapeDtypeStruct(k_cache.shape, k_cache.dtype), jax.ShapeDtypeStruct(v_cache.shape, v_cache.dtype)],
+        out_shape=[jax.ShapeDtypeStruct((n_chips, n_steps, n_seqs, rows // n_steps // n_chips * depth), jnp.bfloat16), jax.ShapeDtypeStruct(k_cache.shape, k_cache.dtype), jax.ShapeDtypeStruct(v_cache.shape, v_cache.dtype)],
         in_specs=[pl.BlockSpec(memory_space=pltpu.SMEM), vmem, vmem, vmem, hbm, hbm],
         out_specs=[vmem, hbm, hbm],
         scratch_shapes=[
             pltpu.VMEM((n_seqs, length, depth), jnp.bfloat16),
             pltpu.VMEM((n_seqs, length, depth), jnp.bfloat16),
             pltpu.VMEM((2, rows, length), jnp.float32),
+            pltpu.VMEM((rows * n_seqs, depth), jnp.float32),
             pltpu.SemaphoreType.DMA((2, n_seqs)),
             pltpu.SemaphoreType.DMA((2, n_seqs)),
         ],
         compiler_params=pltpu.CompilerParams(vmem_limit_bytes=VMEM_LIMIT),
         cost_estimate=pl.CostEstimate(flops=4 * n_seqs * rows * length * depth, bytes_accessed=8 * n_seqs * length * depth, transcendentals=n_seqs * rows * length),
     )(seq_lens, q_rows, jnp.pad(fresh_k, pad), jnp.pad(fresh_v, pad), k_cache, v_cache)
+
+
+MESH = pl.DeviceIdType.MESH
+N_CHIPS = 4
+
+
+def project_kernel(n_steps, a_ref, w_ref, x_ref, b_ref, y_ref, w_buf, x_buf, a_buf, p_buf, mid_buf, fin_buf,
+                   load_sems, w_sems, a_send, a_recv, f_send, f_recv, rs_send, rs_recv, ag_send, ag_recv):
+    me = lax.axis_index('tp')
+    chip, core = me // 2, me % 2
+    n_seqs = a_ref.shape[2]
+    block = 2 * n_seqs
+    own_rows, width = w_ref.shape
+    half = width // 2
+    quarter = half // 2
+
+    def chip_at(k):
+        return (chip + k) % N_CHIPS
+
+    def device(k):
+        return {'tp': chip_at(k) * 2 + core}
+
+    right, left, far, partner = device(1), device(3), device(2), {'tp': chip * 2 + 1 - core}
+
+    barrier = pltpu.get_barrier_semaphore()
+    for peer in (right, left, far, partner):
+        pl.semaphore_signal(barrier, inc=1, device_id=peer, device_id_type=MESH)
+
+    def cols(which, begin, size):
+        return pl.ds(pl.multiple_of(which * half + begin, quarter), size)
+
+    def rows_of(k):
+        return pl.ds(pl.multiple_of(chip_at(k) * block, block), block)
+
+    own_w_rows = pl.ds(pl.multiple_of(core * own_rows, own_rows), own_rows)
+    w_load = pltpu.make_async_copy(w_ref.at[:, cols(core, 0, half)], w_buf.at[own_w_rows, :], load_sems.at[0])
+    x_load = pltpu.make_async_copy(x_ref.at[:, rows_of(0), cols(core, 0, half)], x_buf, load_sems.at[1])
+    w_load.start()
+    x_load.start()
+    pl.semaphore_wait(barrier, 4)
+
+    def remote(src, dst, send, recv, to):
+        return pltpu.make_async_remote_copy(src_ref=src, dst_ref=dst, send_sem=send, recv_sem=recv, device_id=to, device_id_type=MESH)
+
+    def a_copy(s, d):
+        return remote(a_ref.at[chip_at(d), s], a_buf.at[core, chip, s], a_send.at[s, d - 1], a_recv.at[s, d - 1], device(d))
+
+    def a_forward(s, d):
+        src = a_ref.at[chip, s] if d == 0 else a_buf.at[core, chip_at(N_CHIPS - d), s]
+        return remote(src, a_buf.at[core, chip_at(N_CHIPS - d), s], f_send.at[s, d], f_recv.at[s, d], partner)
+
+    for s in range(n_steps):
+        for d in (2, 1, 3):
+            a_copy(s, d).start()
+        if s == 0:
+            w_swap = remote(w_ref.at[:, cols(1 - core, 0, half)], w_buf.at[own_w_rows, :], w_sems.at[0], w_sems.at[1], partner)
+            w_swap.start()
+    for s in range(n_steps):
+        a_forward(s, 0).start()
+        a_buf[core, chip, s] = a_ref[chip, s]
+
+    low, high = pl.ds(0, quarter), pl.ds(quarter, quarter)
+
+    def rs(s, i):
+        part = p_buf.at[s]
+        src, dst, to = (
+            (part.at[rows_of(2), low], mid_buf.at[s, 0], right),
+            (part.at[rows_of(2), high], mid_buf.at[s, 1], left),
+            (part.at[rows_of(1), high], fin_buf.at[s, 0], right),
+            (part.at[rows_of(3), low], fin_buf.at[s, 1], left),
+            (part.at[rows_of(1), low], fin_buf.at[s, 2], right),
+            (part.at[rows_of(3), high], fin_buf.at[s, 3], left),
+        )[i]
+        return remote(src, dst, rs_send.at[s, i], rs_recv.at[s, i], to)
+
+    def ag(s, i):
+        k, begin, size, to = (
+            (0, 0, half, right),
+            (0, 0, half, left),
+            (3, 0, quarter, right),
+            (1, quarter, quarter, left),
+            (0, 0, half, partner),
+            (3, 0, half, partner),
+            (1, 0, half, partner),
+            (2, 0, quarter, partner),
+            (2, quarter, quarter, partner),
+        )[i]
+        where = y_ref.at[s, rows_of(k), cols(core, begin, size)]
+        return remote(where, where, ag_send.at[s, i], ag_recv.at[s, i], to)
+
+    def partial(s):
+        for d in (1, 3, 2):
+            a_copy(s, d).wait_recv()
+            a_forward(s, d).start()
+        for d in range(N_CHIPS):
+            a_forward(s, d).wait_recv()
+        if s == 0:
+            w_load.wait()
+            w_swap.wait_recv()
+        lhs = jnp.concatenate([a_buf[c, t, s] for t in range(N_CHIPS) for c in range(2)], axis=0)
+        for n in range(0, half, 512):
+            p_buf[s, :, n:n + 512] = jnp.dot(lhs, w_buf[:, n:n + 512], preferred_element_type=jnp.float32).astype(p_buf.dtype)
+        for i in range(4):
+            rs(s, i).start()
+
+    def add_into(target, other):
+        target[...] = (target[...].astype(jnp.float32) + other[...].astype(jnp.float32)).astype(target.dtype)
+
+    def middle(s):
+        rs(s, 0).wait_recv()
+        add_into(p_buf.at[s, rows_of(1), low], mid_buf.at[s, 0])
+        rs(s, 4).start()
+        rs(s, 1).wait_recv()
+        add_into(p_buf.at[s, rows_of(3), high], mid_buf.at[s, 1])
+        rs(s, 5).start()
+
+    def finish(s):
+        for i in (2, 3, 4, 5):
+            rs(s, i).wait_recv()
+        if s == 0:
+            x_load.wait()
+        for begin, one, two in ((0, 1, 2), (quarter, 0, 3)):
+            total = p_buf[s, rows_of(0), begin:begin + quarter].astype(jnp.float32)
+            total = total + fin_buf[s, one].astype(jnp.float32)
+            total = total + fin_buf[s, two].astype(jnp.float32)
+            total = total + x_buf[s, :, begin:begin + quarter].astype(jnp.float32)
+            total = total + b_ref[:, cols(core, begin, quarter)].astype(jnp.float32)
+            y_ref[s, rows_of(0), cols(core, begin, quarter)] = total.astype(y_ref.dtype)
+        for i in (0, 1, 4):
+            ag(s, i).start()
+
+    def relay(s):
+        ag(s, 0).wait_recv()
+        ag(s, 2).start()
+        ag(s, 5).start()
+        ag(s, 1).wait_recv()
+        ag(s, 3).start()
+        ag(s, 6).start()
+
+    def last(s):
+        ag(s, 2).wait_recv()
+        ag(s, 7).start()
+        ag(s, 3).wait_recv()
+        ag(s, 8).start()
+
+    stages = (partial, middle, finish, relay, last)
+    for t in range(n_steps + len(stages) - 1):
+        for i, stage in enumerate(stages):
+            if 0 <= t - i < n_steps:
+                stage(t - i)
+    w_swap.wait_send()
+    for s in range(n_steps):
+        for i in range(4, 9):
+            ag(s, i).wait_recv()
+        for i in range(9):
+            ag(s, i).wait_send()
+        for i in range(6):
+            rs(s, i).wait_send()
+        for d in (1, 2, 3):
+            a_copy(s, d).wait_send()
+        for d in range(N_CHIPS):
+            a_forward(s, d).wait_send()
+
+
+def project(attn, w_out, x_steps, b_out):
+    n_chips, n_steps, n_seqs, chip_width = attn.shape
+    width = w_out.shape[1]
+    half, block = width // 2, 2 * n_seqs
+    vmem = pl.BlockSpec(memory_space=pltpu.VMEM)
+    hbm = pl.BlockSpec(memory_space=pl.ANY)
+    dma = pltpu.SemaphoreType.DMA
+    return pl.pallas_call(
+        functools.partial(project_kernel, n_steps),
+        out_shape=jax.ShapeDtypeStruct(x_steps.shape, jnp.bfloat16),
+        in_specs=[vmem, hbm, hbm, vmem],
+        out_specs=vmem,
+        scratch_shapes=[
+            pltpu.VMEM((chip_width, half), jnp.bfloat16),
+            pltpu.VMEM((n_steps, block, half), jnp.bfloat16),
+            pltpu.VMEM((2, n_chips, n_steps, n_seqs, chip_width), jnp.bfloat16),
+            pltpu.VMEM((n_steps, n_chips * block, half), jnp.bfloat16),
+            pltpu.VMEM((n_steps, 2, block, half // 2), jnp.bfloat16),
+            pltpu.VMEM((n_steps, 4, block, half // 2), jnp.bfloat16),
+            dma((2,)), dma((2,)),
+            dma((n_steps, 3)), dma((n_steps, 3)),
+            dma((n_steps, 4)), dma((n_steps, 4)),
+            dma((n_steps, 6)), dma((n_steps, 6)),
+            dma((n_steps, 9)), dma((n_steps, 9)),
+        ],
+        compiler_params=pltpu.CompilerParams(vmem_limit_bytes=40 * 1024 * 1024, collective_id=1, has_side_effects=True),
+        cost_estimate=pl.CostEstimate(flops=2 * n_steps * n_chips * block * chip_width * half, bytes_accessed=4 * width * chip_width, transcendentals=0),
+    )(attn, w_out, x_steps, b_out.reshape(1, width))
 
 
 def solution(mesh):
@@ -140,12 +340,8 @@
         kv_rows = (jnp.einsum('sbk,kn->bsn', own_normed, w_kv, preferred_element_type=jnp.float32) + b_kv.astype(jnp.float32)).astype(jnp.bfloat16)
         fresh_k, fresh_v = kv_rows[:, :, :head_dim], kv_rows[:, :, head_dim:]
         q_rows = q_local.reshape(n_steps, local_rows, n_heads, head_dim).transpose(1, 0, 2, 3).reshape(local_rows, n_steps * n_heads, head_dim)
-        attn, k_out, v_out = attention(q_rows, seq_lens, k_cache, v_cache, fresh_k, fresh_v, n_steps)
-        attn = attn.reshape(local_rows, n_steps, n_heads * head_dim).transpose(1, 0, 2)
-        attn_heads = lax.all_to_all(attn, 'tp', 2, 1, tiled=True)
-        proj_part = jnp.einsum('sbk,kn->sbn', attn_heads, w_out, preferred_element_type=jnp.float32).astype(jnp.bfloat16)
-        proj_sum = lax.psum(proj_part, 'tp')
-        y_steps = (x_steps.astype(jnp.float32) + proj_sum.astype(jnp.float32) + b_out.astype(jnp.float32)).astype(jnp.bfloat16)
+        attn, k_out, v_out = attention(q_rows, seq_lens, k_cache, v_cache, fresh_k, fresh_v, n_steps, N_CHIPS)
+        y_steps = project(attn, w_out, x_steps, b_out)
         return y_steps, k_out, v_out
 
     row_spec = P(('dp', 'tp'), None, None)

time: 168 us -> 91.9 us (0.55); the launches traced: 165 us -> 91.6 us
  waiting for transfers between devices: 65.4 us -> 6.27 us
  Pallas kernels: 20.2 us -> 58.5 us
  local copies, waits for them, and re-layouts: 27.8 us -> 10.5 us
  between operations: 14.3 us -> 0.85 us
  blocking collectives: 11.7 us -> 0 us
  matrix products: 8.97 us -> 3.3 us
  other arithmetic: 11 us -> 6.16 us
    psum x1 -> x0, waiting for transfers between devices: 59.1 us -> none  [local_block(): proj_sum = lax.psum(proj_part, 'tp')]
    pallas_call x0 -> x1, Pallas kernels: none -> 38.3 us  [project(): pl.pallas_call(functools.partial(project_kernel, n_steps), out_shape=jax....]
    all_to_all x1 -> x0, blocking collectives: 11.7 us -> none  [local_block(): attn_heads = lax.all_to_all(attn, 'tp', 2, 1, tiled=True)]
    unnamed x22 -> x25, local copies, waits for them, and re-layouts: 12.7 us -> 6.79 us
    convert_element_type x2 -> x0, other arithmetic: 5.82 us -> none  [the longest x1 5.82 us: local_block(): (x_steps.astype(jnp.float32) + proj_sum.astype(jnp.float32) + b_out.astyp...]
    dot_general x1 -> x0, matrix products: 5.66 us -> none  [local_block(): jnp.einsum('sbk,kn->sbn', attn_heads, w_out, preferred_element_type=jnp.f...]
    all_to_all x1 -> x0, local copies, waits for them, and re-layouts: 5.31 us -> none  [local_block(): attn_heads = lax.all_to_all(attn, 'tp', 2, 1, tiled=True)]
    transpose x1 -> x0, local copies, waits for them, and re-layouts: 4.71 us -> none  [local_block(): attn.reshape(local_rows, n_steps, n_heads * head_dim).transpose(1, 0, 2)]
  transfers between devices with their start and end apart: 2 -> 1, of which waited for: 2 -> 1; matrix products, arithmetic and copies ran while one was open for 2% -> 3% of each run, Pallas kernels for 0% -> 0%
where the time goes in v1:
time: 91.9 us; the launch traced here: 91.6 us
  Pallas kernels  58.5 us (64%)
  local copies, waits for them, and re-layouts  10.5 us (11%)
  waiting for transfers between devices  6.27 us (7%)
  other arithmetic  6.16 us (7%)
  starting transfers between devices  6.02 us (7%)
  matrix products  3.3 us (4%)
    pallas_call x1, Pallas kernels, project(): pl.pallas_call(functools.partial(project_kernel, n_steps), out_shape=jax....  38.3 us
    pallas_call x1, Pallas kernels, attention(): pl.pallas_call(functools.partial(attention_kernel, n_steps), out_shape=[j...  20.2 us
    unnamed x25, local copies, waits for them, and re-layouts  6.79 us
    all_to_all x1, waiting for transfers between devices, local_block(): q_local = lax.all_to_all(q_part, 'tp', 1, 2, tiled=True)  6.27 us
    all_to_all x1, starting transfers between devices, local_block(): q_local = lax.all_to_all(q_part, 'tp', 1, 2, tiled=True)  6.02 us
    reduce_sum x1, other arithmetic, layer_norm(): row_mean = jnp.mean(x_float, axis=-1, keepdims=True)  2.66 us
  transfers between devices with their start and end apart: 1, of which 1 were waited for; matrix products, arithmetic and copies ran while one was open for 3% of the time, Pallas kernels for 0%

profile of v1, /device:TPU:113, one launch (start us, length us, event | category | flops | bytes accessed | tf_op | source)
XLA Modules:
  0.0 91.6 jit_solution(464889649251691204)
XLA Ops:
  0.6 0.0 copy-start
  0.6 0.0 copy-start.2
  0.7 0.0 copy-start.7
  0.7 0.0 copy-start.8
  0.7 0.8 convert_element_type.34
  1.5 2.7 %convert_reduce_fusion = f32[3,128]{1,0:T(4,128)S(1)} fusion(bf16[3,128,4096]{2,1,0:T(8,128)(2,1)} %x_ref.1), kind=kLoop, calls=%fused_computation.1 | loop fusion | flops 3145344 | bytes 3147264 | tf_op jit(solution)/shard_map/reduce_sum | solution.py:19
  4.2 0.0 copy-done.2
  4.2 0.0 copy-start.10
  4.2 1.0 %fusion.2 = f32[3,128]{1,0:T(4,128)S(1)} fusion(bf16[3,128,4096]{2,1,0:T(8,128)(2,1)S(1)} %copy-done.2, f32[3,128]{1,0:T(4,128)S(1)} %broadcast_multiply_fusion), kind=kLoop, calls=%fused_computation.4 | loop fusion | flops 6291072 | bytes 3148800 | tf_op jit(solution)/shard_map/reduce_sum | solution.py:21
  5.2 0.0 copy-done.7
  5.2 0.0 copy-done.8
  5.2 1.6 %fusion.5 = bf16[3,128,4096]{2,1,0:T(8,128)(2,1)S(1)} fusion(bf16[3,128,4096]{2,1,0:T(8,128)(2,1)S(1)} %copy-done.2, f32[4096]{0:T(1024)S(1)} %convert_element_type.32, f32[4096]{0:T(1024)S(1)} %convert_element_type.31, f32[3,128]{1,0:T(4,128)S(1)} %add_rsqrt_fusion, f32[3,128]{1,0:T(4,128)S(1)} %broadcast_multiply_fusion), kind=kLoop, calls=%fused_computation.7 | loop fusion | flops 9437184 | bytes 6327296 | tf_op jit(solution)/shard_map/convert_element_type | solution.py:23
  6.9 0.0 copy-done.10
  6.9 0.0 copy-start.6
  6.9 0.0 copy-start.11
  6.9 0.0 copy-start.9
  6.9 1.8 %fusion.13 = bf16[3,128,512]{2,1,0:T(8,128)(2,1)S(1)} fusion(bf16[3,128,4096]{2,1,0:T(8,128)(2,1)S(1)} %fusion.5, bf16[4096,512]{1,0:T(8,128)(2,1)S(1)} %copy-done.10, f32[512]{0:T(512)S(1)} %convert_element_type.34), kind=kOutput, calls=%fused_computation.13 | convolution fusion | flops 1611005952 | bytes 7735296 | tf_op jit(solution)/shard_map/sbk,kn->sbn/dot_general | solution.py:337
  8.7 0.0 copy-done.6
  8.8 1.1 %copy.20 = bf16[3,128,512]{2,0,1:T(4,128)(2,1)} copy(bf16[3,128,512]{2,1,0:T(8,128)(2,1)S(1)} %fusion.13) | data formatting | bytes 786432 | tf_op jit(solution)/shard_map/convert_element_type | solution.py:337
  9.9 6.0 %all-to-all-start = ((bf16[3,128,512]{2,0,1:T(4,128)(2,1)}), bf16[3,128,512]{2,0,1:T(4,128)(2,1)S(1)}, u32[]{:S(2)}, u32[]{:S(2)}) async-start(bf16[3,128,512]{2,0,1:T(4,128)(2,1)} %copy.20), calls=%async_computation | async-start | bytes 1048576 | tf_op jit(solution)/shard_map/all_to_all | solution.py:338
  15.9 0.0 copy-done.11
  15.9 0.0 copy-done.9
  15.9 0.0 copy-done
  16.0 1.5 %fusion.8 = f32[3,16,256]{2,1,0:T(8,128)S(1)} fusion(bf16[4096,256]{1,0:T(8,128)(2,1)S(1)} %copy-done, bf16[3,128,4096]{2,1,0:T(8,128)(2,1)} %copy-done.6, s32[]{:T(128)S(6)} %select_n.3), kind=kOutput, calls=%fused_computation.10 | convolution fusion | flops 100663296 | bytes 2539524 | tf_op jit(solution)/shard_map/sbk,kn->bsn/dot_general | solution.py:340
  17.5 0.6 pad.8.fv_ref
  18.2 0.6 pad.7.fk_ref
  18.8 6.3 %all-to-all-done = bf16[3,128,512]{2,0,1:T(4,128)(2,1)S(1)} async-done(((bf16[3,128,512]{2,0,1:T(4,128)(2,1)}), bf16[3,128,512]{2,0,1:T(4,128)(2,1)S(1)}, u32[]{:S(2)}, u32[]{:S(2)}) %all-to-all-start) | async-done | bytes 393248 | tf_op jit(solution)/shard_map/all_to_all | solution.py:338
  25.1 0.3 copy.21
  25.3 1.0 %reshape.32 = bf16[3,16,32,128]{3,2,0,1:T(8,128)(2,1)} reshape(bf16[3,16,8,512]{3,2,0,1:T(8,128)(2,1)S(1)} %copy.21) | data formatting | bytes 786432 | tf_op jit(solution)/shard_map/reshape | solution.py:342
  26.3 20.2 %shard_map.139 = (bf16[4,3,16,1024]{3,2,1,0:T(8,128)(2,1)}, bf16[16,3072,128]{2,1,0:T(8,128)(2,1)}, bf16[16,3072,128]{2,1,0:T(8,128)(2,1)}) custom-call(s32[16]{0:T(128)} %len_ref.1, bf16[16,96,128]{2,1,0:T(8,128)(2,1)} %bitcast.24, bf16[16,16,128]{2,1,0:T(8,128)(2,1)} %pad.7.fk_ref, bf16[16,16,128]{2,1,0:T(8,128)(2,1)} %pad.8.fv_ref, ...), custom_call_target="tpu_custom_call" | custom-call | flops 2415919104 | bytes 50331648 | tf_op jit(solution)/shard_map/pallas_call | solution.py:117
  46.5 0.0 copy-start.3
  46.5 1.9 %copy-done.3 = bf16[3,128,4096]{2,1,0:T(8,128)(2,1)S(1)} copy-done((bf16[3,128,4096]{2,1,0:T(8,128)(2,1)S(1)}, bf16[3,128,4096]{2,1,0:T(8,128)(2,1)}, u32[]{:S(2)}) %copy-start.3) | copy-done | bytes 3145752
  48.4 0.0 copy-start.4
  48.4 2.2 %copy-done.4 = bf16[512,4096]{1,0:T(8,128)(2,1)S(1)} copy-done((bf16[512,4096]{1,0:T(8,128)(2,1)S(1)}, bf16[512,4096]{1,0:T(8,128)(2,1)}, u32[]{:S(2)}) %copy-start.4) | copy-done | bytes 4194328
  50.6 0.0 copy-start.5
  50.6 1.0 %copy-done.5 = bf16[4,3,16,1024]{3,2,1,0:T(8,128)(2,1)S(1)} copy-done((bf16[4,3,16,1024]{3,2,1,0:T(8,128)(2,1)S(1)}, bf16[4,3,16,1024]{3,2,1,0:T(8,128)(2,1)}, u32[]{:S(2)}) %copy-start.5) | copy-done | bytes 393240
  51.6 0.0 copy-start.1
  51.6 38.3 %shard_map.140 = bf16[3,128,4096]{2,1,0:T(8,128)(2,1)S(1)} custom-call(bf16[4,3,16,1024]{3,2,1,0:T(8,128)(2,1)S(1)} %copy-done.5, bf16[512,4096]{1,0:T(8,128)(2,1)S(1)} %copy-done.4, bf16[3,128,4096]{2,1,0:T(8,128)(2,1)S(1)} %copy-done.3, bf16[1,4096]{1,0:T(2,128)(2,1)S(1)} %reshape.34.b_ref), custom_call_target="tpu_custom_call" | custom-call | flops 1610612736 | bytes 16777216 | tf_op jit(solution)/shard_map/pallas_call | solution.py:304
  89.9 1.7 %copy.30 = bf16[3,128,4096]{2,1,0:T(8,128)(2,1)} copy(bf16[3,128,4096]{2,1,0:T(8,128)(2,1)S(1)} %shard_map.140) | data formatting | bytes 6291456
  91.6 0.0 copy-done.1
  (8 shorter events, 0.1 us)
Async XLA Ops:
  0.6 15.3 %copy-start = (bf16[4096,256]{1,0:T(8,128)(2,1)S(1)}, bf16[4096,256]{1,0:T(8,128)(2,1)}, u32[]{:S(2)}) copy-start(bf16[4096,256]{1,0:T(8,128)(2,1)} %param.20) | copy-start | bytes 6291460
  0.6 3.5 %copy-start.2 = (bf16[3,128,4096]{2,1,0:T(8,128)(2,1)S(1)}, bf16[3,128,4096]{2,1,0:T(8,128)(2,1)}, u32[]{:S(2)}) copy-start(bf16[3,128,4096]{2,1,0:T(8,128)(2,1)} %x_ref.1) | copy-start | bytes 9437188
  0.7 4.5 %copy-start.7 = (bf16[4096]{0:T(1024)(128)(2,1)S(1)}, bf16[4096]{0:T(1024)(128)(2,1)}, u32[]{:S(2)}) copy-start(bf16[4096]{0:T(1024)(128)(2,1)} %param.16) | copy-start | bytes 24580
  0.7 4.5 %copy-start.8 = (bf16[4096]{0:T(1024)(128)(2,1)S(1)}, bf16[4096]{0:T(1024)(128)(2,1)}, u32[]{:S(2)}) copy-start(bf16[4096]{0:T(1024)(128)(2,1)} %param.17) | copy-start | bytes 24580
  4.2 2.7 %copy-start.10 = (bf16[4096,512]{1,0:T(8,128)(2,1)S(1)}, bf16[4096,512]{1,0:T(8,128)(2,1)}, u32[]{:S(2)}) copy-start(bf16[4096,512]{1,0:T(8,128)(2,1)} %param.18) | copy-start | bytes 12582916
  6.9 1.9 %copy-start.6 = (bf16[3,128,4096]{2,1,0:T(8,128)(2,1)}, bf16[3,128,4096]{2,1,0:T(8,128)(2,1)S(1)}, u32[]{:S(2)}) copy-start(bf16[3,128,4096]{2,1,0:T(8,128)(2,1)S(1)} %fusion.5) | copy-start | bytes 9437188
  6.9 9.0 %copy-start.11 = (bf16[256]{0:T(256)(128)(2,1)S(1)}, bf16[256]{0:T(256)(128)(2,1)}, u32[]{:S(2)}) copy-start(bf16[256]{0:T(256)(128)(2,1)} %param.21) | copy-start | bytes 1540
  6.9 9.0 %copy-start.9 = (bf16[4096]{0:T(1024)(128)(2,1)S(1)}, bf16[4096]{0:T(1024)(128)(2,1)}, u32[]{:S(2)}) copy-start(bf16[4096]{0:T(1024)(128)(2,1)} %param.23) | copy-start | bytes 24580
  9.9 15.2 %all-to-all-start = ((bf16[3,128,512]{2,0,1:T(4,128)(2,1)}), bf16[3,128,512]{2,0,1:T(4,128)(2,1)S(1)}, u32[]{:S(2)}, u32[]{:S(2)}) async-start(bf16[3,128,512]{2,0,1:T(4,128)(2,1)} %copy.20), calls=%async_computation | async-start | bytes 1048576 | tf_op jit(solution)/shard_map/all_to_all | solution.py:338
  46.5 1.9 %copy-start.3 = (bf16[3,128,4096]{2,1,0:T(8,128)(2,1)S(1)}, bf16[3,128,4096]{2,1,0:T(8,128)(2,1)}, u32[]{:S(2)}) copy-start(bf16[3,128,4096]{2,1,0:T(8,128)(2,1)} %x_ref.1) | copy-start | bytes 9437188
  48.4 2.2 %copy-start.4 = (bf16[512,4096]{1,0:T(8,128)(2,1)S(1)}, bf16[512,4096]{1,0:T(8,128)(2,1)}, u32[]{:S(2)}) copy-start(bf16[512,4096]{1,0:T(8,128)(2,1)} %w_ref.1) | copy-start | bytes 12582916
  50.6 1.0 %copy-start.5 = (bf16[4,3,16,1024]{3,2,1,0:T(8,128)(2,1)S(1)}, bf16[4,3,16,1024]{3,2,1,0:T(8,128)(2,1)}, u32[]{:S(2)}) copy-start(bf16[4,3,16,1024]{3,2,1,0:T(8,128)(2,1)} %get-tuple-element.6.a_ref) | copy-start | bytes 1179652
  51.6 40.0 %copy-start.1 = (bf16[4096,256]{1,0:T(8,128)(2,1)S(1)}, bf16[4096,256]{1,0:T(8,128)(2,1)}, u32[]{:S(2)}) copy-start(bf16[4096,256]{1,0:T(8,128)(2,1)} %param.20) | copy-start | bytes 6291460

commit v2 on v0

v2 whole, which is shorter than its diff:
```python
import functools
import math

import jax
import jax.numpy as jnp
from jax import lax
from jax.experimental import pallas as pl
from jax.experimental.pallas import tpu as pltpu
from jax.sharding import PartitionSpec as P

LN_EPS = 1e-5
KEY_TILE = 256
FRESH_ROWS = 16
WINDOW = 16
N_CHIPS = 4
N_CORES = 2
N_PARTS = 2
LN_ROWS = 16
MESH = pl.DeviceIdType.MESH
BLOCK_VMEM = 32 * 1024 * 1024


def attend_one(q_rows, k_ref, v_ref, score_ref, seq_len, fresh_k, fresh_v, fresh_mask):
    rows, depth = q_rows.shape
    length = k_ref.shape[0]
    to_log2 = depth ** -0.5 * math.log2(math.e)
    contract_last = (((1,), (1,)), ((), ()))
    new_scores = lax.dot_general(q_rows, fresh_k, contract_last, preferred_element_type=jnp.float32)
    new_scores = jnp.where(fresh_mask, new_scores, -jnp.inf)
    best = None
    lane = lax.broadcasted_iota(jnp.int32, (rows, KEY_TILE), 1)
    for start in range(0, length, KEY_TILE):
        tile = lax.dot_general(q_rows, k_ref[start:start + KEY_TILE, :], contract_last, preferred_element_type=jnp.float32)
        tile = jnp.where(lane < seq_len - start, tile, -jnp.inf)
        score_ref[:, start:start + KEY_TILE] = tile
        best = tile if best is None else jnp.maximum(best, tile)
    top = jnp.maximum(jnp.max(best, axis=-1, keepdims=True), jnp.max(new_scores, axis=-1, keepdims=True))
    new_weights = jnp.exp2((new_scores - top) * to_log2)
    numerator = jnp.dot(new_weights.astype(jnp.bfloat16), fresh_v, preferred_element_type=jnp.float32)
    total = None
    for start in range(0, length, KEY_TILE):
        weights = jnp.exp2((score_ref[:, start:start + KEY_TILE] - top) * to_log2)
        total = weights if total is None else total + weights
        numerator = numerator + jnp.dot(weights.astype(jnp.bfloat16), v_ref[start:start + KEY_TILE, :], preferred_element_type=jnp.float32)
    denominator = jnp.sum(total, axis=-1, keepdims=True) + jnp.sum(new_weights, axis=-1, keepdims=True)
    return numerator / denominator


def block_kernel(
        len_ref, g_ref, lb_ref, bq_ref, bkv_ref, bo_ref, x_hbm, wq_hbm, wkv_hbm, wo_hbm, k_hbm, v_hbm,
        y_ref, k_buf, v_buf, fk_ref, fv_ref,
        x_buf, h_buf, gain_buf, bias_buf, wq_buf, wkv_buf, w_buf, q_buf, q_in, q_rows, score_buf, head_buf, a_src, a_buf, lhs_buf, p_buf, mid_buf, fin_buf,
        x_sems, w_sems, kv_sems, swap_sems, q_send, q_recv, a_send, a_recv, f_send, f_recv, rs_send, rs_recv, ag_send, ag_recv):
    me = lax.axis_index('tp')
    n_dev = N_CHIPS * N_CORES
    chip, core = me // N_CORES, me % N_CORES
    n_steps, group_rows, width = x_buf.shape
    n_seqs, length, depth = k_buf.shape
    q_width = wq_buf.shape[1]
    dev_heads = q_width // depth
    chip_heads = N_CORES * dev_heads
    part_seqs = n_seqs // N_PARTS
    rows = n_dev * n_steps * dev_heads
    own_rows = wo_hbm.shape[0]
    half, quarter = width // 2, width // 4
    block = n_steps * N_CORES * part_seqs

    def chip_at(k):
        return (chip + k) % N_CHIPS

    def device(k):
        return {'tp': chip_at(k) * N_CORES + core}

    def member(d):
        return (me + d) % n_dev

    right, left, partner = device(1), device(3), {'tp': chip * N_CORES + 1 - core}

    def remote(src, dst, send, recv, to):
        return pltpu.make_async_remote_copy(src_ref=src, dst_ref=dst, send_sem=send, recv_sem=recv, device_id=to, device_id_type=MESH)

    def cols(which, begin, size):
        return pl.ds(pl.multiple_of(which * half + begin, quarter), size)

    def seq_rows(d):
        return pl.ds(pl.multiple_of(member(d) * n_seqs, n_seqs), n_seqs)

    barrier = pltpu.get_barrier_semaphore()
    for d in range(1, n_dev):
        pl.semaphore_signal(barrier, inc=1, device_id={'tp': member(d)}, device_id_type=MESH)

    def x_load(s):
        return pltpu.make_async_copy(x_hbm.at[s], x_buf.at[s], x_sems.at[s])

    def kv_load(b):
        return (pltpu.make_async_copy(k_hbm.at[b], k_buf.at[b], kv_sems.at[0, b]),
                pltpu.make_async_copy(v_hbm.at[b], v_buf.at[b], kv_sems.at[1, b]))

    own_w_rows = pl.ds(pl.multiple_of(core * own_rows, own_rows), own_rows)
    wq_load = pltpu.make_async_copy(wq_hbm, wq_buf, w_sems.at[0])
    wkv_load = pltpu.make_async_copy(wkv_hbm, wkv_buf, w_sems.at[1])
    wo_load = pltpu.make_async_copy(wo_hbm.at[:, cols(core, 0, half)], w_buf.at[own_w_rows, :], w_sems.at[2])
    wo_swap = remote(wo_hbm.at[:, cols(1 - core, 0, half)], w_buf.at[own_w_rows, :], swap_sems.at[0], swap_sems.at[1], partner)
    for s in range(n_steps):
        x_load(s).start()
    wq_load.start()
    wkv_load.start()

    gain_buf[...] = jnp.broadcast_to(g_ref[...].astype(jnp.float32), gain_buf.shape)
    bias_buf[...] = jnp.broadcast_to(lb_ref[...].astype(jnp.float32), bias_buf.shape)

    def q_copy(s, d):
        return remote(q_buf.at[s, seq_rows(d)], q_in.at[me, s], q_send.at[s, d - 1], q_recv.at[s, d - 1], {'tp': member(d)})

    for s in range(n_steps):
        x_load(s).wait()

        def norm_rows(i, carry):
            where = pl.ds(pl.multiple_of(i * LN_ROWS, LN_ROWS), LN_ROWS)
            x_float = x_buf[s, where, :].astype(jnp.float32)
            centered = x_float - jnp.mean(x_float, axis=-1, keepdims=True)
            row_var = jnp.mean(centered * centered, axis=-1, keepdims=True)
            scaled = centered * lax.rsqrt(row_var + LN_EPS)
            h_buf[s, where, :] = (scaled * gain_buf[...] + bias_buf[...]).astype(h_buf.dtype)
            return carry

        lax.fori_loop(0, group_rows // LN_ROWS, norm_rows, 0)
        if s == 0:
            wq_load.wait()
            wo_load.start()
            for b in range(n_seqs):
                for copy in kv_load(b):
                    copy.start()
        for n in range(0, q_width, 256):
            part = jnp.dot(h_buf[s], wq_buf[:, n:n + 256], preferred_element_type=jnp.float32)
            q_buf[s, :, n:n + 256] = (part + bq_ref[:, n:n + 256].astype(jnp.float32)).astype(q_buf.dtype)
        if s == 0:
            pl.semaphore_wait(barrier, n_dev - 1)
        for d in range(1, n_dev):
            q_copy(s, d).start()
        if s == 0:
            wo_swap.start()
        q_in[me, s] = q_buf[s, seq_rows(0), :]

    wkv_load.wait()
    own_h = jnp.concatenate([h_buf[s, seq_rows(0), :] for s in range(n_steps)], axis=0)
    fresh = jnp.dot(own_h, wkv_buf[...], preferred_element_type=jnp.float32) + bkv_ref[...].astype(jnp.float32)
    fresh = fresh.astype(jnp.bfloat16).astype(jnp.float32)
    fk_ref[...] = jnp.zeros_like(fk_ref)
    fv_ref[...] = jnp.zeros_like(fv_ref)
    for s in range(n_steps):
        where = pl.ds(s, n_seqs, stride=FRESH_ROWS)
        fk_ref[where, :] = fresh[s * n_seqs:(s + 1) * n_seqs, :depth]
        fv_ref[where, :] = fresh[s * n_seqs:(s + 1) * n_seqs, depth:]

    for s in range(n_steps):
        for d in range(1, n_dev):
            q_copy(s, d).wait_recv()
    for u in range(n_dev):
        for s in range(n_steps):
            for h in range(dev_heads):
                first = ((u * n_steps + s) * dev_heads + h) * n_seqs
                q_rows[first:first + n_seqs, :] = q_in[u, s, :, h * depth:(h + 1) * depth].astype(jnp.float32)

    shape = (rows, FRESH_ROWS)
    step_of_row = lax.broadcasted_iota(jnp.int32, shape, 0) // dev_heads % n_steps
    fresh_mask = lax.broadcasted_iota(jnp.int32, shape, 1) <= step_of_row

    def a_copy(p, d):
        return remote(a_src.at[p, chip_at(d)], a_buf.at[p, core, chip], a_send.at[p, d - 1], a_recv.at[p, d - 1], device(d))

    def a_forward(p, d):
        where = a_buf.at[p, core, chip_at(N_CHIPS - d)]
        return remote(a_src.at[p, chip] if d == 0 else where, where, f_send.at[p, d], f_recv.at[p, d], partner)

    low, high = pl.ds(0, quarter), pl.ds(quarter, quarter)

    def rs(p, i):
        def part(k, where):
            return p_buf.at[p, chip_at(k), :, where]
        src, dst, to = (
            (part(2, low), mid_buf.at[p, 0], right),
            (part(2, high), mid_buf.at[p, 1], left),
            (part(1, high), fin_buf.at[p, 0], right),
            (part(3, low), fin_buf.at[p, 1], left),
            (part(1, low), fin_buf.at[p, 2], right),
            (part(3, high), fin_buf.at[p, 3], left),
        )[i]
        return remote(src, dst, rs_send.at[p, i], rs_recv.at[p, i], to)

    def ag(p, i):
        k, begin, size, to = (
            (0, 0, half, right),
            (0, 0, half, left),
            (3, 0, quarter, right),
            (1, quarter, quarter, left),
            (0, 0, half, partner),
            (3, 0, half, partner),
            (1, 0, half, partner),
            (2, 0, quarter, partner),
            (2, quarter, quarter, partner),
        )[i]
        where = y_ref.at[:, chip_at(k), :, p, :, cols(core, begin, size)]
        return remote(where, where, ag_send.at[p, i], ag_recv.at[p, i], to)

    def pack(p):
        for t in range(N_CHIPS):
            for s in range(n_steps):
                pieces = []
                for h in range(chip_heads):
                    u = t * N_CORES + h // dev_heads
                    first = ((u * n_steps + s) * dev_heads + h % dev_heads) * n_seqs + p * part_seqs
                    pieces.append(head_buf[first:first + part_seqs, :])
                a_src[p, t, s] = jnp.concatenate(pieces, axis=1).astype(a_src.dtype)
        for d in (2, 1, 3):
            a_copy(p, d).start()
        a_forward(p, 0).start()
        a_buf[p, core, chip] = a_src[p, chip]

    def forward(p):
        for d in (1, 3, 2):
            a_copy(p, d).wait_recv()
            a_forward(p, d).start()

    def partial(p):
        for d in range(N_CHIPS):
            a_forward(p, d).wait_recv()
        if p == 0:
            wo_load.wait()
            wo_swap.wait_recv()
        for t in range(N_CHIPS):
            for s in range(n_steps):
                pair = jnp.concatenate([a_buf[p, c, t, s].astype(jnp.float32) for c in range(N_CORES)], axis=0)
                first = (t * n_steps + s) * N_CORES * part_seqs
                lhs_buf[first:first + N_CORES * part_seqs, :] = pair.astype(lhs_buf.dtype)
        for n in range(0, half, 512):
            out = jnp.dot(lhs_buf[...], w_buf[:, n:n + 512], preferred_element_type=jnp.float32).astype(p_buf.dtype)
            for t in range(N_CHIPS):
                p_buf[p, t, :, n:n + 512] = out[t * block:(t + 1) * block]
        for i in range(4):
            rs(p, i).start()

    def add_into(target, other):
        target[...] = (target[...].astype(jnp.float32) + other[...].astype(jnp.float32)).astype(target.dtype)

    def middle(p):
        rs(p, 0).wait_recv()
        add_into(p_buf.at[p, chip_at(1), :, low], mid_buf.at[p, 0])
        rs(p, 4).start()
        rs(p, 1).wait_recv()
        add_into(p_buf.at[p, chip_at(3), :, high], mid_buf.at[p, 1])
        rs(p, 5).start()

    def finish(p):
        for i in (2, 3, 4, 5):
            rs(p, i).wait_recv()
        chip_rows = pl.ds(pl.multiple_of(chip * N_CORES * n_seqs, N_CORES * n_seqs), N_CORES * n_seqs)
        for begin, one, two in ((0, 1, 2), (quarter, 0, 3)):
            where = cols(core, begin, quarter)
            total = p_buf[p, chip, :, begin:begin + quarter].astype(jnp.float32)
            total = total + fin_buf[p, one].astype(jnp.float32)
            total = total + fin_buf[p, two].astype(jnp.float32)
            total = total + bo_ref[:, where].astype(jnp.float32)
            for s in range(n_steps):
                x_part = x_buf[s, chip_rows, where].astype(jnp.float32)
                for c in range(N_CORES):
                    first = (s * N_CORES + c) * part_seqs
                    x_first = c * n_seqs + p * part_seqs
                    y_ref[s, chip, c, p, :, where] = (x_part[x_first:x_first + part_seqs] + total[first:first + part_seqs]).astype(y_ref.dtype)
        for i in (0, 1, 4):
            ag(p, i).start()

    def relay(p):
        ag(p, 0).wait_recv()
        ag(p, 2).start()
        ag(p, 5).start()
        ag(p, 1).wait_recv()
        ag(p, 3).start()
        ag(p, 6).start()

    def last(p):
        ag(p, 2).wait_recv()
        ag(p, 7).start()
        ag(p, 3).wait_recv()
        ag(p, 8).start()

    def attend_pair(i, carry):
        for j in range(2):
            for copy in kv_load(2 * i + j):
                copy.wait()
        for j in range(2):
            b = 2 * i + j
            q_one = q_rows[pl.ds(b, rows, stride=n_seqs), :].astype(jnp.bfloat16)
            new = pl.ds(pl.multiple_of(b * FRESH_ROWS, FRESH_ROWS), FRESH_ROWS)
            out = attend_one(q_one, k_buf.at[b], v_buf.at[b], score_buf.at[j], len_ref[b],
                             fk_ref[new, :].astype(jnp.bfloat16), fv_ref[new, :].astype(jnp.bfloat16), fresh_mask)
            head_buf[pl.ds(b, rows, stride=n_seqs), :] = out
        for at, stage in STAGES_BESIDE_ATTENTION:
            @pl.when(i == at)
            def _():
                {'pack': pack, 'forward': forward, 'partial': partial, 'middle': middle}[stage](0)
        return carry

    lax.fori_loop(0, n_seqs // 2, attend_pair, 0)
    pack(1)
    finish(0)
    forward(1)
    relay(0)
    partial(1)
    last(0)
    middle(1)
    finish(1)
    relay(1)
    last(1)
    wo_swap.wait_send()
    for s in range(n_steps):
        for d in range(1, n_dev):
            q_copy(s, d).wait_send()
    for p in range(N_PARTS):
        for i in range(4, 9):
            ag(p, i).wait_recv()
        for i in range(9):
            ag(p, i).wait_send()
        for i in range(6):
            rs(p, i).wait_send()
        for d in (1, 2, 3):
            a_copy(p, d).wait_send()
        for d in range(N_CHIPS):
            a_forward(p, d).wait_send()


STAGES_BESIDE_ATTENTION = ((3, 'pack'), (5, 'forward'), (5, 'partial'), (7, 'middle'))


def store_kernel(n_steps, len_ref, fk_ref, fv_ref, y_ref, k_ref, v_ref, y_out, k_out, v_out, k_buf, v_buf, sems, y_sem):
    n_seqs, length, depth = k_buf.shape

    def store(b):
        return (pltpu.make_async_copy(k_buf.at[b], k_out.at[b], sems.at[0, b]),
                pltpu.make_async_copy(v_buf.at[b], v_out.at[b], sems.at[1, b]))

    def patch(b, buf, fresh):
        start = pl.multiple_of(jnp.minimum(len_ref[b] // 8 * 8, length - WINDOW), 8)
        offset = len_ref[b] - start
        row = lax.broadcasted_iota(jnp.int32, (WINDOW, depth), 0)
        window = buf[b, pl.ds(start, WINDOW), :].astype(jnp.float32)
        for s in range(n_steps):
            window = jnp.where(row == offset + s, fresh[b * FRESH_ROWS + s:b * FRESH_ROWS + s + 1, :], window)
        buf[b, pl.ds(start, WINDOW), :] = window.astype(buf.dtype)

    y_copy = pltpu.make_async_copy(y_ref, y_out, y_sem)
    y_copy.start()
    for b in range(n_seqs):
        patch(b, k_buf, fk_ref)
        patch(b, v_buf, fv_ref)
        for copy in store(b):
            copy.start()
    y_copy.wait()
    for b in range(n_seqs):
        for copy in store(b):
            copy.wait()


def solution(mesh):
    def local_block(x_steps, seq_lens, k_cache, v_cache, ln_gain, ln_bias, w_q, b_q, w_kv, b_kv, w_out, b_out):
        n_steps, group_rows, width = x_steps.shape
        n_seqs, length, depth = k_cache.shape
        q_width, kv_width = w_q.shape[1], w_kv.shape[1]
        n_dev = N_CHIPS * N_CORES
        part_seqs = n_seqs // N_PARTS
        rows = n_dev * n_steps * q_width // depth
        chip_width, half = N_CORES * q_width, width // 2
        block = n_steps * N_CORES * part_seqs
        smem = pl.BlockSpec(memory_space=pltpu.SMEM)
        vmem = pl.BlockSpec(memory_space=pltpu.VMEM)
        hbm = pl.BlockSpec(memory_space=pl.ANY)
        dma = pltpu.SemaphoreType.DMA
        bf16, f32 = jnp.bfloat16, jnp.float32
        y_shape = (n_steps, N_CHIPS, N_CORES, N_PARTS, part_seqs, width)
        fresh_shape = (n_seqs * FRESH_ROWS, depth)
        y_vm, k_vm, v_vm, fresh_k, fresh_v = pl.pallas_call(
            block_kernel,
            out_shape=[pltpu.VMEM(y_shape, bf16), pltpu.VMEM(k_cache.shape, bf16), pltpu.VMEM(v_cache.shape, bf16), pltpu.VMEM(fresh_shape, f32), pltpu.VMEM(fresh_shape, f32)],
            in_specs=[smem] + [vmem] * 5 + [hbm] * 6,
            out_specs=[vmem] * 5,
            scratch_shapes=[
                pltpu.VMEM(x_steps.shape, bf16),
                pltpu.VMEM(x_steps.shape, bf16),
                pltpu.VMEM((LN_ROWS, width), f32),
                pltpu.VMEM((LN_ROWS, width), f32),
                pltpu.VMEM(w_q.shape, bf16),
                pltpu.VMEM(w_kv.shape, bf16),
                pltpu.VMEM((chip_width, half), bf16),
                pltpu.VMEM((n_steps, group_rows, q_width), bf16),
                pltpu.VMEM((n_dev, n_steps, n_seqs, q_width), bf16),
                pltpu.VMEM((rows * n_seqs, depth), f32),
                pltpu.VMEM((2, rows, length), f32),
                pltpu.VMEM((rows * n_seqs, depth), f32),
                pltpu.VMEM((N_PARTS, N_CHIPS, n_steps, part_seqs, chip_width), bf16),
                pltpu.VMEM((N_PARTS, N_CORES, N_CHIPS, n_steps, part_seqs, chip_width), bf16),
                pltpu.VMEM((N_CHIPS * block, chip_width), bf16),
                pltpu.VMEM((N_PARTS, N_CHIPS, block, half), bf16),
                pltpu.VMEM((N_PARTS, 2, block, half // 2), bf16),
                pltpu.VMEM((N_PARTS, 4, block, half // 2), bf16),
                dma((n_steps,)), dma((3,)), dma((2, n_seqs)), dma((2,)),
                dma((n_steps, n_dev - 1)), dma((n_steps, n_dev - 1)),
                dma((N_PARTS, 3)), dma((N_PARTS, 3)),
                dma((N_PARTS, N_CHIPS)), dma((N_PARTS, N_CHIPS)),
                dma((N_PARTS, 6)), dma((N_PARTS, 6)),
                dma((N_PARTS, 9)), dma((N_PARTS, 9)),
            ],
            compiler_params=pltpu.CompilerParams(vmem_limit_bytes=BLOCK_VMEM, collective_id=1, has_side_effects=True),
            cost_estimate=pl.CostEstimate(flops=4 * n_seqs * rows * length * depth, bytes_accessed=4 * n_seqs * length * depth, transcendentals=n_seqs * rows * length),
        )(seq_lens, ln_gain.reshape(1, width), ln_bias.reshape(1, width), b_q.reshape(1, q_width), b_kv.reshape(1, kv_width), b_out.reshape(1, width),
          x_steps, w_q, w_kv, w_out, k_cache, v_cache)
        y_steps, k_out, v_out, _, _ = pl.pallas_call(
            functools.partial(store_kernel, n_steps),
            out_shape=[jax.ShapeDtypeStruct(y_shape, bf16), jax.ShapeDtypeStruct(k_cache.shape, bf16), jax.ShapeDtypeStruct(v_cache.shape, bf16), pltpu.VMEM(k_cache.shape, bf16), pltpu.VMEM(v_cache.shape, bf16)],
            in_specs=[smem] + [vmem] * 5,
            out_specs=[hbm] * 3 + [vmem] * 2,
            scratch_shapes=[dma((2, n_seqs)), dma],
            input_output_aliases={4: 3, 5: 4},
            compiler_params=pltpu.CompilerParams(vmem_limit_bytes=2 * 1024 * 1024),
        )(seq_lens, fresh_k, fresh_v, y_vm, k_vm, v_vm)
        return y_steps.reshape(x_steps.shape), k_out, v_out

    row_spec = P(('dp', 'tp'), None, None)
    return jax.shard_map(
        local_block,
        mesh=mesh,
        in_specs=(P(None, 'dp', None), P(('dp', 'tp')), row_spec, row_spec, P(None), P(None), P(None, 'tp'), P('tp'), P(None, None), P(None), P('tp', None), P(None)),
        out_specs=(P(None, 'dp', None), row_spec, row_spec),
        check_vma=False,
    )
```

time: 168 us -> 88.4 us (0.53); the launches traced: 165 us -> 87.7 us
  waiting for transfers between devices: 65.4 us -> 0 us
  Pallas kernels: 20.2 us -> 80.7 us
  local copies, waits for them, and re-layouts: 27.8 us -> 6.39 us
  between operations: 14.3 us -> 0.65 us
  blocking collectives: 11.7 us -> 0 us
  other arithmetic: 11 us -> 0 us
  matrix products: 8.97 us -> 0 us
  starting transfers between devices: 6.02 us -> 0 us
    pallas_call x1 -> x2, Pallas kernels: 20.2 us -> 80.7 us  [the longest x1 70.5 us: local_block(): pl.pallas_call(block_kernel, out_shape=[pltpu.VMEM(y_shape, bf16), pltpu....]
    psum x1 -> x0, waiting for transfers between devices: 59.1 us -> none  [local_block(): proj_sum = lax.psum(proj_part, 'tp')]
    unnamed x22 -> x2, local copies, waits for them, and re-layouts: 12.7 us -> 0.01 us
    all_to_all x1 -> x0, blocking collectives: 11.7 us -> none  [local_block(): attn_heads = lax.all_to_all(attn, 'tp', 2, 1, tiled=True)]
    dot_general x3 -> x0, matrix products: 8.97 us -> none  [the longest x1 5.66 us: local_block(): jnp.einsum('sbk,kn->sbn', attn_heads, w_out, preferred_element_type=jnp.f...]
    convert_element_type x8 -> x0, other arithmetic: 7.53 us -> none  [the longest x1 5.82 us: local_block(): (x_steps.astype(jnp.float32) + proj_sum.astype(jnp.float32) + b_out.astyp...]
    all_to_all x1 -> x0, waiting for transfers between devices: 6.27 us -> none  [local_block(): q_local = lax.all_to_all(q_part, 'tp', 1, 2, tiled=True)]
    all_to_all x1 -> x0, starting transfers between devices: 6.02 us -> none  [local_block(): q_local = lax.all_to_all(q_part, 'tp', 1, 2, tiled=True)]
  transfers between devices with their start and end apart: 2 -> 0, of which waited for: 2 -> 0; matrix products, arithmetic and copies ran while one was open for 2% -> 0% of each run, Pallas kernels for 0% -> 0%
where the time goes in v2:
time: 88.4 us; the launch traced here: 87.7 us
  Pallas kernels  80.7 us (91%)
  local copies, waits for them, and re-layouts  6.39 us (7%)
    pallas_call x1, Pallas kernels, local_block(): pl.pallas_call(block_kernel, out_shape=[pltpu.VMEM(y_shape, bf16), pltpu....  70.5 us
    pallas_call x1, Pallas kernels, local_block(): pl.pallas_call(functools.partial(store_kernel, n_steps), out_shape=[jax.S...  10.1 us

profile of v2, /device:TPU:113, one launch (start us, length us, event | category | flops | bytes accessed | tf_op | source)
XLA Modules:
  0.0 87.7 jit_solution(189670480890303386)
XLA Ops:
  0.6 1.2 %reshape.27.bkv_ref = bf16[1,256]{1,0:T(2,128)(2,1)} reshape(bf16[256]{0:T(256)(128)(2,1)} %param.21) | data formatting | bytes 1024 | tf_op jit(solution)/shard_map/reshape | solution.py:414
  1.8 1.3 %reshape.26.bq_ref = bf16[1,512]{1,0:T(2,128)(2,1)} reshape(bf16[512]{0:T(512)(128)(2,1)} %param.19) | data formatting | bytes 2048 | tf_op jit(solution)/shard_map/reshape | solution.py:414
  3.1 1.3 %reshape.24.g_ref = bf16[1,4096]{1,0:T(2,128)(2,1)} reshape(bf16[4096]{0:T(1024)(128)(2,1)} %param.16) | data formatting | bytes 16384 | tf_op jit(solution)/shard_map/reshape | solution.py:414
  4.4 1.3 %reshape.25.lb_ref = bf16[1,4096]{1,0:T(2,128)(2,1)} reshape(bf16[4096]{0:T(1024)(128)(2,1)} %param.17) | data formatting | bytes 16384 | tf_op jit(solution)/shard_map/reshape | solution.py:414
  5.7 1.3 %reshape.28.bo_ref = bf16[1,4096]{1,0:T(2,128)(2,1)} reshape(bf16[4096]{0:T(1024)(128)(2,1)} %param.23) | data formatting | bytes 16384 | tf_op jit(solution)/shard_map/reshape | solution.py:414
  7.0 0.0 copy-start
  7.0 70.5 %shard_map.139 = (bf16[3,4,2,2,8,4096]{5,4,3,2,1,0:T(8,128)(2,1)S(1)}, bf16[16,3072,128]{2,1,0:T(8,128)(2,1)S(1)}, bf16[16,3072,128]{2,1,0:T(8,128)(2,1)S(1)}, f32[256,128]{1,0:T(8,128)S(1)}, f32[256,128]{1,0:T(8,128)S(1)}) custom-call(s32[16]{0:T(128)} %len_ref.3, bf16[1,4096]{1,0:T(2,128)(2,1)} %reshape.24.g_ref, bf16[1,4096]{1,0:T(2,128)(2,1)} %reshape.25.lb_ref, ...), custom_call_target="tpu_custom_call" | custom-call | flops 2415919104 | bytes 25165824 | tf_op jit(solution)/shard_map/pallas_call | solution.py:381
  77.5 0.0 copy-done
  77.6 10.1 %shard_map.140 = (bf16[3,4,2,2,8,4096]{5,4,3,2,1,0:T(8,128)(2,1)}, bf16[16,3072,128]{2,1,0:T(8,128)(2,1)}, bf16[16,3072,128]{2,1,0:T(8,128)(2,1)}, bf16[16,3072,...) custom-call(s32[16]{0:T(128)S(1)} %copy-done, ...), custom_call_target="tpu_custom_call", output_to_operand_aliasing={{3}: (4, {}), {4}: (5, {})} | custom-call | tf_op jit(solution)/shard_map/pallas_call | solution.py:416
Async XLA Ops:
  7.0 70.5 %copy-start = (s32[16]{0:T(128)S(1)}, s32[16]{0:T(128)}, u32[]{:S(2)}) copy-start(s32[16]{0:T(128)} %len_ref.3) | copy-start | bytes 196

commit v3 on v2

--- a/solution.py
+++ b/solution.py
@@ -49,7 +49,7 @@
 def block_kernel(
         len_ref, g_ref, lb_ref, bq_ref, bkv_ref, bo_ref, x_hbm, wq_hbm, wkv_hbm, wo_hbm, k_hbm, v_hbm,
         y_ref, k_buf, v_buf, fk_ref, fv_ref,
-        x_buf, h_buf, gain_buf, bias_buf, wq_buf, wkv_buf, w_buf, q_buf, q_in, q_rows, score_buf, head_buf, a_src, a_buf, lhs_buf, p_buf, mid_buf, fin_buf,
+        x_buf, h_buf, gain_buf, bias_buf, bo_buf, wq_buf, wkv_buf, w_buf, q_buf, q_in, q_rows, score_buf, head_buf, a_src, a_buf, lhs_buf, p_buf, mid_buf, fin_buf,
         x_sems, w_sems, kv_sems, swap_sems, q_send, q_recv, a_send, a_recv, f_send, f_recv, rs_send, rs_recv, ag_send, ag_recv):
     me = lax.axis_index('tp')
     n_dev = N_CHIPS * N_CORES
@@ -63,7 +63,7 @@
     rows = n_dev * n_steps * dev_heads
     own_rows = wo_hbm.shape[0]
     half, quarter = width // 2, width // 4
-    block = n_steps * N_CORES * part_seqs
+    block = N_CORES * part_seqs
 
     def chip_at(k):
         return (chip + k) % N_CHIPS
@@ -106,8 +106,10 @@
     wq_load.start()
     wkv_load.start()
 
-    gain_buf[...] = jnp.broadcast_to(g_ref[...].astype(jnp.float32), gain_buf.shape)
-    bias_buf[...] = jnp.broadcast_to(lb_ref[...].astype(jnp.float32), bias_buf.shape)
+    bq_row = bq_ref[...].astype(jnp.float32).reshape(1, q_width)
+    bo_buf[...] = bo_ref[...].astype(jnp.float32).reshape(1, width)
+    gain_buf[...] = jnp.broadcast_to(g_ref[...].astype(jnp.float32).reshape(1, width), gain_buf.shape)
+    bias_buf[...] = jnp.broadcast_to(lb_ref[...].astype(jnp.float32).reshape(1, width), bias_buf.shape)
 
     def q_copy(s, d):
         return remote(q_buf.at[s, seq_rows(d)], q_in.at[me, s], q_send.at[s, d - 1], q_recv.at[s, d - 1], {'tp': member(d)})
@@ -128,12 +130,9 @@
         if s == 0:
             wq_load.wait()
             wo_load.start()
-            for b in range(n_seqs):
-                for copy in kv_load(b):
-                    copy.start()
         for n in range(0, q_width, 256):
             part = jnp.dot(h_buf[s], wq_buf[:, n:n + 256], preferred_element_type=jnp.float32)
-            q_buf[s, :, n:n + 256] = (part + bq_ref[:, n:n + 256].astype(jnp.float32)).astype(q_buf.dtype)
+            q_buf[s, :, n:n + 256] = (part + bq_row[:, n:n + 256]).astype(q_buf.dtype)
         if s == 0:
             pl.semaphore_wait(barrier, n_dev - 1)
         for d in range(1, n_dev):
@@ -141,10 +140,13 @@
         if s == 0:
             wo_swap.start()
         q_in[me, s] = q_buf[s, seq_rows(0), :]
+    for b in range(n_seqs):
+        for copy in kv_load(b):
+            copy.start()
 
     wkv_load.wait()
     own_h = jnp.concatenate([h_buf[s, seq_rows(0), :] for s in range(n_steps)], axis=0)
-    fresh = jnp.dot(own_h, wkv_buf[...], preferred_element_type=jnp.float32) + bkv_ref[...].astype(jnp.float32)
+    fresh = jnp.dot(own_h, wkv_buf[...], preferred_element_type=jnp.float32) + bkv_ref[...].astype(jnp.float32).reshape(1, -1)
     fresh = fresh.astype(jnp.bfloat16).astype(jnp.float32)
     fk_ref[...] = jnp.zeros_like(fk_ref)
     fv_ref[...] = jnp.zeros_like(fv_ref)
@@ -175,20 +177,20 @@
 
     low, high = pl.ds(0, quarter), pl.ds(quarter, quarter)
 
-    def rs(p, i):
+    def rs(p, s, i):
         def part(k, where):
-            return p_buf.at[p, chip_at(k), :, where]
+            return p_buf.at[p, s, chip_at(k), :, where]
         src, dst, to = (
-            (part(2, low), mid_buf.at[p, 0], right),
-            (part(2, high), mid_buf.at[p, 1], left),
-            (part(1, high), fin_buf.at[p, 0], right),
-            (part(3, low), fin_buf.at[p, 1], left),
-            (part(1, low), fin_buf.at[p, 2], right),
-            (part(3, high), fin_buf.at[p, 3], left),
+            (part(2, low), mid_buf.at[p, s, 0], right),
+            (part(2, high), mid_buf.at[p, s, 1], left),
+            (part(1, high), fin_buf.at[p, s, 0], right),
+            (part(3, low), fin_buf.at[p, s, 1], left),
+            (part(1, low), fin_buf.at[p, s, 2], right),
+            (part(3, high), fin_buf.at[p, s, 3], left),
         )[i]
-        return remote(src, dst, rs_send.at[p, i], rs_recv.at[p, i], to)
-
-    def ag(p, i):
+        return remote(src, dst, rs_send.at[p, s, i], rs_recv.at[p, s, i], to)
+
+    def ag(p, s, i):
         k, begin, size, to = (
             (0, 0, half, right),
             (0, 0, half, left),
@@ -200,8 +202,8 @@
             (2, 0, quarter, partner),
             (2, quarter, quarter, partner),
         )[i]
-        where = y_ref.at[:, chip_at(k), :, p, :, cols(core, begin, size)]
-        return remote(where, where, ag_send.at[p, i], ag_recv.at[p, i], to)
+        where = y_ref.at[s, chip_at(k), :, p, :, cols(core, begin, size)]
+        return remote(where, where, ag_send.at[p, s, i], ag_recv.at[p, s, i], to)
 
     def pack(p):
         for t in range(N_CHIPS):
@@ -228,61 +230,67 @@
         if p == 0:
             wo_load.wait()
             wo_swap.wait_recv()
-        for t in range(N_CHIPS):
-            for s in range(n_steps):
+        for s in range(n_steps):
+            for t in range(N_CHIPS):
                 pair = jnp.concatenate([a_buf[p, c, t, s].astype(jnp.float32) for c in range(N_CORES)], axis=0)
-                first = (t * n_steps + s) * N_CORES * part_seqs
-                lhs_buf[first:first + N_CORES * part_seqs, :] = pair.astype(lhs_buf.dtype)
+                first = (s * N_CHIPS + t) * block
+                lhs_buf[first:first + block, :] = pair.astype(lhs_buf.dtype)
         for n in range(0, half, 512):
             out = jnp.dot(lhs_buf[...], w_buf[:, n:n + 512], preferred_element_type=jnp.float32).astype(p_buf.dtype)
-            for t in range(N_CHIPS):
-                p_buf[p, t, :, n:n + 512] = out[t * block:(t + 1) * block]
-        for i in range(4):
-            rs(p, i).start()
+            for s in range(n_steps):
+                for t in range(N_CHIPS):
+                    first = (s * N_CHIPS + t) * block
+                    p_buf[p, s, t, :, n:n + 512] = out[first:first + block]
+        for pair in ((0, 1), (2, 3)):
+            for s in range(n_steps):
+                for i in pair:
+                    rs(p, s, i).start()
 
     def add_into(target, other):
         target[...] = (target[...].astype(jnp.float32) + other[...].astype(jnp.float32)).astype(target.dtype)
 
-    def middle(p):
-        rs(p, 0).wait_recv()
-        add_into(p_buf.at[p, chip_at(1), :, low], mid_buf.at[p, 0])
-        rs(p, 4).start()
-        rs(p, 1).wait_recv()
-        add_into(p_buf.at[p, chip_at(3), :, high], mid_buf.at[p, 1])
-        rs(p, 5).start()
-
-    def finish(p):
+    def middle(p, s):
+        rs(p, s, 0).wait_recv()
+        add_into(p_buf.at[p, s, chip_at(1), :, low], mid_buf.at[p, s, 0])
+        rs(p, s, 4).start()
+        rs(p, s, 1).wait_recv()
+        add_into(p_buf.at[p, s, chip_at(3), :, high], mid_buf.at[p, s, 1])
+        rs(p, s, 5).start()
+
+    def finish(p, s):
         for i in (2, 3, 4, 5):
-            rs(p, i).wait_recv()
+            rs(p, s, i).wait_recv()
         chip_rows = pl.ds(pl.multiple_of(chip * N_CORES * n_seqs, N_CORES * n_seqs), N_CORES * n_seqs)
         for begin, one, two in ((0, 1, 2), (quarter, 0, 3)):
             where = cols(core, begin, quarter)
-            total = p_buf[p, chip, :, begin:begin + quarter].astype(jnp.float32)
-            total = total + fin_buf[p, one].astype(jnp.float32)
-            total = total + fin_buf[p, two].astype(jnp.float32)
-            total = total + bo_ref[:, where].astype(jnp.float32)
-            for s in range(n_steps):
-                x_part = x_buf[s, chip_rows, where].astype(jnp.float32)
-                for c in range(N_CORES):
-                    first = (s * N_CORES + c) * part_seqs
-                    x_first = c * n_seqs + p * part_seqs
-                    y_ref[s, chip, c, p, :, where] = (x_part[x_first:x_first + part_seqs] + total[first:first + part_seqs]).astype(y_ref.dtype)
+            total = p_buf[p, s, chip, :, begin:begin + quarter].astype(jnp.float32)
+            total = total + fin_buf[p, s, one].astype(jnp.float32)
+            total = total + fin_buf[p, s, two].astype(jnp.float32)
+            total = total + bo_buf[:, where]
+            x_part = x_buf[s, chip_rows, where].astype(jnp.float32)
+            for c in range(N_CORES):
+                x_first = c * n_seqs + p * part_seqs
+                y_ref[s, chip, c, p, :, where] = (x_part[x_first:x_first + part_seqs] + total[c * part_seqs:(c + 1) * part_seqs]).astype(y_ref.dtype)
         for i in (0, 1, 4):
-            ag(p, i).start()
-
-    def relay(p):
-        ag(p, 0).wait_recv()
-        ag(p, 2).start()
-        ag(p, 5).start()
-        ag(p, 1).wait_recv()
-        ag(p, 3).start()
-        ag(p, 6).start()
-
-    def last(p):
-        ag(p, 2).wait_recv()
-        ag(p, 7).start()
-        ag(p, 3).wait_recv()
-        ag(p, 8).start()
+            ag(p, s, i).start()
+
+    def relay(p, s):
+        ag(p, s, 0).wait_recv()
+        ag(p, s, 2).start()
+        ag(p, s, 5).start()
+        ag(p, s, 1).wait_recv()
+        ag(p, s, 3).start()
+        ag(p, s, 6).start()
+
+    def last(p, s):
+        ag(p, s, 2).wait_recv()
+        ag(p, s, 7).start()
+        ag(p, s, 3).wait_recv()
+        ag(p, s, 8).start()
+
+    def each(stage, p):
+        for s in range(n_steps):
+            stage(p, s)
 
     def attend_pair(i, carry):
         for j in range(2):
@@ -295,41 +303,47 @@
             out = attend_one(q_one, k_buf.at[b], v_buf.at[b], score_buf.at[j], len_ref[b],
                              fk_ref[new, :].astype(jnp.bfloat16), fv_ref[new, :].astype(jnp.bfloat16), fresh_mask)
             head_buf[pl.ds(b, rows, stride=n_seqs), :] = out
-        for at, stage in STAGES_BESIDE_ATTENTION:
-            @pl.when(i == at)
-            def _():
-                {'pack': pack, 'forward': forward, 'partial': partial, 'middle': middle}[stage](0)
+        @pl.when(i == 3)
+        def _():
+            pack(0)
+
+        @pl.when(i == 5)
+        def _():
+            forward(0)
+            partial(0)
+
+        @pl.when(i == 7)
+        def _():
+            each(middle, 0)
         return carry
 
     lax.fori_loop(0, n_seqs // 2, attend_pair, 0)
     pack(1)
-    finish(0)
+    each(finish, 0)
     forward(1)
-    relay(0)
     partial(1)
-    last(0)
-    middle(1)
-    finish(1)
-    relay(1)
-    last(1)
+    each(relay, 0)
+    each(middle, 1)
+    each(last, 0)
+    each(finish, 1)
+    each(relay, 1)
+    each(last, 1)
     wo_swap.wait_send()
     for s in range(n_steps):
         for d in range(1, n_dev):
             q_copy(s, d).wait_send()
     for p in range(N_PARTS):
-        for i in range(4, 9):
-            ag(p, i).wait_recv()
-        for i in range(9):
-            ag(p, i).wait_send()
-        for i in range(6):
-            rs(p, i).wait_send()
+        for s in range(n_steps):
+            for i in range(4, 9):
+                ag(p, s, i).wait_recv()
+            for i in range(9):
+                ag(p, s, i).wait_send()
+            for i in range(6):
+                rs(p, s, i).wait_send()
         for d in (1, 2, 3):
             a_copy(p, d).wait_send()
         for d in range(N_CHIPS):
             a_forward(p, d).wait_send()
-
-
-STAGES_BESIDE_ATTENTION = ((3, 'pack'), (5, 'forward'), (5, 'partial'), (7, 'middle'))
 
 
 def store_kernel(n_steps, len_ref, fk_ref, fv_ref, y_ref, k_ref, v_ref, y_out, k_out, v_out, k_buf, v_buf, sems, y_sem):
@@ -365,12 +379,12 @@
     def local_block(x_steps, seq_lens, k_cache, v_cache, ln_gain, ln_bias, w_q, b_q, w_kv, b_kv, w_out, b_out):
         n_steps, group_rows, width = x_steps.shape
         n_seqs, length, depth = k_cache.shape
-        q_width, kv_width = w_q.shape[1], w_kv.shape[1]
+        q_width = w_q.shape[1]
         n_dev = N_CHIPS * N_CORES
         part_seqs = n_seqs // N_PARTS
         rows = n_dev * n_steps * q_width // depth
         chip_width, half = N_CORES * q_width, width // 2
-        block = n_steps * N_CORES * part_seqs
+        block = N_CORES * part_seqs
         smem = pl.BlockSpec(memory_space=pltpu.SMEM)
         vmem = pl.BlockSpec(memory_space=pltpu.VMEM)
         hbm = pl.BlockSpec(memory_space=pl.ANY)
@@ -388,6 +402,7 @@
                 pltpu.VMEM(x_steps.shape, bf16),
                 pltpu.VMEM((LN_ROWS, width), f32),
                 pltpu.VMEM((LN_ROWS, width), f32),
+                pltpu.VMEM((1, width), f32),
                 pltpu.VMEM(w_q.shape, bf16),
                 pltpu.VMEM(w_kv.shape, bf16),
                 pltpu.VMEM((chip_width, half), bf16),
@@ -398,20 +413,20 @@
                 pltpu.VMEM((rows * n_seqs, depth), f32),
                 pltpu.VMEM((N_PARTS, N_CHIPS, n_steps, part_seqs, chip_width), bf16),
                 pltpu.VMEM((N_PARTS, N_CORES, N_CHIPS, n_steps, part_seqs, chip_width), bf16),
-                pltpu.VMEM((N_CHIPS * block, chip_width), bf16),
-                pltpu.VMEM((N_PARTS, N_CHIPS, block, half), bf16),
-                pltpu.VMEM((N_PARTS, 2, block, half // 2), bf16),
-                pltpu.VMEM((N_PARTS, 4, block, half // 2), bf16),
+                pltpu.VMEM((n_steps * N_CHIPS * block, chip_width), bf16),
+                pltpu.VMEM((N_PARTS, n_steps, N_CHIPS, block, half), bf16),
+                pltpu.VMEM((N_PARTS, n_steps, 2, block, half // 2), bf16),
+                pltpu.VMEM((N_PARTS, n_steps, 4, block, half // 2), bf16),
                 dma((n_steps,)), dma((3,)), dma((2, n_seqs)), dma((2,)),
                 dma((n_steps, n_dev - 1)), dma((n_steps, n_dev - 1)),
                 dma((N_PARTS, 3)), dma((N_PARTS, 3)),
                 dma((N_PARTS, N_CHIPS)), dma((N_PARTS, N_CHIPS)),
-                dma((N_PARTS, 6)), dma((N_PARTS, 6)),
-                dma((N_PARTS, 9)), dma((N_PARTS, 9)),
+                dma((N_PARTS, n_steps, 6)), dma((N_PARTS, n_steps, 6)),
+                dma((N_PARTS, n_steps, 9)), dma((N_PARTS, n_steps, 9)),
             ],
             compiler_params=pltpu.CompilerParams(vmem_limit_bytes=BLOCK_VMEM, collective_id=1, has_side_effects=True),
             cost_estimate=pl.CostEstimate(flops=4 * n_seqs * rows * length * depth, bytes_accessed=4 * n_seqs * length * depth, transcendentals=n_seqs * rows * length),
-        )(seq_lens, ln_gain.reshape(1, width), ln_bias.reshape(1, width), b_q.reshape(1, q_width), b_kv.reshape(1, kv_width), b_out.reshape(1, width),
+        )(seq_lens, ln_gain, ln_bias, b_q, b_kv, b_out,
           x_steps, w_q, w_kv, w_out, k_cache, v_cache)
         y_steps, k_out, v_out, _, _ = pl.pallas_call(
             functools.partial(store_kernel, n_steps),

time: 88.4 us -> 78.1 us (0.88)
  local copies, waits for them, and re-layouts: 6.39 us -> 0.01 us
  Pallas kernels: 80.7 us -> 77.3 us
    reshape x5 -> x0, local copies, waits for them, and re-layouts: 6.39 us -> none  [the longest x1 1.31 us: local_block(): ln_gain.reshape(1, width)]
    pallas_call x1, Pallas kernels: 70.5 us -> 67.2 us  [local_block(): pl.pallas_call(block_kernel, out_shape=[pltpu.VMEM(y_shape, bf16), pltpu....]
where the time goes in v3:
time: 78.1 us; the launch traced here: 78 us
  Pallas kernels  77.3 us (99%)
    pallas_call x1, Pallas kernels, local_block(): pl.pallas_call(block_kernel, out_shape=[pltpu.VMEM(y_shape, bf16), pltpu....  67.2 us
    pallas_call x1, Pallas kernels, local_block(): pl.pallas_call(functools.partial(store_kernel, n_steps), out_shape=[jax.S...  10.1 us

profile of v3, /device:TPU:113, one launch (start us, length us, event | category | flops | bytes accessed | tf_op | source)
XLA Modules:
  0.0 78.0 jit_solution(1015276277800091169)
XLA Ops:
  0.6 0.0 copy-start
  0.6 67.2 %shard_map.139 = (bf16[3,4,2,2,8,4096]{5,4,3,2,1,0:T(8,128)(2,1)S(1)}, bf16[16,3072,128]{2,1,0:T(8,128)(2,1)S(1)}, bf16[16,3072,128]{2,1,0:T(8,128)(2,1)S(1)}, f32[256,128]{1,0:T(8,128)S(1)}, f32[256,128]{1,0:T(8,128)S(1)}) custom-call(s32[16]{0:T(128)} %len_ref.3, bf16[4096]{0:T(1024)(128)(2,1)} %g_ref.1, bf16[4096]{0:T(1024)(128)(2,1)} %lb_ref.1, ...), custom_call_target="tpu_custom_call" | custom-call | flops 2415919104 | bytes 25165824 | tf_op jit(solution)/shard_map/pallas_call | solution.py:395
  67.8 0.0 copy-done
  67.8 10.1 %shard_map.140 = (bf16[3,4,2,2,8,4096]{5,4,3,2,1,0:T(8,128)(2,1)}, bf16[16,3072,128]{2,1,0:T(8,128)(2,1)}, bf16[16,3072,128]{2,1,0:T(8,128)(2,1)}, bf16[16,3072,...) custom-call(s32[16]{0:T(128)S(1)} %copy-done, ...), custom_call_target="tpu_custom_call", output_to_operand_aliasing={{3}: (4, {}), {4}: (5, {})} | custom-call | tf_op jit(solution)/shard_map/pallas_call | solution.py:431
Async XLA Ops:
  0.6 67.2 %copy-start = (s32[16]{0:T(128)S(1)}, s32[16]{0:T(128)}, u32[]{:S(2)}) copy-start(s32[16]{0:T(128)} %len_ref.3) | copy-start | bytes 196

commit v4 on v3

--- a/solution.py
+++ b/solution.py
@@ -10,6 +10,8 @@
 
 LN_EPS = 1e-5
 KEY_TILE = 256
+LANES = 128
+AHEAD = 3
 FRESH_ROWS = 16
 WINDOW = 16
 N_CHIPS = 4
@@ -20,7 +22,7 @@
 BLOCK_VMEM = 32 * 1024 * 1024
 
 
-def attend_one(q_rows, k_ref, v_ref, score_ref, seq_len, fresh_k, fresh_v, fresh_mask):
+def attend_one(q_rows, k_ref, v_ref, score_ref, prob_ref, seq_len, fresh_k, fresh_v, fresh_mask):
     rows, depth = q_rows.shape
     length = k_ref.shape[0]
     to_log2 = depth ** -0.5 * math.log2(math.e)
@@ -28,20 +30,22 @@
     new_scores = lax.dot_general(q_rows, fresh_k, contract_last, preferred_element_type=jnp.float32)
     new_scores = jnp.where(fresh_mask, new_scores, -jnp.inf)
     best = None
-    lane = lax.broadcasted_iota(jnp.int32, (rows, KEY_TILE), 1)
+    lane = lax.broadcasted_iota(jnp.int32, (rows, LANES), 1)
     for start in range(0, length, KEY_TILE):
         tile = lax.dot_general(q_rows, k_ref[start:start + KEY_TILE, :], contract_last, preferred_element_type=jnp.float32)
-        tile = jnp.where(lane < seq_len - start, tile, -jnp.inf)
-        score_ref[:, start:start + KEY_TILE] = tile
-        best = tile if best is None else jnp.maximum(best, tile)
+        for first in range(0, KEY_TILE, LANES):
+            piece = jnp.where(lane < seq_len - (start + first), tile[:, first:first + LANES], -jnp.inf)
+            score_ref[:, start + first:start + first + LANES] = piece
+            best = piece if best is None else jnp.maximum(best, piece)
     top = jnp.maximum(jnp.max(best, axis=-1, keepdims=True), jnp.max(new_scores, axis=-1, keepdims=True))
     new_weights = jnp.exp2((new_scores - top) * to_log2)
-    numerator = jnp.dot(new_weights.astype(jnp.bfloat16), fresh_v, preferred_element_type=jnp.float32)
     total = None
-    for start in range(0, length, KEY_TILE):
-        weights = jnp.exp2((score_ref[:, start:start + KEY_TILE] - top) * to_log2)
+    for start in range(0, length, LANES):
+        weights = jnp.exp2((score_ref[:, start:start + LANES] - top) * to_log2)
         total = weights if total is None else total + weights
-        numerator = numerator + jnp.dot(weights.astype(jnp.bfloat16), v_ref[start:start + KEY_TILE, :], preferred_element_type=jnp.float32)
+        prob_ref[:, start:start + LANES] = weights.astype(prob_ref.dtype)
+    numerator = jnp.dot(prob_ref[...], v_ref[...], preferred_element_type=jnp.float32)
+    numerator = numerator + jnp.dot(new_weights.astype(jnp.bfloat16), fresh_v, preferred_element_type=jnp.float32)
     denominator = jnp.sum(total, axis=-1, keepdims=True) + jnp.sum(new_weights, axis=-1, keepdims=True)
     return numerator / denominator
 
@@ -49,7 +53,7 @@
 def block_kernel(
         len_ref, g_ref, lb_ref, bq_ref, bkv_ref, bo_ref, x_hbm, wq_hbm, wkv_hbm, wo_hbm, k_hbm, v_hbm,
         y_ref, k_buf, v_buf, fk_ref, fv_ref,
-        x_buf, h_buf, gain_buf, bias_buf, bo_buf, wq_buf, wkv_buf, w_buf, q_buf, q_in, q_rows, score_buf, head_buf, a_src, a_buf, lhs_buf, p_buf, mid_buf, fin_buf,
+        x_buf, h_buf, gain_buf, bias_buf, bo_buf, wq_buf, wkv_buf, w_buf, q_buf, q_in, q_rows, score_buf, prob_buf, head_buf, a_src, a_buf, lhs_buf, p_buf, mid_buf, fin_buf,
         x_sems, w_sems, kv_sems, swap_sems, q_send, q_recv, a_send, a_recv, f_send, f_recv, rs_send, rs_recv, ag_send, ag_recv):
     me = lax.axis_index('tp')
     n_dev = N_CHIPS * N_CORES
@@ -130,6 +134,9 @@
         if s == 0:
             wq_load.wait()
             wo_load.start()
+            for b in range(2 * AHEAD):
+                for copy in kv_load(b):
+                    copy.start()
         for n in range(0, q_width, 256):
             part = jnp.dot(h_buf[s], wq_buf[:, n:n + 256], preferred_element_type=jnp.float32)
             q_buf[s, :, n:n + 256] = (part + bq_row[:, n:n + 256]).astype(q_buf.dtype)
@@ -140,9 +147,6 @@
         if s == 0:
             wo_swap.start()
         q_in[me, s] = q_buf[s, seq_rows(0), :]
-    for b in range(n_seqs):
-        for copy in kv_load(b):
-            copy.start()
 
     wkv_load.wait()
     own_h = jnp.concatenate([h_buf[s, seq_rows(0), :] for s in range(n_steps)], axis=0)
@@ -293,6 +297,12 @@
             stage(p, s)
 
     def attend_pair(i, carry):
+        @pl.when(i < n_seqs // 2 - AHEAD)
+        def _():
+            for j in range(2):
+                for copy in kv_load(2 * (i + AHEAD) + j):
+                    copy.start()
+
         for j in range(2):
             for copy in kv_load(2 * i + j):
                 copy.wait()
@@ -300,7 +310,7 @@
             b = 2 * i + j
             q_one = q_rows[pl.ds(b, rows, stride=n_seqs), :].astype(jnp.bfloat16)
             new = pl.ds(pl.multiple_of(b * FRESH_ROWS, FRESH_ROWS), FRESH_ROWS)
-            out = attend_one(q_one, k_buf.at[b], v_buf.at[b], score_buf.at[j], len_ref[b],
+            out = attend_one(q_one, k_buf.at[b], v_buf.at[b], score_buf.at[j], prob_buf.at[j], len_ref[b],
                              fk_ref[new, :].astype(jnp.bfloat16), fv_ref[new, :].astype(jnp.bfloat16), fresh_mask)
             head_buf[pl.ds(b, rows, stride=n_seqs), :] = out
         @pl.when(i == 3)
@@ -410,6 +420,7 @@
                 pltpu.VMEM((n_dev, n_steps, n_seqs, q_width), bf16),
                 pltpu.VMEM((rows * n_seqs, depth), f32),
                 pltpu.VMEM((2, rows, length), f32),
+                pltpu.VMEM((2, rows, length), bf16),
                 pltpu.VMEM((rows * n_seqs, depth), f32),
                 pltpu.VMEM((N_PARTS, N_CHIPS, n_steps, part_seqs, chip_width), bf16),
                 pltpu.VMEM((N_PARTS, N_CORES, N_CHIPS, n_steps, part_seqs, chip_width), bf16),

time: 78.1 us -> 78.3 us (level)
  no operation moved by 1% of the time
where the time goes in v4:
time: 78.3 us; the launch traced here: 78.2 us
  Pallas kernels  77.5 us (99%)
    pallas_call x1, Pallas kernels, local_block(): pl.pallas_call(block_kernel, out_shape=[pltpu.VMEM(y_shape, bf16), pltpu....  67.4 us
    pallas_call x1, Pallas kernels, local_block(): pl.pallas_call(functools.partial(store_kernel, n_steps), out_shape=[jax.S...  10.1 us

profile of v4, /device:TPU:113, one launch (start us, length us, event | category | flops | bytes accessed | tf_op | source)
XLA Modules:
  0.0 78.2 jit_solution(595848241291743328)
XLA Ops:
  0.6 0.0 copy-start
  0.6 67.4 %shard_map.139 = (bf16[3,4,2,2,8,4096]{5,4,3,2,1,0:T(8,128)(2,1)S(1)}, bf16[16,3072,128]{2,1,0:T(8,128)(2,1)S(1)}, bf16[16,3072,128]{2,1,0:T(8,128)(2,1)S(1)}, f32[256,128]{1,0:T(8,128)S(1)}, f32[256,128]{1,0:T(8,128)S(1)}) custom-call(s32[16]{0:T(128)} %len_ref.3, bf16[4096]{0:T(1024)(128)(2,1)} %g_ref.1, bf16[4096]{0:T(1024)(128)(2,1)} %lb_ref.1, ...), custom_call_target="tpu_custom_call" | custom-call | flops 2415919104 | bytes 25165824 | tf_op jit(solution)/shard_map/pallas_call | solution.py:405
  68.0 0.0 copy-done
  68.1 10.1 %shard_map.140 = (bf16[3,4,2,2,8,4096]{5,4,3,2,1,0:T(8,128)(2,1)}, bf16[16,3072,128]{2,1,0:T(8,128)(2,1)}, bf16[16,3072,128]{2,1,0:T(8,128)(2,1)}, bf16[16,3072,...) custom-call(s32[16]{0:T(128)S(1)} %copy-done, ...), custom_call_target="tpu_custom_call", output_to_operand_aliasing={{3}: (4, {}), {4}: (5, {})} | custom-call | tf_op jit(solution)/shard_map/pallas_call | solution.py:442
Async XLA Ops:
  0.6 67.4 %copy-start = (s32[16]{0:T(128)S(1)}, s32[16]{0:T(128)}, u32[]{:S(2)}) copy-start(s32[16]{0:T(128)} %len_ref.3) | copy-start | bytes 196

commit v5 on v4

--- a/solution.py
+++ b/solution.py
@@ -50,41 +50,22 @@
     return numerator / denominator
 
 
-def block_kernel(
-        len_ref, g_ref, lb_ref, bq_ref, bkv_ref, bo_ref, x_hbm, wq_hbm, wkv_hbm, wo_hbm, k_hbm, v_hbm,
-        y_ref, k_buf, v_buf, fk_ref, fv_ref,
-        x_buf, h_buf, gain_buf, bias_buf, bo_buf, wq_buf, wkv_buf, w_buf, q_buf, q_in, q_rows, score_buf, prob_buf, head_buf, a_src, a_buf, lhs_buf, p_buf, mid_buf, fin_buf,
-        x_sems, w_sems, kv_sems, swap_sems, q_send, q_recv, a_send, a_recv, f_send, f_recv, rs_send, rs_recv, ag_send, ag_recv):
+def query_kernel(
+        g_ref, lb_ref, bq_ref, bkv_ref, x_hbm, wq_hbm, wkv_hbm,
+        q_in, fk_ref, fv_ref,
+        x_buf, h_buf, gain_buf, bias_buf, wq_buf, wkv_buf, q_buf,
+        x_sems, w_sems, q_send, q_recv):
     me = lax.axis_index('tp')
     n_dev = N_CHIPS * N_CORES
-    chip, core = me // N_CORES, me % N_CORES
     n_steps, group_rows, width = x_buf.shape
-    n_seqs, length, depth = k_buf.shape
-    q_width = wq_buf.shape[1]
-    dev_heads = q_width // depth
-    chip_heads = N_CORES * dev_heads
-    part_seqs = n_seqs // N_PARTS
-    rows = n_dev * n_steps * dev_heads
-    own_rows = wo_hbm.shape[0]
-    half, quarter = width // 2, width // 4
-    block = N_CORES * part_seqs
-
-    def chip_at(k):
-        return (chip + k) % N_CHIPS
-
-    def device(k):
-        return {'tp': chip_at(k) * N_CORES + core}
+    n_seqs, q_width = q_in.shape[2], wq_buf.shape[1]
+    depth = fk_ref.shape[1]
 
     def member(d):
         return (me + d) % n_dev
 
-    right, left, partner = device(1), device(3), {'tp': chip * N_CORES + 1 - core}
-
     def remote(src, dst, send, recv, to):
         return pltpu.make_async_remote_copy(src_ref=src, dst_ref=dst, send_sem=send, recv_sem=recv, device_id=to, device_id_type=MESH)
-
-    def cols(which, begin, size):
-        return pl.ds(pl.multiple_of(which * half + begin, quarter), size)
 
     def seq_rows(d):
         return pl.ds(pl.multiple_of(member(d) * n_seqs, n_seqs), n_seqs)
@@ -96,22 +77,14 @@
     def x_load(s):
         return pltpu.make_async_copy(x_hbm.at[s], x_buf.at[s], x_sems.at[s])
 
-    def kv_load(b):
-        return (pltpu.make_async_copy(k_hbm.at[b], k_buf.at[b], kv_sems.at[0, b]),
-                pltpu.make_async_copy(v_hbm.at[b], v_buf.at[b], kv_sems.at[1, b]))
-
-    own_w_rows = pl.ds(pl.multiple_of(core * own_rows, own_rows), own_rows)
     wq_load = pltpu.make_async_copy(wq_hbm, wq_buf, w_sems.at[0])
     wkv_load = pltpu.make_async_copy(wkv_hbm, wkv_buf, w_sems.at[1])
-    wo_load = pltpu.make_async_copy(wo_hbm.at[:, cols(core, 0, half)], w_buf.at[own_w_rows, :], w_sems.at[2])
-    wo_swap = remote(wo_hbm.at[:, cols(1 - core, 0, half)], w_buf.at[own_w_rows, :], swap_sems.at[0], swap_sems.at[1], partner)
     for s in range(n_steps):
         x_load(s).start()
     wq_load.start()
     wkv_load.start()
 
     bq_row = bq_ref[...].astype(jnp.float32).reshape(1, q_width)
-    bo_buf[...] = bo_ref[...].astype(jnp.float32).reshape(1, width)
     gain_buf[...] = jnp.broadcast_to(g_ref[...].astype(jnp.float32).reshape(1, width), gain_buf.shape)
     bias_buf[...] = jnp.broadcast_to(lb_ref[...].astype(jnp.float32).reshape(1, width), bias_buf.shape)
 
@@ -133,10 +106,6 @@
         lax.fori_loop(0, group_rows // LN_ROWS, norm_rows, 0)
         if s == 0:
             wq_load.wait()
-            wo_load.start()
-            for b in range(2 * AHEAD):
-                for copy in kv_load(b):
-                    copy.start()
         for n in range(0, q_width, 256):
             part = jnp.dot(h_buf[s], wq_buf[:, n:n + 256], preferred_element_type=jnp.float32)
             q_buf[s, :, n:n + 256] = (part + bq_row[:, n:n + 256]).astype(q_buf.dtype)
@@ -144,8 +113,6 @@
             pl.semaphore_wait(barrier, n_dev - 1)
         for d in range(1, n_dev):
             q_copy(s, d).start()
-        if s == 0:
-            wo_swap.start()
         q_in[me, s] = q_buf[s, seq_rows(0), :]
 
     wkv_load.wait()
@@ -162,6 +129,66 @@
     for s in range(n_steps):
         for d in range(1, n_dev):
             q_copy(s, d).wait_recv()
+    for s in range(n_steps):
+        for d in range(1, n_dev):
+            q_copy(s, d).wait_send()
+
+
+def block_kernel(
+        len_ref, q_in, fk_ref, fv_ref, bo_ref, x_hbm, wo_hbm, k_hbm, v_hbm,
+        y_ref, k_buf, v_buf,
+        x_buf, w_buf, bo_buf, q_rows, score_buf, prob_buf, head_buf, a_src, a_buf, lhs_buf, p_buf, mid_buf, fin_buf,
+        w_sems, kv_sems, swap_sems, a_send, a_recv, f_send, f_recv, rs_send, rs_recv, ag_send, ag_recv):
+    me = lax.axis_index('tp')
+    n_dev = N_CHIPS * N_CORES
+    chip, core = me // N_CORES, me % N_CORES
+    n_steps, _, half = x_buf.shape
+    width, quarter = 2 * half, half // 2
+    n_seqs, length, depth = k_buf.shape
+    q_width = q_in.shape[3]
+    dev_heads = q_width // depth
+    chip_heads = N_CORES * dev_heads
+    part_seqs = n_seqs // N_PARTS
+    rows = n_dev * n_steps * dev_heads
+    own_rows = wo_hbm.shape[0]
+    block = N_CORES * part_seqs
+
+    def chip_at(k):
+        return (chip + k) % N_CHIPS
+
+    def device(k):
+        return {'tp': chip_at(k) * N_CORES + core}
+
+    right, left, far, partner = device(1), device(3), device(2), {'tp': chip * N_CORES + 1 - core}
+
+    def remote(src, dst, send, recv, to):
+        return pltpu.make_async_remote_copy(src_ref=src, dst_ref=dst, send_sem=send, recv_sem=recv, device_id=to, device_id_type=MESH)
+
+    def cols(which, begin, size):
+        return pl.ds(pl.multiple_of(which * half + begin, quarter), size)
+
+    barrier = pltpu.get_barrier_semaphore()
+    for peer in (right, left, far, partner):
+        pl.semaphore_signal(barrier, inc=1, device_id=peer, device_id_type=MESH)
+
+    def kv_load(b):
+        return (pltpu.make_async_copy(k_hbm.at[b], k_buf.at[b], kv_sems.at[0, b]),
+                pltpu.make_async_copy(v_hbm.at[b], v_buf.at[b], kv_sems.at[1, b]))
+
+    for b in range(2 * AHEAD):
+        for copy in kv_load(b):
+            copy.start()
+    own_w_rows = pl.ds(pl.multiple_of(core * own_rows, own_rows), own_rows)
+    chip_rows = pl.ds(pl.multiple_of(chip * N_CORES * n_seqs, N_CORES * n_seqs), N_CORES * n_seqs)
+    wo_load = pltpu.make_async_copy(wo_hbm.at[:, cols(core, 0, half)], w_buf.at[own_w_rows, :], w_sems.at[0])
+    wo_swap = remote(wo_hbm.at[:, cols(1 - core, 0, half)], w_buf.at[own_w_rows, :], swap_sems.at[0], swap_sems.at[1], partner)
+    x_load = pltpu.make_async_copy(x_hbm.at[:, chip_rows, cols(core, 0, half)], x_buf, w_sems.at[1])
+    wo_load.start()
+    x_load.start()
+    bo_buf[...] = bo_ref[...].astype(jnp.float32).reshape(1, width)
+    pl.semaphore_wait(barrier, 4)
+    wo_swap.start()
+
     for u in range(n_dev):
         for s in range(n_steps):
             for h in range(dev_heads):
@@ -234,6 +261,7 @@
         if p == 0:
             wo_load.wait()
             wo_swap.wait_recv()
+            x_load.wait()
         for s in range(n_steps):
             for t in range(N_CHIPS):
                 pair = jnp.concatenate([a_buf[p, c, t, s].astype(jnp.float32) for c in range(N_CORES)], axis=0)
@@ -264,14 +292,13 @@
     def finish(p, s):
         for i in (2, 3, 4, 5):
             rs(p, s, i).wait_recv()
-        chip_rows = pl.ds(pl.multiple_of(chip * N_CORES * n_seqs, N_CORES * n_seqs), N_CORES * n_seqs)
         for begin, one, two in ((0, 1, 2), (quarter, 0, 3)):
             where = cols(core, begin, quarter)
             total = p_buf[p, s, chip, :, begin:begin + quarter].astype(jnp.float32)
             total = total + fin_buf[p, s, one].astype(jnp.float32)
             total = total + fin_buf[p, s, two].astype(jnp.float32)
             total = total + bo_buf[:, where]
-            x_part = x_buf[s, chip_rows, where].astype(jnp.float32)
+            x_part = x_buf[s, :, begin:begin + quarter].astype(jnp.float32)
             for c in range(N_CORES):
                 x_first = c * n_seqs + p * part_seqs
                 y_ref[s, chip, c, p, :, where] = (x_part[x_first:x_first + part_seqs] + total[c * part_seqs:(c + 1) * part_seqs]).astype(y_ref.dtype)
@@ -339,9 +366,6 @@
     each(relay, 1)
     each(last, 1)
     wo_swap.wait_send()
-    for s in range(n_steps):
-        for d in range(1, n_dev):
-            q_copy(s, d).wait_send()
     for p in range(N_PARTS):
         for s in range(n_steps):
             for i in range(4, 9):
@@ -402,22 +426,33 @@
         bf16, f32 = jnp.bfloat16, jnp.float32
         y_shape = (n_steps, N_CHIPS, N_CORES, N_PARTS, part_seqs, width)
         fresh_shape = (n_seqs * FRESH_ROWS, depth)
-        y_vm, k_vm, v_vm, fresh_k, fresh_v = pl.pallas_call(
-            block_kernel,
-            out_shape=[pltpu.VMEM(y_shape, bf16), pltpu.VMEM(k_cache.shape, bf16), pltpu.VMEM(v_cache.shape, bf16), pltpu.VMEM(fresh_shape, f32), pltpu.VMEM(fresh_shape, f32)],
-            in_specs=[smem] + [vmem] * 5 + [hbm] * 6,
-            out_specs=[vmem] * 5,
+        q_in, fresh_k, fresh_v = pl.pallas_call(
+            query_kernel,
+            out_shape=[pltpu.VMEM((n_dev, n_steps, n_seqs, q_width), bf16), pltpu.VMEM(fresh_shape, f32), pltpu.VMEM(fresh_shape, f32)],
+            in_specs=[vmem] * 4 + [hbm] * 3,
+            out_specs=[vmem] * 3,
             scratch_shapes=[
                 pltpu.VMEM(x_steps.shape, bf16),
                 pltpu.VMEM(x_steps.shape, bf16),
                 pltpu.VMEM((LN_ROWS, width), f32),
                 pltpu.VMEM((LN_ROWS, width), f32),
-                pltpu.VMEM((1, width), f32),
                 pltpu.VMEM(w_q.shape, bf16),
                 pltpu.VMEM(w_kv.shape, bf16),
+                pltpu.VMEM((n_steps, group_rows, q_width), bf16),
+                dma((n_steps,)), dma((2,)),
+                dma((n_steps, n_dev - 1)), dma((n_steps, n_dev - 1)),
+            ],
+            compiler_params=pltpu.CompilerParams(vmem_limit_bytes=20 * 1024 * 1024, collective_id=2, has_side_effects=True),
+        )(ln_gain, ln_bias, b_q, b_kv, x_steps, w_q, w_kv)
+        y_vm, k_vm, v_vm = pl.pallas_call(
+            block_kernel,
+            out_shape=[pltpu.VMEM(y_shape, bf16), pltpu.VMEM(k_cache.shape, bf16), pltpu.VMEM(v_cache.shape, bf16)],
+            in_specs=[smem] + [vmem] * 4 + [hbm] * 4,
+            out_specs=[vmem] * 3,
+            scratch_shapes=[
+                pltpu.VMEM((n_steps, N_CORES * n_seqs, half), bf16),
                 pltpu.VMEM((chip_width, half), bf16),
-                pltpu.VMEM((n_steps, group_rows, q_width), bf16),
-                pltpu.VMEM((n_dev, n_steps, n_seqs, q_width), bf16),
+                pltpu.VMEM((1, width), f32),
                 pltpu.VMEM((rows * n_seqs, depth), f32),
                 pltpu.VMEM((2, rows, length), f32),
                 pltpu.VMEM((2, rows, length), bf16),
@@ -428,17 +463,14 @@
                 pltpu.VMEM((N_PARTS, n_steps, N_CHIPS, block, half), bf16),
                 pltpu.VMEM((N_PARTS, n_steps, 2, block, half // 2), bf16),
                 pltpu.VMEM((N_PARTS, n_steps, 4, block, half // 2), bf16),
-                dma((n_steps,)), dma((3,)), dma((2, n_seqs)), dma((2,)),
-                dma((n_steps, n_dev - 1)), dma((n_steps, n_dev - 1)),
+                dma((2,)), dma((2, n_seqs)), dma((2,)),
                 dma((N_PARTS, 3)), dma((N_PARTS, 3)),
                 dma((N_PARTS, N_CHIPS)), dma((N_PARTS, N_CHIPS)),
                 dma((N_PARTS, n_steps, 6)), dma((N_PARTS, n_steps, 6)),
                 dma((N_PARTS, n_steps, 9)), dma((N_PARTS, n_steps, 9)),
             ],
             compiler_params=pltpu.CompilerParams(vmem_limit_bytes=BLOCK_VMEM, collective_id=1, has_side_effects=True),
-            cost_estimate=pl.CostEstimate(flops=4 * n_seqs * rows * length * depth, bytes_accessed=4 * n_seqs * length * depth, transcendentals=n_seqs * rows * length),
-        )(seq_lens, ln_gain, ln_bias, b_q, b_kv, b_out,
-          x_steps, w_q, w_kv, w_out, k_cache, v_cache)
+        )(seq_lens, q_in, fresh_k, fresh_v, b_out, x_steps, w_out, k_cache, v_cache)
         y_steps, k_out, v_out, _, _ = pl.pallas_call(
             functools.partial(store_kernel, n_steps),
             out_shape=[jax.ShapeDtypeStruct(y_shape, bf16), jax.ShapeDtypeStruct(k_cache.shape, bf16), jax.ShapeDtypeStruct(v_cache.shape, bf16), pltpu.VMEM(k_cache.shape, bf16), pltpu.VMEM(v_cache.shape, bf16)],

time: 78.3 us -> 90.7 us (1.16)
  local copies, waits for them, and re-layouts: 0.01 us -> 10.4 us
  Pallas kernels: 77.5 us -> 79.2 us
    pallas_call x0 -> x1, Pallas kernels: none -> 17 us  [local_block(): pl.pallas_call(query_kernel, out_shape=[pltpu.VMEM((n_dev, n_steps, n_seq...]
    pallas_call x1, Pallas kernels: 67.4 us -> 52.1 us  [local_block(): pl.pallas_call(block_kernel, out_shape=[pltpu.VMEM(y_shape, bf16), pltpu....]
    unnamed x2 -> x26, local copies, waits for them, and re-layouts: 0.01 us -> 10.4 us
where the time goes in v5:
time: 90.7 us; the launch traced here: 90.4 us
  Pallas kernels  79.2 us (87%)
  local copies, waits for them, and re-layouts  10.4 us (11%)
    pallas_call x1, Pallas kernels, local_block(): pl.pallas_call(block_kernel, out_shape=[pltpu.VMEM(y_shape, bf16), pltpu....  52.1 us
    pallas_call x1, Pallas kernels, local_block(): pl.pallas_call(query_kernel, out_shape=[pltpu.VMEM((n_dev, n_steps, n_seq...  17 us
    unnamed x26, local copies, waits for them, and re-layouts  10.4 us
    pallas_call x1, Pallas kernels, local_block(): pl.pallas_call(functools.partial(store_kernel, n_steps), out_shape=[jax.S...  10.1 us

profile of v5, /device:TPU:113, one launch (start us, length us, event | category | flops | bytes accessed | tf_op | source)
XLA Modules:
  0.0 90.4 jit_solution(3562160798173653843)
XLA Ops:
  0.6 0.0 copy-start
  0.6 1.9 %copy-done = bf16[3,128,4096]{2,1,0:T(8,128)(2,1)S(1)} copy-done((bf16[3,128,4096]{2,1,0:T(8,128)(2,1)S(1)}, bf16[3,128,4096]{2,1,0:T(8,128)(2,1)}, u32[]{:S(2)}) %copy-start) | copy-done | bytes 3145752
  2.5 0.0 copy-start.1
  2.5 2.2 %copy-done.1 = bf16[4096,512]{1,0:T(8,128)(2,1)S(1)} copy-done((bf16[4096,512]{1,0:T(8,128)(2,1)S(1)}, bf16[4096,512]{1,0:T(8,128)(2,1)}, u32[]{:S(2)}) %copy-start.1) | copy-done | bytes 4194328
  4.7 0.0 copy-start.2
  4.7 1.6 %copy-done.2 = bf16[4096,256]{1,0:T(8,128)(2,1)S(1)} copy-done((bf16[4096,256]{1,0:T(8,128)(2,1)S(1)}, bf16[4096,256]{1,0:T(8,128)(2,1)}, u32[]{:S(2)}) %copy-start.2) | copy-done | bytes 2097176
  6.3 0.0 copy-start.8
  6.3 0.7 copy-done.8
  7.0 0.0 copy-start.9
  7.0 0.7 copy-done.9
  7.7 0.0 copy-start.11
  7.7 0.7 copy-done.11
  8.4 0.0 copy-start.12
  8.4 0.7 copy-done.12
  9.0 17.0 %shard_map.139 = (bf16[8,3,16,512]{3,2,1,0:T(8,128)(2,1)S(1)}, f32[256,128]{1,0:T(8,128)S(1)}, f32[256,128]{1,0:T(8,128)S(1)}) custom-call(bf16[4096]{0:T(1024)(128)(2,1)S(1)} %copy-done.8, bf16[4096]{0:T(1024)(128)(2,1)S(1)} %copy-done.9, bf16[512]{0:T(512)(128)(2,1)S(1)} %copy-done.11, bf16[256]{0:T(256)(128)(2,1)S(1)} %copy-done.12, ...), custom_call_target="tpu_custom_call" | custom-call | tf_op jit(solution)/shard_map/pallas_call | solution.py:429
  26.0 0.0 copy-start.3
  26.0 0.6 copy-done.3
  26.7 0.0 copy-start.5
  26.7 0.7 copy-done.5
  27.3 0.0 copy-start.7
  27.3 0.7 copy-done.7
  28.1 0.0 copy-start.4
  28.1 0.0 copy-start.6
  28.1 0.0 copy-start.10
  28.1 52.1 %shard_map.140 = (bf16[3,4,2,2,8,4096]{5,4,3,2,1,0:T(8,128)(2,1)S(1)}, bf16[16,3072,128]{2,1,0:T(8,128)(2,1)S(1)}, bf16[16,3072,128]{2,1,0:T(8,128)(2,1)S(1)}) custom-call(s32[16]{0:T(128)} %len_ref.3, bf16[8,3,16,512]{3,2,1,0:T(8,128)(2,1)} %copy-done.7, f32[256,128]{1,0:T(8,128)} %copy-done.3, f32[256,128]{1,0:T(8,128)} %copy-done.5, ...), custom_call_target="tpu_custom_call" | custom-call | tf_op jit(solution)/shard_map/pallas_call | solution.py:447
  80.2 0.0 copy-done.4
  80.2 0.0 copy-done.6
  80.2 0.0 copy-done.10
  80.2 10.1 %shard_map.141 = (bf16[3,4,2,2,8,4096]{5,4,3,2,1,0:T(8,128)(2,1)}, bf16[16,3072,128]{2,1,0:T(8,128)(2,1)}, bf16[16,3072,128]{2,1,0:T(8,128)(2,1)}, bf16[16,3072,...) custom-call(s32[16]{0:T(128)S(1)} %copy-done.10, ...), custom_call_target="tpu_custom_call", output_to_operand_aliasing={{3}: (4, {}), {4}: (5, {})} | custom-call | tf_op jit(solution)/shard_map/pallas_call | solution.py:474
Async XLA Ops:
  0.6 1.9 %copy-start = (bf16[3,128,4096]{2,1,0:T(8,128)(2,1)S(1)}, bf16[3,128,4096]{2,1,0:T(8,128)(2,1)}, u32[]{:S(2)}) copy-start(bf16[3,128,4096]{2,1,0:T(8,128)(2,1)} %x_hbm.3) | copy-start | bytes 9437188
  2.5 2.2 %copy-start.1 = (bf16[4096,512]{1,0:T(8,128)(2,1)S(1)}, bf16[4096,512]{1,0:T(8,128)(2,1)}, u32[]{:S(2)}) copy-start(bf16[4096,512]{1,0:T(8,128)(2,1)} %wq_hbm.1) | copy-start | bytes 12582916
  4.7 1.6 %copy-start.2 = (bf16[4096,256]{1,0:T(8,128)(2,1)S(1)}, bf16[4096,256]{1,0:T(8,128)(2,1)}, u32[]{:S(2)}) copy-start(bf16[4096,256]{1,0:T(8,128)(2,1)} %wkv_hbm.1) | copy-start | bytes 6291460
  6.3 0.7 copy-start.8
  7.0 0.7 copy-start.9
  7.7 0.7 copy-start.11
  8.4 0.7 copy-start.12
  26.0 0.7 copy-start.3
  26.7 0.7 copy-start.5
  27.3 0.7 copy-start.7
  28.1 52.2 %copy-start.4 = (f32[256,128]{1,0:T(8,128)S(1)}, f32[256,128]{1,0:T(8,128)}, u32[]{:S(2)}) copy-start(f32[256,128]{1,0:T(8,128)} %copy-done.3) | copy-start | bytes 393220
  28.1 52.2 %copy-start.6 = (f32[256,128]{1,0:T(8,128)S(1)}, f32[256,128]{1,0:T(8,128)}, u32[]{:S(2)}) copy-start(f32[256,128]{1,0:T(8,128)} %copy-done.5) | copy-start | bytes 393220
  28.1 52.2 %copy-start.10 = (s32[16]{0:T(128)S(1)}, s32[16]{0:T(128)}, u32[]{:S(2)}) copy-start(s32[16]{0:T(128)} %len_ref.3) | copy-start | bytes 196

commit v6 on v4

--- a/solution.py
+++ b/solution.py
@@ -11,7 +11,7 @@
 LN_EPS = 1e-5
 KEY_TILE = 256
 LANES = 128
-AHEAD = 3
+ROW_BLOCK = 16
 FRESH_ROWS = 16
 WINDOW = 16
 N_CHIPS = 4
@@ -22,32 +22,41 @@
 BLOCK_VMEM = 32 * 1024 * 1024
 
 
-def attend_one(q_rows, k_ref, v_ref, score_ref, prob_ref, seq_len, fresh_k, fresh_v, fresh_mask):
+CONTRACT_LAST = (((1,), (1,)), ((), ()))
+
+
+def score_one(q_rows, k_ref, score_ref, seq_len):
+    lane = lax.broadcasted_iota(jnp.int32, (q_rows.shape[0], LANES), 1)
+    for start in range(0, k_ref.shape[0], KEY_TILE):
+        tile = lax.dot_general(q_rows, k_ref[start:start + KEY_TILE, :], CONTRACT_LAST, preferred_element_type=jnp.float32)
+        for first in range(0, KEY_TILE, LANES):
+            score_ref[:, start + first:start + first + LANES] = jnp.where(lane < seq_len - (start + first), tile[:, first:first + LANES], -jnp.inf)
+
+
+def attend_one(q_rows, v_ref, score_ref, prob_ref, fresh_k, fresh_v, fresh_mask):
     rows, depth = q_rows.shape
-    length = k_ref.shape[0]
+    length = v_ref.shape[0]
     to_log2 = depth ** -0.5 * math.log2(math.e)
-    contract_last = (((1,), (1,)), ((), ()))
-    new_scores = lax.dot_general(q_rows, fresh_k, contract_last, preferred_element_type=jnp.float32)
+    new_scores = lax.dot_general(q_rows, fresh_k, CONTRACT_LAST, preferred_element_type=jnp.float32)
     new_scores = jnp.where(fresh_mask, new_scores, -jnp.inf)
-    best = None
-    lane = lax.broadcasted_iota(jnp.int32, (rows, LANES), 1)
-    for start in range(0, length, KEY_TILE):
-        tile = lax.dot_general(q_rows, k_ref[start:start + KEY_TILE, :], contract_last, preferred_element_type=jnp.float32)
-        for first in range(0, KEY_TILE, LANES):
-            piece = jnp.where(lane < seq_len - (start + first), tile[:, first:first + LANES], -jnp.inf)
-            score_ref[:, start + first:start + first + LANES] = piece
-            best = piece if best is None else jnp.maximum(best, piece)
-    top = jnp.maximum(jnp.max(best, axis=-1, keepdims=True), jnp.max(new_scores, axis=-1, keepdims=True))
-    new_weights = jnp.exp2((new_scores - top) * to_log2)
-    total = None
-    for start in range(0, length, LANES):
-        weights = jnp.exp2((score_ref[:, start:start + LANES] - top) * to_log2)
-        total = weights if total is None else total + weights
-        prob_ref[:, start:start + LANES] = weights.astype(prob_ref.dtype)
+    new_weights, totals = [], []
+    for row in range(0, rows, ROW_BLOCK):
+        part = slice(row, row + ROW_BLOCK)
+        best = score_ref[part, 0:LANES]
+        for start in range(LANES, length, LANES):
+            best = jnp.maximum(best, score_ref[part, start:start + LANES])
+        top = jnp.maximum(jnp.max(best, axis=-1, keepdims=True), jnp.max(new_scores[part], axis=-1, keepdims=True))
+        new = jnp.exp2((new_scores[part] - top) * to_log2)
+        total = None
+        for start in range(0, length, LANES):
+            weights = jnp.exp2((score_ref[part, start:start + LANES] - top) * to_log2)
+            total = weights if total is None else total + weights
+            prob_ref[part, start:start + LANES] = weights.astype(prob_ref.dtype)
+        new_weights.append(new)
+        totals.append(jnp.sum(total, axis=-1, keepdims=True) + jnp.sum(new, axis=-1, keepdims=True))
     numerator = jnp.dot(prob_ref[...], v_ref[...], preferred_element_type=jnp.float32)
-    numerator = numerator + jnp.dot(new_weights.astype(jnp.bfloat16), fresh_v, preferred_element_type=jnp.float32)
-    denominator = jnp.sum(total, axis=-1, keepdims=True) + jnp.sum(new_weights, axis=-1, keepdims=True)
-    return numerator / denominator
+    numerator = numerator + jnp.dot(jnp.concatenate(new_weights, axis=0).astype(jnp.bfloat16), fresh_v, preferred_element_type=jnp.float32)
+    return numerator / jnp.concatenate(totals, axis=0)
 
 
 def block_kernel(
@@ -105,10 +114,8 @@
     wkv_load = pltpu.make_async_copy(wkv_hbm, wkv_buf, w_sems.at[1])
     wo_load = pltpu.make_async_copy(wo_hbm.at[:, cols(core, 0, half)], w_buf.at[own_w_rows, :], w_sems.at[2])
     wo_swap = remote(wo_hbm.at[:, cols(1 - core, 0, half)], w_buf.at[own_w_rows, :], swap_sems.at[0], swap_sems.at[1], partner)
-    for s in range(n_steps):
-        x_load(s).start()
+    x_load(0).start()
     wq_load.start()
-    wkv_load.start()
 
     bq_row = bq_ref[...].astype(jnp.float32).reshape(1, q_width)
     bo_buf[...] = bo_ref[...].astype(jnp.float32).reshape(1, width)
@@ -120,6 +127,10 @@
 
     for s in range(n_steps):
         x_load(s).wait()
+        if s == 0:
+            for later in range(1, n_steps):
+                x_load(later).start()
+            wkv_load.start()
 
         def norm_rows(i, carry):
             where = pl.ds(pl.multiple_of(i * LN_ROWS, LN_ROWS), LN_ROWS)
@@ -134,9 +145,6 @@
         if s == 0:
             wq_load.wait()
             wo_load.start()
-            for b in range(2 * AHEAD):
-                for copy in kv_load(b):
-                    copy.start()
         for n in range(0, q_width, 256):
             part = jnp.dot(h_buf[s], wq_buf[:, n:n + 256], preferred_element_type=jnp.float32)
             q_buf[s, :, n:n + 256] = (part + bq_row[:, n:n + 256]).astype(q_buf.dtype)
@@ -146,6 +154,9 @@
             q_copy(s, d).start()
         if s == 0:
             wo_swap.start()
+        for b in range(s * n_seqs // 4, n_seqs if s == n_steps - 1 else (s + 1) * n_seqs // 4):
+            for copy in kv_load(b):
+                copy.start()
         q_in[me, s] = q_buf[s, seq_rows(0), :]
 
     wkv_load.wait()
@@ -296,47 +307,56 @@
         for s in range(n_steps):
             stage(p, s)
 
+    def query(b):
+        return q_rows[pl.ds(b, rows, stride=n_seqs), :].astype(jnp.bfloat16)
+
+    def score(b, slot):
+        score_one(query(b), k_buf.at[b], score_buf.at[slot], len_ref[b])
+
+    def attend(b, slot):
+        new = pl.ds(pl.multiple_of(b * FRESH_ROWS, FRESH_ROWS), FRESH_ROWS)
+        out = attend_one(query(b), v_buf.at[b], score_buf.at[slot], prob_buf.at[slot],
+                         fk_ref[new, :].astype(jnp.bfloat16), fv_ref[new, :].astype(jnp.bfloat16), fresh_mask)
+        head_buf[pl.ds(b, rows, stride=n_seqs), :] = out
+
+    def wait_caches(b):
+        for copy in kv_load(b):
+            copy.wait()
+
     def attend_pair(i, carry):
-        @pl.when(i < n_seqs // 2 - AHEAD)
+        first = 2 * i
+        after = jnp.minimum(first + 2, n_seqs - 1)
+        wait_caches(first + 1)
+
+        @pl.when(first + 2 < n_seqs)
         def _():
-            for j in range(2):
-                for copy in kv_load(2 * (i + AHEAD) + j):
-                    copy.start()
-
-        for j in range(2):
-            for copy in kv_load(2 * i + j):
-                copy.wait()
-        for j in range(2):
-            b = 2 * i + j
-            q_one = q_rows[pl.ds(b, rows, stride=n_seqs), :].astype(jnp.bfloat16)
-            new = pl.ds(pl.multiple_of(b * FRESH_ROWS, FRESH_ROWS), FRESH_ROWS)
-            out = attend_one(q_one, k_buf.at[b], v_buf.at[b], score_buf.at[j], prob_buf.at[j], len_ref[b],
-                             fk_ref[new, :].astype(jnp.bfloat16), fv_ref[new, :].astype(jnp.bfloat16), fresh_mask)
-            head_buf[pl.ds(b, rows, stride=n_seqs), :] = out
-        @pl.when(i == 3)
+            wait_caches(after)
+
+        score(first + 1, 1)
+        attend(first, 0)
+        score(after, 0)
+        attend(first + 1, 1)
+
+        @pl.when(i == n_seqs // 4 - 1)
         def _():
             pack(0)
-
-        @pl.when(i == 5)
-        def _():
-            forward(0)
-            partial(0)
-
-        @pl.when(i == 7)
-        def _():
-            each(middle, 0)
         return carry
 
+    wait_caches(0)
+    score(0, 0)
     lax.fori_loop(0, n_seqs // 2, attend_pair, 0)
     pack(1)
-    each(finish, 0)
+    forward(0)
+    partial(0)
     forward(1)
     partial(1)
+    each(middle, 0)
+    each(middle, 1)
+    each(finish, 0)
+    each(finish, 1)
     each(relay, 0)
-    each(middle, 1)
+    each(relay, 1)
     each(last, 0)
-    each(finish, 1)
-    each(relay, 1)
     each(last, 1)
     wo_swap.wait_send()
     for s in range(n_steps):

time: 78.3 us -> 77.4 us (0.989)
  Pallas kernels: 77.5 us -> 76.6 us
    pallas_call x1, Pallas kernels: 67.4 us -> 66.4 us  [local_block(): pl.pallas_call(block_kernel, out_shape=[pltpu.VMEM(y_shape, bf16), pltpu....]
where the time goes in v6:
time: 77.4 us; the launch traced here: 77.2 us
  Pallas kernels  76.6 us (99%)
    pallas_call x1, Pallas kernels, local_block(): pl.pallas_call(block_kernel, out_shape=[pltpu.VMEM(y_shape, bf16), pltpu....  66.4 us
    pallas_call x1, Pallas kernels, local_block(): pl.pallas_call(functools.partial(store_kernel, n_steps), out_shape=[jax.S...  10.1 us

profile of v6, /device:TPU:113, one launch (start us, length us, event | category | flops | bytes accessed | tf_op | source)
XLA Modules:
  0.0 77.2 jit_solution(5534805980399356709)
XLA Ops:
  0.6 0.0 copy-start
  0.6 66.4 %shard_map.139 = (bf16[3,4,2,2,8,4096]{5,4,3,2,1,0:T(8,128)(2,1)S(1)}, bf16[16,3072,128]{2,1,0:T(8,128)(2,1)S(1)}, bf16[16,3072,128]{2,1,0:T(8,128)(2,1)S(1)}, f32[256,128]{1,0:T(8,128)S(1)}, f32[256,128]{1,0:T(8,128)S(1)}) custom-call(s32[16]{0:T(128)} %len_ref.3, bf16[4096]{0:T(1024)(128)(2,1)} %g_ref.1, bf16[4096]{0:T(1024)(128)(2,1)} %lb_ref.1, ...), custom_call_target="tpu_custom_call" | custom-call | flops 2415919104 | bytes 25165824 | tf_op jit(solution)/shard_map/pallas_call | solution.py:425
  67.1 0.0 copy-done
  67.1 10.1 %shard_map.140 = (bf16[3,4,2,2,8,4096]{5,4,3,2,1,0:T(8,128)(2,1)}, bf16[16,3072,128]{2,1,0:T(8,128)(2,1)}, bf16[16,3072,128]{2,1,0:T(8,128)(2,1)}, bf16[16,3072,...) custom-call(s32[16]{0:T(128)S(1)} %copy-done, ...), custom_call_target="tpu_custom_call", output_to_operand_aliasing={{3}: (4, {}), {4}: (5, {})} | custom-call | tf_op jit(solution)/shard_map/pallas_call | solution.py:462
Async XLA Ops:
  0.6 66.5 %copy-start = (s32[16]{0:T(128)S(1)}, s32[16]{0:T(128)}, u32[]{:S(2)}) copy-start(s32[16]{0:T(128)} %len_ref.3) | copy-start | bytes 196

commit v7 on v1

v7 whole, which is shorter than its diff:
```python
import functools
import math

import jax
import jax.numpy as jnp
from jax import lax
from jax.experimental import pallas as pl
from jax.experimental.pallas import tpu as pltpu
from jax.sharding import PartitionSpec as P

LN_EPS = 1e-5
KEY_TILE = 256
LANES = 128
AHEAD = 4
FRESH_ROWS = 16
WINDOW = 16
N_CHIPS = 4
N_CORES = 2
LN_ROWS = 16
MESH = pl.DeviceIdType.MESH
FRONT_VMEM = 62 * 1024 * 1024
ATTENTION_VMEM = 62 * 1024 * 1024
BACK_VMEM = 59 * 1024 * 1024
KEY_RANGE = 1024


def attend_one(length, q_rows, k_ref, v_ref, score_ref, prob_ref, seq_len, fresh_k, fresh_v, fresh_mask):
    rows, depth = q_rows.shape
    to_log2 = depth ** -0.5 * math.log2(math.e)
    contract_last = (((1,), (1,)), ((), ()))
    new_scores = lax.dot_general(q_rows, fresh_k, contract_last, preferred_element_type=jnp.float32)
    new_scores = jnp.where(fresh_mask, new_scores, -jnp.inf)
    best = None
    lane = lax.broadcasted_iota(jnp.int32, (rows, LANES), 1)
    for start in range(0, length, KEY_TILE):
        tile = lax.dot_general(q_rows, k_ref[start:start + KEY_TILE, :], contract_last, preferred_element_type=jnp.float32)
        for first in range(0, KEY_TILE, LANES):
            piece = jnp.where(lane < seq_len - (start + first), tile[:, first:first + LANES], -jnp.inf)
            score_ref[:, start + first:start + first + LANES] = piece
            best = piece if best is None else jnp.maximum(best, piece)
    top = jnp.maximum(jnp.max(best, axis=-1, keepdims=True), jnp.max(new_scores, axis=-1, keepdims=True))
    new_weights = jnp.exp2((new_scores - top) * to_log2)
    total = None
    for start in range(0, length, LANES):
        weights = jnp.exp2((score_ref[:, start:start + LANES] - top) * to_log2)
        total = weights if total is None else total + weights
        prob_ref[:, start:start + LANES] = weights.astype(prob_ref.dtype)
    numerator = jnp.dot(prob_ref[:, :length], v_ref[:length, :], preferred_element_type=jnp.float32)
    numerator = numerator + jnp.dot(new_weights.astype(jnp.bfloat16), fresh_v, preferred_element_type=jnp.float32)
    denominator = jnp.sum(total, axis=-1, keepdims=True) + jnp.sum(new_weights, axis=-1, keepdims=True)
    return numerator / denominator


def query_kernel(
        g_ref, lb_ref, bq_ref, bkv_ref, x_hbm, wq_hbm, wkv_hbm,
        q_in, fk_ref, fv_ref,
        x_buf, h_buf, gain_buf, bias_buf, wq_buf, wkv_buf, q_buf,
        x_sems, w_sems, q_send, q_recv):
    me = lax.axis_index('tp')
    n_dev = N_CHIPS * N_CORES
    n_steps, group_rows, width = x_buf.shape
    n_seqs, q_width = q_in.shape[2], wq_buf.shape[1]
    depth = fk_ref.shape[1]

    def member(d):
        return (me + d) % n_dev

    def remote(src, dst, send, recv, to):
        return pltpu.make_async_remote_copy(src_ref=src, dst_ref=dst, send_sem=send, recv_sem=recv, device_id=to, device_id_type=MESH)

    def seq_rows(d):
        return pl.ds(pl.multiple_of(member(d) * n_seqs, n_seqs), n_seqs)

    barrier = pltpu.get_barrier_semaphore()
    for d in range(1, n_dev):
        pl.semaphore_signal(barrier, inc=1, device_id={'tp': member(d)}, device_id_type=MESH)

    def x_load(s):
        return pltpu.make_async_copy(x_hbm.at[s], x_buf.at[s], x_sems.at[s])

    wq_load = pltpu.make_async_copy(wq_hbm, wq_buf, w_sems.at[0])
    wkv_load = pltpu.make_async_copy(wkv_hbm, wkv_buf, w_sems.at[1])
    x_load(0).start()
    wq_load.start()

    bq_row = bq_ref[...].astype(jnp.float32).reshape(1, q_width)
    gain_buf[...] = jnp.broadcast_to(g_ref[...].astype(jnp.float32).reshape(1, width), gain_buf.shape)
    bias_buf[...] = jnp.broadcast_to(lb_ref[...].astype(jnp.float32).reshape(1, width), bias_buf.shape)

    def q_copy(s, d):
        return remote(q_buf.at[s, seq_rows(d)], q_in.at[me, s], q_send.at[s, d - 1], q_recv.at[s, d - 1], {'tp': member(d)})

    for s in range(n_steps):
        x_load(s).wait()
        if s == 0:
            for later in range(1, n_steps):
                x_load(later).start()
            wkv_load.start()

        def norm_rows(i, carry):
            where = pl.ds(pl.multiple_of(i * LN_ROWS, LN_ROWS), LN_ROWS)
            x_float = x_buf[s, where, :].astype(jnp.float32)
            centered = x_float - jnp.mean(x_float, axis=-1, keepdims=True)
            row_var = jnp.mean(centered * centered, axis=-1, keepdims=True)
            scaled = centered * lax.rsqrt(row_var + LN_EPS)
            h_buf[s, where, :] = (scaled * gain_buf[...] + bias_buf[...]).astype(h_buf.dtype)
            return carry

        lax.fori_loop(0, group_rows // LN_ROWS, norm_rows, 0)
        if s == 0:
            wq_load.wait()
        for n in range(0, q_width, 256):
            part = jnp.dot(h_buf[s], wq_buf[:, n:n + 256], preferred_element_type=jnp.float32)
            q_buf[s, :, n:n + 256] = (part + bq_row[:, n:n + 256]).astype(q_buf.dtype)
        if s == 0:
            pl.semaphore_wait(barrier, n_dev - 1)
        for d in range(1, n_dev):
            q_copy(s, d).start()
        q_in[me, s] = q_buf[s, seq_rows(0), :]

    wkv_load.wait()
    own_h = jnp.concatenate([h_buf[s, seq_rows(0), :] for s in range(n_steps)], axis=0)
    fresh = jnp.dot(own_h, wkv_buf[...], preferred_element_type=jnp.float32) + bkv_ref[...].astype(jnp.float32).reshape(1, -1)
    fresh = fresh.astype(jnp.bfloat16).astype(jnp.float32)
    fk_ref[...] = jnp.zeros_like(fk_ref)
    fv_ref[...] = jnp.zeros_like(fv_ref)
    for s in range(n_steps):
        where = pl.ds(s, n_seqs, stride=FRESH_ROWS)
        fk_ref[where, :] = fresh[s * n_seqs:(s + 1) * n_seqs, :depth]
        fv_ref[where, :] = fresh[s * n_seqs:(s + 1) * n_seqs, depth:]

    for s in range(n_steps):
        for d in range(1, n_dev):
            q_copy(s, d).wait_recv()
    for s in range(n_steps):
        for d in range(1, n_dev):
            q_copy(s, d).wait_send()


def attention_kernel(len_ref, q_in, fk_ref, fv_ref, k_hbm, v_hbm, out_ref, k_out, v_out, k_buf, v_buf, q_rows, score_buf, prob_buf, head_buf, sems, out_sems):
    n_seqs, length, depth = k_buf.shape
    n_dev, n_steps, _, q_width = q_in.shape
    dev_heads = q_width // depth
    rows = n_dev * n_steps * dev_heads

    def fetch(b):
        return (pltpu.make_async_copy(k_hbm.at[b], k_buf.at[b], sems.at[0, b]),
                pltpu.make_async_copy(v_hbm.at[b], v_buf.at[b], sems.at[1, b]))

    def store(b):
        return (pltpu.make_async_copy(k_buf.at[b], k_out.at[b], out_sems.at[0, b]),
                pltpu.make_async_copy(v_buf.at[b], v_out.at[b], out_sems.at[1, b]))

    def patch(b, buf, fresh):
        start = pl.multiple_of(jnp.minimum(len_ref[b] // 8 * 8, length - WINDOW), 8)
        offset = len_ref[b] - start
        row = lax.broadcasted_iota(jnp.int32, (WINDOW, depth), 0)
        window = buf[b, pl.ds(start, WINDOW), :].astype(jnp.float32)
        for s in range(n_steps):
            window = jnp.where(row == offset + s, fresh[pl.ds(b * FRESH_ROWS + s, 1), :], window)
        buf[b, pl.ds(start, WINDOW), :] = window.astype(buf.dtype)

    def land(i):
        for j in range(2):
            b = 2 * i + j
            for copy in fetch(b):
                copy.wait()
            patch(b, k_buf, fk_ref)
            patch(b, v_buf, fv_ref)
            for copy in store(b):
                copy.start()

    for b in range(2 * AHEAD):
        for copy in fetch(b):
            copy.start()
    for u in range(n_dev):
        for s in range(n_steps):
            for h in range(dev_heads):
                first = ((u * n_steps + s) * dev_heads + h) * n_seqs
                q_rows[first:first + n_seqs, :] = q_in[u, s, :, h * depth:(h + 1) * depth].astype(jnp.float32)
    shape = (rows, FRESH_ROWS)
    step_of_row = lax.broadcasted_iota(jnp.int32, shape, 0) // dev_heads % n_steps
    fresh_mask = lax.broadcasted_iota(jnp.int32, shape, 1) <= step_of_row
    land(0)

    def attend_pair(i, carry):
        @pl.when(i < n_seqs // 2 - AHEAD)
        def _():
            for j in range(2):
                for copy in fetch(2 * (i + AHEAD) + j):
                    copy.start()

        @pl.when(i < n_seqs // 2 - 1)
        def _():
            land(i + 1)

        longest = jnp.maximum(len_ref[2 * i], len_ref[2 * i + 1])
        for first in range(0, length, KEY_RANGE):
            @pl.when((longest > first) & (longest <= first + KEY_RANGE))
            def _():
                for j in range(2):
                    b = 2 * i + j
                    q_one = q_rows[pl.ds(b, rows, stride=n_seqs), :].astype(jnp.bfloat16)
                    new = pl.ds(pl.multiple_of(b * FRESH_ROWS, FRESH_ROWS), FRESH_ROWS)
                    out = attend_one(first + KEY_RANGE, q_one, k_buf.at[b], v_buf.at[b], score_buf.at[j], prob_buf.at[j], len_ref[b],
                                     fk_ref[new, :].astype(jnp.bfloat16), fv_ref[new, :].astype(jnp.bfloat16), fresh_mask)
                    head_buf[pl.ds(b, rows, stride=n_seqs), :] = out
        return carry

    lax.fori_loop(0, n_seqs // 2, attend_pair, 0)
    for t in range(N_CHIPS):
        for s in range(n_steps):
            pieces = []
            for h in range(N_CORES * dev_heads):
                u = t * N_CORES + h // dev_heads
                first = ((u * n_steps + s) * dev_heads + h % dev_heads) * n_seqs
                pieces.append(head_buf[first:first + n_seqs, :])
            out_ref[t, s] = jnp.concatenate(pieces, axis=1).astype(out_ref.dtype)
    for b in range(n_seqs):
        for copy in store(b):
            copy.wait()


def project_kernel(n_steps, a_ref, w_ref, x_ref, b_ref, y_ref, w_buf, x_buf, a_buf, p_buf, mid_buf, fin_buf,
                   load_sems, w_sems, a_send, a_recv, f_send, f_recv, rs_send, rs_recv, ag_send, ag_recv):
    me = lax.axis_index('tp')
    chip, core = me // 2, me % 2
    n_seqs = a_ref.shape[2]
    block = 2 * n_seqs
    own_rows, width = w_ref.shape
    half = width // 2
    quarter = half // 2

    def chip_at(k):
        return (chip + k) % N_CHIPS

    def device(k):
        return {'tp': chip_at(k) * 2 + core}

    right, left, far, partner = device(1), device(3), device(2), {'tp': chip * 2 + 1 - core}

    barrier = pltpu.get_barrier_semaphore()
    for peer in (right, left, far, partner):
        pl.semaphore_signal(barrier, inc=1, device_id=peer, device_id_type=MESH)

    def cols(which, begin, size):
        return pl.ds(pl.multiple_of(which * half + begin, quarter), size)

    def rows_of(k):
        return pl.ds(pl.multiple_of(chip_at(k) * block, block), block)

    own_w_rows = pl.ds(pl.multiple_of(core * own_rows, own_rows), own_rows)
    w_load = pltpu.make_async_copy(w_ref.at[:, cols(core, 0, half)], w_buf.at[own_w_rows, :], load_sems.at[0])
    x_load = pltpu.make_async_copy(x_ref.at[:, rows_of(0), cols(core, 0, half)], x_buf, load_sems.at[1])
    w_load.start()
    x_load.start()
    pl.semaphore_wait(barrier, 4)

    def remote(src, dst, send, recv, to):
        return pltpu.make_async_remote_copy(src_ref=src, dst_ref=dst, send_sem=send, recv_sem=recv, device_id=to, device_id_type=MESH)

    def a_copy(s, d):
        return remote(a_ref.at[chip_at(d), s], a_buf.at[core, chip, s], a_send.at[s, d - 1], a_recv.at[s, d - 1], device(d))

    def a_forward(s, d):
        src = a_ref.at[chip, s] if d == 0 else a_buf.at[core, chip_at(N_CHIPS - d), s]
        return remote(src, a_buf.at[core, chip_at(N_CHIPS - d), s], f_send.at[s, d], f_recv.at[s, d], partner)

    for s in range(n_steps):
        for d in (2, 1, 3):
            a_copy(s, d).start()
        if s == 0:
            w_swap = remote(w_ref.at[:, cols(1 - core, 0, half)], w_buf.at[own_w_rows, :], w_sems.at[0], w_sems.at[1], partner)
            w_swap.start()
    for s in range(n_steps):
        a_forward(s, 0).start()
        a_buf[core, chip, s] = a_ref[chip, s]

    low, high = pl.ds(0, quarter), pl.ds(quarter, quarter)

    def rs(s, i):
        part = p_buf.at[s]
        src, dst, to = (
            (part.at[rows_of(2), low], mid_buf.at[s, 0], right),
            (part.at[rows_of(2), high], mid_buf.at[s, 1], left),
            (part.at[rows_of(1), high], fin_buf.at[s, 0], right),
            (part.at[rows_of(3), low], fin_buf.at[s, 1], left),
            (part.at[rows_of(1), low], fin_buf.at[s, 2], right),
            (part.at[rows_of(3), high], fin_buf.at[s, 3], left),
        )[i]
        return remote(src, dst, rs_send.at[s, i], rs_recv.at[s, i], to)

    def ag(s, i):
        k, begin, size, to = (
            (0, 0, half, right),
            (0, 0, half, left),
            (3, 0, quarter, right),
            (1, quarter, quarter, left),
            (0, 0, half, partner),
            (3, 0, half, partner),
            (1, 0, half, partner),
            (2, 0, quarter, partner),
            (2, quarter, quarter, partner),
        )[i]
        where = y_ref.at[s, rows_of(k), cols(core, begin, size)]
        return remote(where, where, ag_send.at[s, i], ag_recv.at[s, i], to)

    def partial(s):
        for d in (1, 3, 2):
            a_copy(s, d).wait_recv()
            a_forward(s, d).start()
        for d in range(N_CHIPS):
            a_forward(s, d).wait_recv()
        if s == 0:
            w_load.wait()
            w_swap.wait_recv()
        lhs = jnp.concatenate([a_buf[c, t, s] for t in range(N_CHIPS) for c in range(2)], axis=0)
        for n in range(0, half, 512):
            p_buf[s, :, n:n + 512] = jnp.dot(lhs, w_buf[:, n:n + 512], preferred_element_type=jnp.float32).astype(p_buf.dtype)
        for i in range(4):
            rs(s, i).start()

    def add_into(target, other):
        target[...] = (target[...].astype(jnp.float32) + other[...].astype(jnp.float32)).astype(target.dtype)

    def middle(s):
        rs(s, 0).wait_recv()
        add_into(p_buf.at[s, rows_of(1), low], mid_buf.at[s, 0])
        rs(s, 4).start()
        rs(s, 1).wait_recv()
        add_into(p_buf.at[s, rows_of(3), high], mid_buf.at[s, 1])
        rs(s, 5).start()

    def finish(s):
        for i in (2, 3, 4, 5):
            rs(s, i).wait_recv()
        if s == 0:
            x_load.wait()
        bias_row = b_ref[cols(core, 0, half)].astype(jnp.float32).reshape(1, half)
        for begin, one, two in ((0, 1, 2), (quarter, 0, 3)):
            total = p_buf[s, rows_of(0), begin:begin + quarter].astype(jnp.float32)
            total = total + fin_buf[s, one].astype(jnp.float32)
            total = total + fin_buf[s, two].astype(jnp.float32)
            total = total + x_buf[s, :, begin:begin + quarter].astype(jnp.float32)
            total = total + bias_row[:, begin:begin + quarter]
            y_ref[s, rows_of(0), cols(core, begin, quarter)] = total.astype(y_ref.dtype)
        for i in (0, 1, 4):
            ag(s, i).start()

    def relay(s):
        ag(s, 0).wait_recv()
        ag(s, 2).start()
        ag(s, 5).start()
        ag(s, 1).wait_recv()
        ag(s, 3).start()
        ag(s, 6).start()

    def last(s):
        ag(s, 2).wait_recv()
        ag(s, 7).start()
        ag(s, 3).wait_recv()
        ag(s, 8).start()

    stages = (partial, middle, finish, relay, last)
    for t in range(n_steps + len(stages) - 1):
        for i, stage in enumerate(stages):
            if 0 <= t - i < n_steps:
                stage(t - i)
    w_swap.wait_send()
    for s in range(n_steps):
        for i in range(4, 9):
            ag(s, i).wait_recv()
        for i in range(9):
            ag(s, i).wait_send()
        for i in range(6):
            rs(s, i).wait_send()
        for d in (1, 2, 3):
            a_copy(s, d).wait_send()
        for d in range(N_CHIPS):
            a_forward(s, d).wait_send()


def solution(mesh):
    def local_block(x_steps, seq_lens, k_cache, v_cache, ln_gain, ln_bias, w_q, b_q, w_kv, b_kv, w_out, b_out):
        n_steps, group_rows, width = x_steps.shape
        n_seqs, length, depth = k_cache.shape
        q_width = w_q.shape[1]
        n_dev = N_CHIPS * N_CORES
        rows = n_dev * n_steps * q_width // depth
        chip_width, half = N_CORES * q_width, width // 2
        block = N_CORES * n_seqs
        smem = pl.BlockSpec(memory_space=pltpu.SMEM)
        vmem = pl.BlockSpec(memory_space=pltpu.VMEM)
        hbm = pl.BlockSpec(memory_space=pltpu.HBM)
        dma = pltpu.SemaphoreType.DMA
        bf16, f32 = jnp.bfloat16, jnp.float32
        fresh_shape = (n_seqs * FRESH_ROWS, depth)
        q_in, fresh_k, fresh_v = pl.pallas_call(
            query_kernel,
            out_shape=[pltpu.VMEM((n_dev, n_steps, n_seqs, q_width), bf16), pltpu.VMEM(fresh_shape, f32), pltpu.VMEM(fresh_shape, f32)],
            in_specs=[vmem] * 4 + [hbm] * 3,
            out_specs=[vmem] * 3,
            scratch_shapes=[
                pltpu.VMEM(x_steps.shape, bf16),
                pltpu.VMEM(x_steps.shape, bf16),
                pltpu.VMEM((LN_ROWS, width), f32),
                pltpu.VMEM((LN_ROWS, width), f32),
                pltpu.VMEM(w_q.shape, bf16),
                pltpu.VMEM(w_kv.shape, bf16),
                pltpu.VMEM((n_steps, group_rows, q_width), bf16),
                dma((n_steps,)), dma((2,)),
                dma((n_steps, n_dev - 1)), dma((n_steps, n_dev - 1)),
            ],
            compiler_params=pltpu.CompilerParams(vmem_limit_bytes=FRONT_VMEM, collective_id=2, has_side_effects=True),
        )(ln_gain, ln_bias, b_q, b_kv, x_steps, w_q, w_kv)
        attn, k_out, v_out = pl.pallas_call(
            attention_kernel,
            out_shape=[pltpu.VMEM((N_CHIPS, n_steps, n_seqs, chip_width), bf16), jax.ShapeDtypeStruct(k_cache.shape, bf16), jax.ShapeDtypeStruct(v_cache.shape, bf16)],
            in_specs=[smem] + [vmem] * 3 + [hbm] * 2,
            out_specs=[vmem, hbm, hbm],
            scratch_shapes=[
                pltpu.VMEM(k_cache.shape, bf16),
                pltpu.VMEM(v_cache.shape, bf16),
                pltpu.VMEM((rows * n_seqs, depth), f32),
                pltpu.VMEM((2, rows, length), f32),
                pltpu.VMEM((2, rows, length), bf16),
                pltpu.VMEM((rows * n_seqs, depth), f32),
                dma((2, n_seqs)), dma((2, n_seqs)),
            ],
            compiler_params=pltpu.CompilerParams(vmem_limit_bytes=ATTENTION_VMEM),
            cost_estimate=pl.CostEstimate(flops=4 * n_seqs * rows * length * depth, bytes_accessed=8 * n_seqs * length * depth, transcendentals=n_seqs * rows * length),
        )(seq_lens, q_in, fresh_k, fresh_v, k_cache, v_cache)
        y_steps = pl.pallas_call(
            functools.partial(project_kernel, n_steps),
            out_shape=jax.ShapeDtypeStruct(x_steps.shape, bf16),
            in_specs=[vmem, hbm, hbm, vmem],
            out_specs=vmem,
            scratch_shapes=[
                pltpu.VMEM((chip_width, half), bf16),
                pltpu.VMEM((n_steps, block, half), bf16),
                pltpu.VMEM((2, N_CHIPS, n_steps, n_seqs, chip_width), bf16),
                pltpu.VMEM((n_steps, N_CHIPS * block, half), bf16),
                pltpu.VMEM((n_steps, 2, block, half // 2), bf16),
                pltpu.VMEM((n_steps, 4, block, half // 2), bf16),
                dma((2,)), dma((2,)),
                dma((n_steps, 3)), dma((n_steps, 3)),
                dma((n_steps, 4)), dma((n_steps, 4)),
                dma((n_steps, 6)), dma((n_steps, 6)),
                dma((n_steps, 9)), dma((n_steps, 9)),
            ],
            compiler_params=pltpu.CompilerParams(vmem_limit_bytes=BACK_VMEM, collective_id=1, has_side_effects=True),
            cost_estimate=pl.CostEstimate(flops=2 * n_steps * N_CHIPS * block * chip_width * half, bytes_accessed=4 * width * chip_width, transcendentals=0),
        )(attn, w_out, x_steps, b_out)
        return y_steps, k_out, v_out

    row_spec = P(('dp', 'tp'), None, None)
    return jax.shard_map(
        local_block,
        mesh=mesh,
        in_specs=(P(None, 'dp', None), P(('dp', 'tp')), row_spec, row_spec, P(None), P(None), P(None, 'tp'), P('tp'), P(None, None), P(None), P('tp', None), P(None)),
        out_specs=(P(None, 'dp', None), row_spec, row_spec),
        check_vma=False,
    )
```

time: 91.9 us -> 87.4 us (0.951)
  Pallas kernels: 58.5 us -> 79.9 us
  waiting for transfers between devices: 6.27 us -> 0 us
  other arithmetic: 6.16 us -> 0 us
  starting transfers between devices: 6.02 us -> 0 us
  local copies, waits for them, and re-layouts: 10.5 us -> 6.68 us
  matrix products: 3.3 us -> 0 us
    pallas_call x2 -> x3, Pallas kernels: 58.5 us -> 79.9 us  [the longest x1 40.3 us: local_block(): pl.pallas_call(functools.partial(project_kernel, n_steps), out_shape=jax....]
    all_to_all x1 -> x0, waiting for transfers between devices: 6.27 us -> none  [local_block(): q_local = lax.all_to_all(q_part, 'tp', 1, 2, tiled=True)]
    all_to_all x1 -> x0, starting transfers between devices: 6.02 us -> none  [local_block(): q_local = lax.all_to_all(q_part, 'tp', 1, 2, tiled=True)]
    reduce_sum x2 -> x0, other arithmetic: 3.62 us -> none  [the longest x1 2.66 us: layer_norm(): row_mean = jnp.mean(x_float, axis=-1, keepdims=True)]
    dot_general x2 -> x0, matrix products: 3.3 us -> none  [the longest x1 1.83 us: local_block(): jnp.einsum('sbk,kn->sbn', normed, w_q, preferred_element_type=jnp.float32)]
    convert_element_type x6 -> x0, other arithmetic: 2.53 us -> none  [the longest x1 1.65 us: layer_norm(): (scaled * ln_gain.astype(jnp.float32) + ln_bias.astype(jnp.float32)).asty...]
    pad x2 -> x0, local copies, waits for them, and re-layouts: 1.27 us -> none  [the longest x1 0.64 us: attention(): jnp.pad(fresh_v, pad)]
    convert_element_type x1 -> x0, local copies, waits for them, and re-layouts: 1.13 us -> none  [local_block(): (jnp.einsum('sbk,kn->sbn', normed, w_q, preferred_element_type=jnp.float3...]
  transfers between devices with their start and end apart: 1 -> 0, of which waited for: 1 -> 0; matrix products, arithmetic and copies ran while one was open for 3% -> 0% of each run, Pallas kernels for 0% -> 0%
where the time goes in v7:
time: 87.4 us; the launch traced here: 87.3 us
  Pallas kernels  79.9 us (91%)
  local copies, waits for them, and re-layouts  6.68 us (8%)
    pallas_call x1, Pallas kernels, local_block(): pl.pallas_call(functools.partial(project_kernel, n_steps), out_shape=jax....  40.3 us
    pallas_call x1, Pallas kernels, local_block(): pl.pallas_call(attention_kernel, out_shape=[pltpu.VMEM((N_CHIPS, n_steps,...  21.3 us
    pallas_call x1, Pallas kernels, local_block(): pl.pallas_call(query_kernel, out_shape=[pltpu.VMEM((n_dev, n_steps, n_seq...  18.3 us
    unnamed x9, local copies, waits for them, and re-layouts  6.68 us

profile of v7, /device:TPU:113, one launch (start us, length us, event | category | flops | bytes accessed | tf_op | source)
XLA Modules:
  0.0 87.3 jit_solution(15906068215561955382)
XLA Ops:
  0.6 18.3 %shard_map.139 = (bf16[8,3,16,512]{3,2,1,0:T(8,128)(2,1)S(1)}, f32[256,128]{1,0:T(8,128)S(1)}, f32[256,128]{1,0:T(8,128)S(1)}) custom-call(bf16[4096]{0:T(1024)(128)(2,1)} %g_ref.1, bf16[4096]{0:T(1024)(128)(2,1)} %lb_ref.1, bf16[512]{0:T(512)(128)(2,1)} %bq_ref.1, bf16[256]{0:T(256)(128)(2,1)} %bkv_ref.1, bf16[3,128,4096]{2,1,0:T(8,128)(2,1)} %x_ref.1, ...), custom_call_target="tpu_custom_call" | custom-call | tf_op jit(solution)/shard_map/pallas_call | solution.py:398
  18.9 0.0 copy-start.1
  18.9 0.7 copy-done.1
  19.7 0.0 copy-start.2
  19.7 0.6 copy-done.2
  20.3 0.0 copy-start.3
  20.3 0.6 copy-done.3
  21.0 21.3 %shard_map.140 = (bf16[4,3,16,1024]{3,2,1,0:T(8,128)(2,1)S(1)}, bf16[16,3072,128]{2,1,0:T(8,128)(2,1)}, bf16[16,3072,128]{2,1,0:T(8,128)(2,1)}) custom-call(s32[16]{0:T(128)} %len_ref.1, bf16[8,3,16,512]{3,2,1,0:T(8,128)(2,1)} %copy-done.1, f32[256,128]{1,0:T(8,128)} %copy-done.2, f32[256,128]{1,0:T(8,128)} %copy-done.3, bf16[16,3072,128]{2,1,0:T(8,128)(2,1)} %k_hbm.1, ...), custom_call_target="tpu_custom_call" | custom-call | flops 2415919104 | bytes 50331648 | tf_op jit(solution)/shard_map/pallas_call | solution.py:416
  42.3 0.0 copy-start
  42.3 0.7 copy-done
  43.0 40.3 %shard_map.141 = bf16[3,128,4096]{2,1,0:T(8,128)(2,1)} custom-call(bf16[4,3,16,1024]{3,2,1,0:T(8,128)(2,1)} %copy-done, bf16[512,4096]{1,0:T(8,128)(2,1)} %w_ref.1, bf16[3,128,4096]{2,1,0:T(8,128)(2,1)} %x_ref.1, bf16[4096]{0:T(1024)(128)(2,1)} %b_ref.1), custom_call_target="tpu_custom_call" | custom-call | flops 1610612736 | bytes 16777216 | tf_op jit(solution)/shard_map/pallas_call | solution.py:433
  83.4 3.9 %copy.16 = bf16[3,128,4096]{2,1,0:T(8,128)(2,1)} copy(bf16[3,128,4096]{2,1,0:T(8,128)(2,1)} %shard_map.141) | data formatting | bytes 6291456
Async XLA Ops:
  18.9 0.7 copy-start.1
  19.7 0.6 copy-start.2
  20.3 0.7 copy-start.3
  42.3 0.7 copy-start

commit v8 on v6

--- a/solution.py
+++ b/solution.py
@@ -11,7 +11,6 @@
 LN_EPS = 1e-5
 KEY_TILE = 256
 LANES = 128
-ROW_BLOCK = 16
 FRESH_ROWS = 16
 WINDOW = 16
 N_CHIPS = 4
@@ -25,49 +24,42 @@
 CONTRACT_LAST = (((1,), (1,)), ((), ()))
 
 
-def score_one(q_rows, k_ref, score_ref, seq_len):
-    lane = lax.broadcasted_iota(jnp.int32, (q_rows.shape[0], LANES), 1)
-    for start in range(0, k_ref.shape[0], KEY_TILE):
-        tile = lax.dot_general(q_rows, k_ref[start:start + KEY_TILE, :], CONTRACT_LAST, preferred_element_type=jnp.float32)
-        for first in range(0, KEY_TILE, LANES):
-            score_ref[:, start + first:start + first + LANES] = jnp.where(lane < seq_len - (start + first), tile[:, first:first + LANES], -jnp.inf)
-
-
-def attend_one(q_rows, v_ref, score_ref, prob_ref, fresh_k, fresh_v, fresh_mask):
-    rows, depth = q_rows.shape
-    length = v_ref.shape[0]
+def score_tile(q_rows, k_ref, score_ref, start, seq_len, best):
+    tile = lax.dot_general(q_rows, k_ref[start:start + KEY_TILE, :], CONTRACT_LAST, preferred_element_type=jnp.float32)
+    lane = lax.broadcasted_iota(jnp.int32, tile.shape, 1)
+    tile = jnp.where(lane < seq_len - start, tile, -jnp.inf)
+    score_ref[:, start:start + KEY_TILE] = tile
+    high = jnp.maximum(tile[:, :LANES], tile[:, LANES:])
+    return high if best is None else jnp.maximum(best, high)
+
+
+def attend_one(q_rows, v_ref, score_ref, best, fresh_k, fresh_v, fresh_mask, beside):
+    length, depth = v_ref.shape
     to_log2 = depth ** -0.5 * math.log2(math.e)
     new_scores = lax.dot_general(q_rows, fresh_k, CONTRACT_LAST, preferred_element_type=jnp.float32)
     new_scores = jnp.where(fresh_mask, new_scores, -jnp.inf)
-    new_weights, totals = [], []
-    for row in range(0, rows, ROW_BLOCK):
-        part = slice(row, row + ROW_BLOCK)
-        best = score_ref[part, 0:LANES]
-        for start in range(LANES, length, LANES):
-            best = jnp.maximum(best, score_ref[part, start:start + LANES])
-        top = jnp.maximum(jnp.max(best, axis=-1, keepdims=True), jnp.max(new_scores[part], axis=-1, keepdims=True))
-        new = jnp.exp2((new_scores[part] - top) * to_log2)
-        total = None
-        for start in range(0, length, LANES):
-            weights = jnp.exp2((score_ref[part, start:start + LANES] - top) * to_log2)
-            total = weights if total is None else total + weights
-            prob_ref[part, start:start + LANES] = weights.astype(prob_ref.dtype)
-        new_weights.append(new)
-        totals.append(jnp.sum(total, axis=-1, keepdims=True) + jnp.sum(new, axis=-1, keepdims=True))
-    numerator = jnp.dot(prob_ref[...], v_ref[...], preferred_element_type=jnp.float32)
-    numerator = numerator + jnp.dot(jnp.concatenate(new_weights, axis=0).astype(jnp.bfloat16), fresh_v, preferred_element_type=jnp.float32)
-    return numerator / jnp.concatenate(totals, axis=0)
+    top = jnp.maximum(jnp.max(best, axis=-1, keepdims=True), jnp.max(new_scores, axis=-1, keepdims=True))
+    new_weights = jnp.exp2((new_scores - top) * to_log2)
+    numerator = jnp.dot(new_weights.astype(jnp.bfloat16), fresh_v, preferred_element_type=jnp.float32)
+    total = None
+    for start in range(0, length, KEY_TILE):
+        beside(start)
+        weights = jnp.exp2((score_ref[:, start:start + KEY_TILE] - top) * to_log2)
+        folded = weights[:, :LANES] + weights[:, LANES:]
+        total = folded if total is None else total + folded
+        numerator = numerator + jnp.dot(weights.astype(jnp.bfloat16), v_ref[start:start + KEY_TILE, :], preferred_element_type=jnp.float32)
+    return numerator / (jnp.sum(total, axis=-1, keepdims=True) + jnp.sum(new_weights, axis=-1, keepdims=True))
 
 
 def block_kernel(
         len_ref, g_ref, lb_ref, bq_ref, bkv_ref, bo_ref, x_hbm, wq_hbm, wkv_hbm, wo_hbm, k_hbm, v_hbm,
         y_ref, k_buf, v_buf, fk_ref, fv_ref,
-        x_buf, h_buf, gain_buf, bias_buf, bo_buf, wq_buf, wkv_buf, w_buf, q_buf, q_in, q_rows, score_buf, prob_buf, head_buf, a_src, a_buf, lhs_buf, p_buf, mid_buf, fin_buf,
+        x_buf, own_x, own_h, h_buf, gain_buf, bias_buf, bo_buf, wq_buf, wkv_buf, w_buf, swap_buf, q_buf, q_in, q_rows, score_buf, best_buf, head_buf, a_src, a_buf, lhs_buf, p_buf, mid_buf, fin_buf,
         x_sems, w_sems, kv_sems, swap_sems, q_send, q_recv, a_send, a_recv, f_send, f_recv, rs_send, rs_recv, ag_send, ag_recv):
     me = lax.axis_index('tp')
     n_dev = N_CHIPS * N_CORES
     chip, core = me // N_CORES, me % N_CORES
-    n_steps, group_rows, width = x_buf.shape
+    n_steps, _, width = own_x.shape
     n_seqs, length, depth = k_buf.shape
     q_width = wq_buf.shape[1]
     dev_heads = q_width // depth
@@ -95,25 +87,24 @@
     def cols(which, begin, size):
         return pl.ds(pl.multiple_of(which * half + begin, quarter), size)
 
-    def seq_rows(d):
-        return pl.ds(pl.multiple_of(member(d) * n_seqs, n_seqs), n_seqs)
-
     barrier = pltpu.get_barrier_semaphore()
     for d in range(1, n_dev):
         pl.semaphore_signal(barrier, inc=1, device_id={'tp': member(d)}, device_id_type=MESH)
 
-    def x_load(s):
-        return pltpu.make_async_copy(x_hbm.at[s], x_buf.at[s], x_sems.at[s])
+    def x_load(p):
+        return pltpu.make_async_copy(x_hbm.at[:, :, p], x_buf.at[p], x_sems.at[p])
 
     def kv_load(b):
         return (pltpu.make_async_copy(k_hbm.at[b], k_buf.at[b], kv_sems.at[0, b]),
                 pltpu.make_async_copy(v_hbm.at[b], v_buf.at[b], kv_sems.at[1, b]))
 
+    own_x_loads = [pltpu.make_async_copy(x_hbm.at[:, me, p], own_x.at[:, p * part_seqs:(p + 1) * part_seqs, :], x_sems.at[N_PARTS + p]) for p in range(N_PARTS)]
     own_w_rows = pl.ds(pl.multiple_of(core * own_rows, own_rows), own_rows)
     wq_load = pltpu.make_async_copy(wq_hbm, wq_buf, w_sems.at[0])
     wkv_load = pltpu.make_async_copy(wkv_hbm, wkv_buf, w_sems.at[1])
     wo_load = pltpu.make_async_copy(wo_hbm.at[:, cols(core, 0, half)], w_buf.at[own_w_rows, :], w_sems.at[2])
-    wo_swap = remote(wo_hbm.at[:, cols(1 - core, 0, half)], w_buf.at[own_w_rows, :], swap_sems.at[0], swap_sems.at[1], partner)
+    swap_load = pltpu.make_async_copy(wo_hbm.at[:, cols(1 - core, 0, half)], swap_buf, w_sems.at[3])
+    wo_swap = remote(swap_buf, w_buf.at[own_w_rows, :], swap_sems.at[0], swap_sems.at[1], partner)
     x_load(0).start()
     wq_load.start()
 
@@ -122,46 +113,61 @@
     gain_buf[...] = jnp.broadcast_to(g_ref[...].astype(jnp.float32).reshape(1, width), gain_buf.shape)
     bias_buf[...] = jnp.broadcast_to(lb_ref[...].astype(jnp.float32).reshape(1, width), bias_buf.shape)
 
-    def q_copy(s, d):
-        return remote(q_buf.at[s, seq_rows(d)], q_in.at[me, s], q_send.at[s, d - 1], q_recv.at[s, d - 1], {'tp': member(d)})
-
-    for s in range(n_steps):
-        x_load(s).wait()
-        if s == 0:
-            for later in range(1, n_steps):
+    def norm(x_float):
+        centered = x_float - jnp.mean(x_float, axis=-1, keepdims=True)
+        row_var = jnp.mean(centered * centered, axis=-1, keepdims=True)
+        scaled = centered * lax.rsqrt(row_var + LN_EPS)
+        return (scaled * gain_buf[...] + bias_buf[...]).astype(h_buf.dtype)
+
+    def q_copy(p, d):
+        return remote(q_buf.at[p, :, member(d)], q_in.at[p, me], q_send.at[p, d - 1], q_recv.at[p, d - 1], {'tp': member(d)})
+
+    group = LN_ROWS // part_seqs
+    for p in range(N_PARTS):
+        x_load(p).wait()
+        if p == 0:
+            for later in range(1, N_PARTS):
                 x_load(later).start()
+            for copy in own_x_loads:
+                copy.start()
             wkv_load.start()
 
-        def norm_rows(i, carry):
-            where = pl.ds(pl.multiple_of(i * LN_ROWS, LN_ROWS), LN_ROWS)
-            x_float = x_buf[s, where, :].astype(jnp.float32)
-            centered = x_float - jnp.mean(x_float, axis=-1, keepdims=True)
-            row_var = jnp.mean(centered * centered, axis=-1, keepdims=True)
-            scaled = centered * lax.rsqrt(row_var + LN_EPS)
-            h_buf[s, where, :] = (scaled * gain_buf[...] + bias_buf[...]).astype(h_buf.dtype)
-            return carry
-
-        lax.fori_loop(0, group_rows // LN_ROWS, norm_rows, 0)
-        if s == 0:
+        for s in range(n_steps):
+            def norm_rows(i, carry):
+                x_float = jnp.concatenate([x_buf[p, s, i * group + j].astype(jnp.float32) for j in range(group)], axis=0)
+                where = pl.ds(pl.multiple_of((s * n_dev // group + i) * LN_ROWS, LN_ROWS), LN_ROWS)
+                h_buf[p, where, :] = norm(x_float)
+                return carry
+
+            lax.fori_loop(0, n_dev // group, norm_rows, 0)
+        if p == 0:
             wq_load.wait()
+            swap_load.start()
             wo_load.start()
         for n in range(0, q_width, 256):
-            part = jnp.dot(h_buf[s], wq_buf[:, n:n + 256], preferred_element_type=jnp.float32)
-            q_buf[s, :, n:n + 256] = (part + bq_row[:, n:n + 256]).astype(q_buf.dtype)
-        if s == 0:
+            part = jnp.dot(h_buf[p], wq_buf[:, n:n + 256], preferred_element_type=jnp.float32) + bq_row[:, n:n + 256]
+            for s in range(n_steps):
+                for u in range(n_dev):
+                    first = (s * n_dev + u) * part_seqs
+                    q_buf[p, s, u, :, n:n + 256] = part[first:first + part_seqs].astype(q_buf.dtype)
+        if p == 0:
             pl.semaphore_wait(barrier, n_dev - 1)
         for d in range(1, n_dev):
-            q_copy(s, d).start()
-        if s == 0:
+            q_copy(p, d).start()
+        if p == 0:
+            swap_load.wait()
             wo_swap.start()
-        for b in range(s * n_seqs // 4, n_seqs if s == n_steps - 1 else (s + 1) * n_seqs // 4):
+        for b in range(p * part_seqs, (p + 1) * part_seqs):
             for copy in kv_load(b):
                 copy.start()
-        q_in[me, s] = q_buf[s, seq_rows(0), :]
-
+        q_in[p, me] = q_buf[p, :, me]
+
+    for copy in own_x_loads:
+        copy.wait()
+    for s in range(n_steps):
+        own_h[s * n_seqs:(s + 1) * n_seqs, :] = norm(own_x[s].astype(jnp.float32))
     wkv_load.wait()
-    own_h = jnp.concatenate([h_buf[s, seq_rows(0), :] for s in range(n_steps)], axis=0)
-    fresh = jnp.dot(own_h, wkv_buf[...], preferred_element_type=jnp.float32) + bkv_ref[...].astype(jnp.float32).reshape(1, -1)
+    fresh = jnp.dot(own_h[...], wkv_buf[...], preferred_element_type=jnp.float32) + bkv_ref[...].astype(jnp.float32).reshape(1, -1)
     fresh = fresh.astype(jnp.bfloat16).astype(jnp.float32)
     fk_ref[...] = jnp.zeros_like(fk_ref)
     fv_ref[...] = jnp.zeros_like(fv_ref)
@@ -170,14 +176,14 @@
         fk_ref[where, :] = fresh[s * n_seqs:(s + 1) * n_seqs, :depth]
         fv_ref[where, :] = fresh[s * n_seqs:(s + 1) * n_seqs, depth:]
 
-    for s in range(n_steps):
+    def unpack(p):
         for d in range(1, n_dev):
-            q_copy(s, d).wait_recv()
-    for u in range(n_dev):
-        for s in range(n_steps):
-            for h in range(dev_heads):
-                first = ((u * n_steps + s) * dev_heads + h) * n_seqs
-                q_rows[first:first + n_seqs, :] = q_in[u, s, :, h * depth:(h + 1) * depth].astype(jnp.float32)
+            q_copy(p, d).wait_recv()
+        for u in range(n_dev):
+            for s in range(n_steps):
+                for h in range(dev_heads):
+                    first = ((u * n_steps + s) * dev_heads + h) * n_seqs + p * part_seqs
+                    q_rows[first:first + part_seqs, :] = q_in[p, u, s, :, h * depth:(h + 1) * depth].astype(jnp.float32)
 
     shape = (rows, FRESH_ROWS)
     step_of_row = lax.broadcasted_iota(jnp.int32, shape, 0) // dev_heads % n_steps
@@ -275,17 +281,15 @@
     def finish(p, s):
         for i in (2, 3, 4, 5):
             rs(p, s, i).wait_recv()
-        chip_rows = pl.ds(pl.multiple_of(chip * N_CORES * n_seqs, N_CORES * n_seqs), N_CORES * n_seqs)
         for begin, one, two in ((0, 1, 2), (quarter, 0, 3)):
             where = cols(core, begin, quarter)
             total = p_buf[p, s, chip, :, begin:begin + quarter].astype(jnp.float32)
             total = total + fin_buf[p, s, one].astype(jnp.float32)
             total = total + fin_buf[p, s, two].astype(jnp.float32)
             total = total + bo_buf[:, where]
-            x_part = x_buf[s, chip_rows, where].astype(jnp.float32)
             for c in range(N_CORES):
-                x_first = c * n_seqs + p * part_seqs
-                y_ref[s, chip, c, p, :, where] = (x_part[x_first:x_first + part_seqs] + total[c * part_seqs:(c + 1) * part_seqs]).astype(y_ref.dtype)
+                x_part = x_buf[p, s, chip * N_CORES + c, :, where].astype(jnp.float32)
+                y_ref[s, chip, c, p, :, where] = (x_part + total[c * part_seqs:(c + 1) * part_seqs]).astype(y_ref.dtype)
         for i in (0, 1, 4):
             ag(p, s, i).start()
 
@@ -310,13 +314,17 @@
     def query(b):
         return q_rows[pl.ds(b, rows, stride=n_seqs), :].astype(jnp.bfloat16)
 
-    def score(b, slot):
-        score_one(query(b), k_buf.at[b], score_buf.at[slot], len_ref[b])
-
-    def attend(b, slot):
+    def attend(b, slot, after):
         new = pl.ds(pl.multiple_of(b * FRESH_ROWS, FRESH_ROWS), FRESH_ROWS)
-        out = attend_one(query(b), v_buf.at[b], score_buf.at[slot], prob_buf.at[slot],
-                         fk_ref[new, :].astype(jnp.bfloat16), fv_ref[new, :].astype(jnp.bfloat16), fresh_mask)
+        q_after = query(after)
+        maxima = [None]
+
+        def beside(start):
+            maxima[0] = score_tile(q_after, k_buf.at[after], score_buf.at[1 - slot], start, len_ref[after], maxima[0])
+
+        out = attend_one(query(b), v_buf.at[b], score_buf.at[slot], best_buf[slot],
+                         fk_ref[new, :].astype(jnp.bfloat16), fv_ref[new, :].astype(jnp.bfloat16), fresh_mask, beside)
+        best_buf[1 - slot] = maxima[0]
         head_buf[pl.ds(b, rows, stride=n_seqs), :] = out
 
     def wait_caches(b):
@@ -332,37 +340,46 @@
         def _():
             wait_caches(after)
 
-        score(first + 1, 1)
-        attend(first, 0)
-        score(after, 0)
-        attend(first + 1, 1)
-
-        @pl.when(i == n_seqs // 4 - 1)
+        attend(first, 0, first + 1)
+        attend(first + 1, 1, after)
+
+        @pl.when(i == part_seqs // 2 - 2)
+        def _():
+            unpack(1)
+
+        @pl.when(i == part_seqs // 2 - 1)
         def _():
             pack(0)
+
+        @pl.when(i == n_seqs // 2 - 2)
+        def _():
+            forward(0)
+
         return carry
 
+    unpack(0)
     wait_caches(0)
-    score(0, 0)
+    best = None
+    for start in range(0, length, KEY_TILE):
+        best = score_tile(query(0), k_buf.at[0], score_buf.at[0], start, len_ref[0], best)
+    best_buf[0] = best
     lax.fori_loop(0, n_seqs // 2, attend_pair, 0)
     pack(1)
-    forward(0)
     partial(0)
     forward(1)
+    each(middle, 0)
     partial(1)
-    each(middle, 0)
+    each(finish, 0)
     each(middle, 1)
-    each(finish, 0)
+    each(relay, 0)
     each(finish, 1)
-    each(relay, 0)
+    each(last, 0)
     each(relay, 1)
-    each(last, 0)
     each(last, 1)
     wo_swap.wait_send()
-    for s in range(n_steps):
+    for p in range(N_PARTS):
         for d in range(1, n_dev):
-            q_copy(s, d).wait_send()
-    for p in range(N_PARTS):
+            q_copy(p, d).wait_send()
         for s in range(n_steps):
             for i in range(4, 9):
                 ag(p, s, i).wait_recv()
@@ -407,7 +424,7 @@
 
 def solution(mesh):
     def local_block(x_steps, seq_lens, k_cache, v_cache, ln_gain, ln_bias, w_q, b_q, w_kv, b_kv, w_out, b_out):
-        n_steps, group_rows, width = x_steps.shape
+        n_steps, _, width = x_steps.shape
         n_seqs, length, depth = k_cache.shape
         q_width = w_q.shape[1]
         n_dev = N_CHIPS * N_CORES
@@ -428,19 +445,22 @@
             in_specs=[smem] + [vmem] * 5 + [hbm] * 6,
             out_specs=[vmem] * 5,
             scratch_shapes=[
-                pltpu.VMEM(x_steps.shape, bf16),
-                pltpu.VMEM(x_steps.shape, bf16),
+                pltpu.VMEM((N_PARTS, n_steps, n_dev, part_seqs, width), bf16),
+                pltpu.VMEM((n_steps, n_seqs, width), bf16),
+                pltpu.VMEM((n_steps * n_seqs, width), bf16),
+                pltpu.VMEM((N_PARTS, n_steps * n_dev * part_seqs, width), bf16),
                 pltpu.VMEM((LN_ROWS, width), f32),
                 pltpu.VMEM((LN_ROWS, width), f32),
                 pltpu.VMEM((1, width), f32),
                 pltpu.VMEM(w_q.shape, bf16),
                 pltpu.VMEM(w_kv.shape, bf16),
                 pltpu.VMEM((chip_width, half), bf16),
-                pltpu.VMEM((n_steps, group_rows, q_width), bf16),
-                pltpu.VMEM((n_dev, n_steps, n_seqs, q_width), bf16),
+                pltpu.VMEM((q_width, half), bf16),
+                pltpu.VMEM((N_PARTS, n_steps, n_dev, part_seqs, q_width), bf16),
+                pltpu.VMEM((N_PARTS, n_dev, n_steps, part_seqs, q_width), bf16),
                 pltpu.VMEM((rows * n_seqs, depth), f32),
                 pltpu.VMEM((2, rows, length), f32),
-                pltpu.VMEM((2, rows, length), bf16),
+                pltpu.VMEM((2, rows, LANES), f32),
                 pltpu.VMEM((rows * n_seqs, depth), f32),
                 pltpu.VMEM((N_PARTS, N_CHIPS, n_steps, part_seqs, chip_width), bf16),
                 pltpu.VMEM((N_PARTS, N_CORES, N_CHIPS, n_steps, part_seqs, chip_width), bf16),
@@ -448,8 +468,8 @@
                 pltpu.VMEM((N_PARTS, n_steps, N_CHIPS, block, half), bf16),
                 pltpu.VMEM((N_PARTS, n_steps, 2, block, half // 2), bf16),
                 pltpu.VMEM((N_PARTS, n_steps, 4, block, half // 2), bf16),
-                dma((n_steps,)), dma((3,)), dma((2, n_seqs)), dma((2,)),
-                dma((n_steps, n_dev - 1)), dma((n_steps, n_dev - 1)),
+                dma((2 * N_PARTS,)), dma((4,)), dma((2, n_seqs)), dma((2,)),
+                dma((N_PARTS, n_dev - 1)), dma((N_PARTS, n_dev - 1)),
                 dma((N_PARTS, 3)), dma((N_PARTS, 3)),
                 dma((N_PARTS, N_CHIPS)), dma((N_PARTS, N_CHIPS)),
                 dma((N_PARTS, n_steps, 6)), dma((N_PARTS, n_steps, 6)),
@@ -458,7 +478,7 @@
             compiler_params=pltpu.CompilerParams(vmem_limit_bytes=BLOCK_VMEM, collective_id=1, has_side_effects=True),
             cost_estimate=pl.CostEstimate(flops=4 * n_seqs * rows * length * depth, bytes_accessed=4 * n_seqs * length * depth, transcendentals=n_seqs * rows * length),
         )(seq_lens, ln_gain, ln_bias, b_q, b_kv, b_out,
-          x_steps, w_q, w_kv, w_out, k_cache, v_cache)
+          x_steps.reshape(n_steps, n_dev, N_PARTS, part_seqs, width), w_q, w_kv, w_out, k_cache, v_cache)
         y_steps, k_out, v_out, _, _ = pl.pallas_call(
             functools.partial(store_kernel, n_steps),
             out_shape=[jax.ShapeDtypeStruct(y_shape, bf16), jax.ShapeDtypeStruct(k_cache.shape, bf16), jax.ShapeDtypeStruct(v_cache.shape, bf16), pltpu.VMEM(k_cache.shape, bf16), pltpu.VMEM(v_cache.shape, bf16)],

time: 77.4 us -> 73.9 us (0.955)
  Pallas kernels: 76.6 us -> 73.1 us
    pallas_call x1, Pallas kernels: 66.4 us -> 62.9 us  [local_block(): pl.pallas_call(block_kernel, out_shape=[pltpu.VMEM(y_shape, bf16), pltpu....]
where the time goes in v8:
time: 73.9 us; the launch traced here: 73.7 us
  Pallas kernels  73.1 us (99%)
    pallas_call x1, Pallas kernels, local_block(): pl.pallas_call(block_kernel, out_shape=[pltpu.VMEM(y_shape, bf16), pltpu....  62.9 us
    pallas_call x1, Pallas kernels, local_block(): pl.pallas_call(functools.partial(store_kernel, n_steps), out_shape=[jax.S...  10.1 us

profile of v8, /device:TPU:113, one launch (start us, length us, event | category | flops | bytes accessed | tf_op | source)
XLA Modules:
  0.0 73.7 jit_solution(1320289827487394765)
XLA Ops:
  0.6 0.0 copy-start
  0.6 62.9 %shard_map.139 = (bf16[3,4,2,2,8,4096]{5,4,3,2,1,0:T(8,128)(2,1)S(1)}, bf16[16,3072,128]{2,1,0:T(8,128)(2,1)S(1)}, bf16[16,3072,128]{2,1,0:T(8,128)(2,1)S(1)}, f32[256,128]{1,0:T(8,128)S(1)}, f32[256,128]{1,0:T(8,128)S(1)}) custom-call(s32[16]{0:T(128)} %len_ref.3, bf16[4096]{0:T(1024)(128)(2,1)} %g_ref.1, bf16[4096]{0:T(1024)(128)(2,1)} %lb_ref.1, ...), custom_call_target="tpu_custom_call" | custom-call | flops 2415919104 | bytes 25165824 | tf_op jit(solution)/shard_map/pallas_call | solution.py:442
  63.6 0.0 copy-done
  63.6 10.1 %shard_map.140 = (bf16[3,4,2,2,8,4096]{5,4,3,2,1,0:T(8,128)(2,1)}, bf16[16,3072,128]{2,1,0:T(8,128)(2,1)}, bf16[16,3072,128]{2,1,0:T(8,128)(2,1)}, bf16[16,3072,...) custom-call(s32[16]{0:T(128)S(1)} %copy-done, ...), custom_call_target="tpu_custom_call", output_to_operand_aliasing={{3}: (4, {}), {4}: (5, {})} | custom-call | tf_op jit(solution)/shard_map/pallas_call | solution.py:482
Async XLA Ops:
  0.6 63.0 %copy-start = (s32[16]{0:T(128)S(1)}, s32[16]{0:T(128)}, u32[]{:S(2)}) copy-start(s32[16]{0:T(128)} %len_ref.3) | copy-start | bytes 196

commit v9 on v8

--- a/solution.py
+++ b/solution.py
@@ -52,10 +52,10 @@
 
 
 def block_kernel(
-        len_ref, g_ref, lb_ref, bq_ref, bkv_ref, bo_ref, x_hbm, wq_hbm, wkv_hbm, wo_hbm, k_hbm, v_hbm,
+        len_hbm, g_hbm, lb_hbm, bq_hbm, bkv_hbm, bo_hbm, x_hbm, wq_hbm, wkv_hbm, wo_hbm, k_hbm, v_hbm,
         y_ref, k_buf, v_buf, fk_ref, fv_ref,
-        x_buf, own_x, own_h, h_buf, gain_buf, bias_buf, bo_buf, wq_buf, wkv_buf, w_buf, swap_buf, q_buf, q_in, q_rows, score_buf, best_buf, head_buf, a_src, a_buf, lhs_buf, p_buf, mid_buf, fin_buf,
-        x_sems, w_sems, kv_sems, swap_sems, q_send, q_recv, a_send, a_recv, f_send, f_recv, rs_send, rs_recv, ag_send, ag_recv):
+        len_ref, g_ref, lb_ref, bq_ref, bkv_ref, bo_ref, x_buf, own_x, own_h, h_buf, gain_buf, bias_buf, bo_buf, wq_buf, wkv_buf, w_buf, swap_buf, q_buf, q_in, q_rows, score_buf, best_buf, head_buf, a_src, a_buf, lhs_buf, p_buf, mid_buf, fin_buf,
+        vec_sems, x_sems, w_sems, kv_sems, swap_sems, q_send, q_recv, a_send, a_recv, f_send, f_recv, rs_send, rs_recv, ag_send, ag_recv):
     me = lax.axis_index('tp')
     n_dev = N_CHIPS * N_CORES
     chip, core = me // N_CORES, me % N_CORES
@@ -87,10 +87,6 @@
     def cols(which, begin, size):
         return pl.ds(pl.multiple_of(which * half + begin, quarter), size)
 
-    barrier = pltpu.get_barrier_semaphore()
-    for d in range(1, n_dev):
-        pl.semaphore_signal(barrier, inc=1, device_id={'tp': member(d)}, device_id_type=MESH)
-
     def x_load(p):
         return pltpu.make_async_copy(x_hbm.at[:, :, p], x_buf.at[p], x_sems.at[p])
 
@@ -105,8 +101,19 @@
     wo_load = pltpu.make_async_copy(wo_hbm.at[:, cols(core, 0, half)], w_buf.at[own_w_rows, :], w_sems.at[2])
     swap_load = pltpu.make_async_copy(wo_hbm.at[:, cols(1 - core, 0, half)], swap_buf, w_sems.at[3])
     wo_swap = remote(swap_buf, w_buf.at[own_w_rows, :], swap_sems.at[0], swap_sems.at[1], partner)
+    vector_loads = [pltpu.make_async_copy(src, dst, vec_sems.at[i]) for i, (src, dst) in enumerate(
+        ((g_hbm, g_ref), (lb_hbm, lb_ref), (bq_hbm, bq_ref), (bkv_hbm, bkv_ref), (bo_hbm, bo_ref), (len_hbm, len_ref)))]
+    for copy in vector_loads:
+        copy.start()
     x_load(0).start()
     wq_load.start()
+
+    barrier = pltpu.get_barrier_semaphore()
+    for d in range(1, n_dev):
+        pl.semaphore_signal(barrier, inc=1, device_id={'tp': member(d)}, device_id_type=MESH)
+
+    for copy in vector_loads:
+        copy.wait()
 
     bq_row = bq_ref[...].astype(jnp.float32).reshape(1, q_width)
     bo_buf[...] = bo_ref[...].astype(jnp.float32).reshape(1, width)
@@ -442,9 +449,15 @@
         y_vm, k_vm, v_vm, fresh_k, fresh_v = pl.pallas_call(
             block_kernel,
             out_shape=[pltpu.VMEM(y_shape, bf16), pltpu.VMEM(k_cache.shape, bf16), pltpu.VMEM(v_cache.shape, bf16), pltpu.VMEM(fresh_shape, f32), pltpu.VMEM(fresh_shape, f32)],
-            in_specs=[smem] + [vmem] * 5 + [hbm] * 6,
+            in_specs=[hbm] * 12,
             out_specs=[vmem] * 5,
             scratch_shapes=[
+                pltpu.SMEM(seq_lens.shape, jnp.int32),
+                pltpu.VMEM(ln_gain.shape, bf16),
+                pltpu.VMEM(ln_bias.shape, bf16),
+                pltpu.VMEM(b_q.shape, bf16),
+                pltpu.VMEM(b_kv.shape, bf16),
+                pltpu.VMEM(b_out.shape, bf16),
                 pltpu.VMEM((N_PARTS, n_steps, n_dev, part_seqs, width), bf16),
                 pltpu.VMEM((n_steps, n_seqs, width), bf16),
                 pltpu.VMEM((n_steps * n_seqs, width), bf16),
@@ -468,7 +481,7 @@
                 pltpu.VMEM((N_PARTS, n_steps, N_CHIPS, block, half), bf16),
                 pltpu.VMEM((N_PARTS, n_steps, 2, block, half // 2), bf16),
                 pltpu.VMEM((N_PARTS, n_steps, 4, block, half // 2), bf16),
-                dma((2 * N_PARTS,)), dma((4,)), dma((2, n_seqs)), dma((2,)),
+                dma((6,)), dma((2 * N_PARTS,)), dma((4,)), dma((2, n_seqs)), dma((2,)),
                 dma((N_PARTS, n_dev - 1)), dma((N_PARTS, n_dev - 1)),
                 dma((N_PARTS, 3)), dma((N_PARTS, 3)),
                 dma((N_PARTS, N_CHIPS)), dma((N_PARTS, N_CHIPS)),

time: 73.9 us -> 73 us (0.988)
  Pallas kernels: 73.1 us -> 72.2 us
    pallas_call x1, Pallas kernels: 62.9 us -> 62.1 us  [local_block(): pl.pallas_call(block_kernel, out_shape=[pltpu.VMEM(y_shape, bf16), pltpu....]
where the time goes in v9:
time: 73 us; the launch traced here: 72.9 us
  Pallas kernels  72.2 us (99%)
    pallas_call x1, Pallas kernels, local_block(): pl.pallas_call(block_kernel, out_shape=[pltpu.VMEM(y_shape, bf16), pltpu....  62.1 us
    pallas_call x1, Pallas kernels, local_block(): pl.pallas_call(functools.partial(store_kernel, n_steps), out_shape=[jax.S...  10.1 us

profile of v9, /device:TPU:113, one launch (start us, length us, event | category | flops | bytes accessed | tf_op | source)
XLA Modules:
  0.0 72.9 jit_solution(397610121064000017)
XLA Ops:
  0.6 0.0 copy-start
  0.6 62.1 %shard_map.139 = (bf16[3,4,2,2,8,4096]{5,4,3,2,1,0:T(8,128)(2,1)S(1)}, bf16[16,3072,128]{2,1,0:T(8,128)(2,1)S(1)}, bf16[16,3072,128]{2,1,0:T(8,128)(2,1)S(1)}, f32[256,128]{1,0:T(8,128)S(1)}, f32[256,128]{1,0:T(8,128)S(1)}) custom-call(s32[16]{0:T(128)} %len_ref.1, bf16[4096]{0:T(1024)(128)(2,1)} %g_hbm.1, bf16[4096]{0:T(1024)(128)(2,1)} %lb_hbm.1, ...), custom_call_target="tpu_custom_call" | custom-call | flops 2415919104 | bytes 25165824 | tf_op jit(solution)/shard_map/pallas_call | solution.py:449
  62.7 0.0 copy-done
  62.7 10.1 %shard_map.140 = (bf16[3,4,2,2,8,4096]{5,4,3,2,1,0:T(8,128)(2,1)}, bf16[16,3072,128]{2,1,0:T(8,128)(2,1)}, bf16[16,3072,128]{2,1,0:T(8,128)(2,1)}, bf16[16,3072,...) custom-call(s32[16]{0:T(128)S(1)} %copy-done, ...), custom_call_target="tpu_custom_call", output_to_operand_aliasing={{3}: (4, {}), {4}: (5, {})} | custom-call | tf_op jit(solution)/shard_map/pallas_call | solution.py:495
Async XLA Ops:
  0.6 62.1 %copy-start = (s32[16]{0:T(128)S(1)}, s32[16]{0:T(128)}, u32[]{:S(2)}) copy-start(s32[16]{0:T(128)} %len_ref.1) | copy-start | bytes 196

commit v10 on v9

--- a/solution.py
+++ b/solution.py
@@ -41,13 +41,14 @@
     top = jnp.maximum(jnp.max(best, axis=-1, keepdims=True), jnp.max(new_scores, axis=-1, keepdims=True))
     new_weights = jnp.exp2((new_scores - top) * to_log2)
     numerator = jnp.dot(new_weights.astype(jnp.bfloat16), fresh_v, preferred_element_type=jnp.float32)
-    total = None
+    total, pieces = None, []
     for start in range(0, length, KEY_TILE):
         beside(start)
         weights = jnp.exp2((score_ref[:, start:start + KEY_TILE] - top) * to_log2)
         folded = weights[:, :LANES] + weights[:, LANES:]
         total = folded if total is None else total + folded
-        numerator = numerator + jnp.dot(weights.astype(jnp.bfloat16), v_ref[start:start + KEY_TILE, :], preferred_element_type=jnp.float32)
+        pieces.append(weights.astype(jnp.bfloat16))
+    numerator = numerator + jnp.dot(jnp.concatenate(pieces, axis=1), v_ref[...], preferred_element_type=jnp.float32)
     return numerator / (jnp.sum(total, axis=-1, keepdims=True) + jnp.sum(new_weights, axis=-1, keepdims=True))
 
 

time: 73 us -> 71.4 us (0.978)
  Pallas kernels: 72.2 us -> 70.6 us
    pallas_call x1, Pallas kernels: 62.1 us -> 60.5 us  [local_block(): pl.pallas_call(block_kernel, out_shape=[pltpu.VMEM(y_shape, bf16), pltpu....]
where the time goes in v10:
time: 71.4 us; the launch traced here: 71.3 us
  Pallas kernels  70.6 us (99%)
    pallas_call x1, Pallas kernels, local_block(): pl.pallas_call(block_kernel, out_shape=[pltpu.VMEM(y_shape, bf16), pltpu....  60.5 us
    pallas_call x1, Pallas kernels, local_block(): pl.pallas_call(functools.partial(store_kernel, n_steps), out_shape=[jax.S...  10.1 us

profile of v10, /device:TPU:113, one launch (start us, length us, event | category | flops | bytes accessed | tf_op | source)
XLA Modules:
  0.0 71.3 jit_solution(5013251746603941557)
XLA Ops:
  0.6 0.0 copy-start
  0.6 60.5 %shard_map.139 = (bf16[3,4,2,2,8,4096]{5,4,3,2,1,0:T(8,128)(2,1)S(1)}, bf16[16,3072,128]{2,1,0:T(8,128)(2,1)S(1)}, bf16[16,3072,128]{2,1,0:T(8,128)(2,1)S(1)}, f32[256,128]{1,0:T(8,128)S(1)}, f32[256,128]{1,0:T(8,128)S(1)}) custom-call(s32[16]{0:T(128)} %len_ref.1, bf16[4096]{0:T(1024)(128)(2,1)} %g_hbm.1, bf16[4096]{0:T(1024)(128)(2,1)} %lb_hbm.1, ...), custom_call_target="tpu_custom_call" | custom-call | flops 2415919104 | bytes 25165824 | tf_op jit(solution)/shard_map/pallas_call | solution.py:450
  61.1 0.0 copy-done
  61.1 10.1 %shard_map.140 = (bf16[3,4,2,2,8,4096]{5,4,3,2,1,0:T(8,128)(2,1)}, bf16[16,3072,128]{2,1,0:T(8,128)(2,1)}, bf16[16,3072,128]{2,1,0:T(8,128)(2,1)}, bf16[16,3072,...) custom-call(s32[16]{0:T(128)S(1)} %copy-done, ...), custom_call_target="tpu_custom_call", output_to_operand_aliasing={{3}: (4, {}), {4}: (5, {})} | custom-call | tf_op jit(solution)/shard_map/pallas_call | solution.py:496
Async XLA Ops:
  0.6 60.5 %copy-start = (s32[16]{0:T(128)S(1)}, s32[16]{0:T(128)}, u32[]{:S(2)}) copy-start(s32[16]{0:T(128)} %len_ref.1) | copy-start | bytes 196

commit v11 on v10

--- a/solution.py
+++ b/solution.py
@@ -11,6 +11,7 @@
 LN_EPS = 1e-5
 KEY_TILE = 256
 LANES = 128
+Q_TILE = 256
 FRESH_ROWS = 16
 WINDOW = 16
 N_CHIPS = 4
@@ -127,8 +128,9 @@
         scaled = centered * lax.rsqrt(row_var + LN_EPS)
         return (scaled * gain_buf[...] + bias_buf[...]).astype(h_buf.dtype)
 
-    def q_copy(p, d):
-        return remote(q_buf.at[p, :, member(d)], q_in.at[p, me], q_send.at[p, d - 1], q_recv.at[p, d - 1], {'tp': member(d)})
+    def q_copy(p, n, d):
+        where = pl.ds(n * Q_TILE, Q_TILE)
+        return remote(q_buf.at[p, :, member(d), :, where], q_in.at[p, me, :, :, where], q_send.at[p, n, d - 1], q_recv.at[p, n, d - 1], {'tp': member(d)})
 
     group = LN_ROWS // part_seqs
     for p in range(N_PARTS):
@@ -152,16 +154,17 @@
             wq_load.wait()
             swap_load.start()
             wo_load.start()
-        for n in range(0, q_width, 256):
-            part = jnp.dot(h_buf[p], wq_buf[:, n:n + 256], preferred_element_type=jnp.float32) + bq_row[:, n:n + 256]
+        for n in range(q_width // Q_TILE):
+            where = slice(n * Q_TILE, (n + 1) * Q_TILE)
+            part = jnp.dot(h_buf[p], wq_buf[:, where], preferred_element_type=jnp.float32) + bq_row[:, where]
             for s in range(n_steps):
                 for u in range(n_dev):
                     first = (s * n_dev + u) * part_seqs
-                    q_buf[p, s, u, :, n:n + 256] = part[first:first + part_seqs].astype(q_buf.dtype)
-        if p == 0:
-            pl.semaphore_wait(barrier, n_dev - 1)
-        for d in range(1, n_dev):
-            q_copy(p, d).start()
+                    q_buf[p, s, u, :, where] = part[first:first + part_seqs].astype(q_buf.dtype)
+            if p == 0 and n == 0:
+                pl.semaphore_wait(barrier, n_dev - 1)
+            for d in range(1, n_dev):
+                q_copy(p, n, d).start()
         if p == 0:
             swap_load.wait()
             wo_swap.start()
@@ -185,8 +188,9 @@
         fv_ref[where, :] = fresh[s * n_seqs:(s + 1) * n_seqs, depth:]
 
     def unpack(p):
-        for d in range(1, n_dev):
-            q_copy(p, d).wait_recv()
+        for n in range(q_width // Q_TILE):
+            for d in range(1, n_dev):
+                q_copy(p, n, d).wait_recv()
         for u in range(n_dev):
             for s in range(n_steps):
                 for h in range(dev_heads):
@@ -386,8 +390,9 @@
     each(last, 1)
     wo_swap.wait_send()
     for p in range(N_PARTS):
-        for d in range(1, n_dev):
-            q_copy(p, d).wait_send()
+        for n in range(q_width // Q_TILE):
+            for d in range(1, n_dev):
+                q_copy(p, n, d).wait_send()
         for s in range(n_steps):
             for i in range(4, 9):
                 ag(p, s, i).wait_recv()
@@ -483,7 +488,7 @@
                 pltpu.VMEM((N_PARTS, n_steps, 2, block, half // 2), bf16),
                 pltpu.VMEM((N_PARTS, n_steps, 4, block, half // 2), bf16),
                 dma((6,)), dma((2 * N_PARTS,)), dma((4,)), dma((2, n_seqs)), dma((2,)),
-                dma((N_PARTS, n_dev - 1)), dma((N_PARTS, n_dev - 1)),
+                dma((N_PARTS, q_width // Q_TILE, n_dev - 1)), dma((N_PARTS, q_width // Q_TILE, n_dev - 1)),
                 dma((N_PARTS, 3)), dma((N_PARTS, 3)),
                 dma((N_PARTS, N_CHIPS)), dma((N_PARTS, N_CHIPS)),
                 dma((N_PARTS, n_steps, 6)), dma((N_PARTS, n_steps, 6)),

time: 71.4 us -> 73.4 us (1.028)
  Pallas kernels: 70.6 us -> 72.6 us
    pallas_call x1, Pallas kernels: 60.5 us -> 62.5 us  [local_block(): pl.pallas_call(block_kernel, out_shape=[pltpu.VMEM(y_shape, bf16), pltpu....]
where the time goes in v11:
time: 73.4 us; the launch traced here: 73.3 us
  Pallas kernels  72.6 us (99%)
    pallas_call x1, Pallas kernels, local_block(): pl.pallas_call(block_kernel, out_shape=[pltpu.VMEM(y_shape, bf16), pltpu....  62.5 us
    pallas_call x1, Pallas kernels, local_block(): pl.pallas_call(functools.partial(store_kernel, n_steps), out_shape=[jax.S...  10.1 us

profile of v11, /device:TPU:113, one launch (start us, length us, event | category | flops | bytes accessed | tf_op | source)
XLA Modules:
  0.0 73.3 jit_solution(8571865713782735823)
XLA Ops:
  0.6 0.0 copy-start
  0.6 62.5 %shard_map.139 = (bf16[3,4,2,2,8,4096]{5,4,3,2,1,0:T(8,128)(2,1)S(1)}, bf16[16,3072,128]{2,1,0:T(8,128)(2,1)S(1)}, bf16[16,3072,128]{2,1,0:T(8,128)(2,1)S(1)}, f32[256,128]{1,0:T(8,128)S(1)}, f32[256,128]{1,0:T(8,128)S(1)}) custom-call(s32[16]{0:T(128)} %len_ref.1, bf16[4096]{0:T(1024)(128)(2,1)} %g_hbm.1, bf16[4096]{0:T(1024)(128)(2,1)} %lb_hbm.1, ...), custom_call_target="tpu_custom_call" | custom-call | flops 2415919104 | bytes 25165824 | tf_op jit(solution)/shard_map/pallas_call | solution.py:455
  63.1 0.0 copy-done
  63.1 10.1 %shard_map.140 = (bf16[3,4,2,2,8,4096]{5,4,3,2,1,0:T(8,128)(2,1)}, bf16[16,3072,128]{2,1,0:T(8,128)(2,1)}, bf16[16,3072,128]{2,1,0:T(8,128)(2,1)}, bf16[16,3072,...) custom-call(s32[16]{0:T(128)S(1)} %copy-done, ...), custom_call_target="tpu_custom_call", output_to_operand_aliasing={{3}: (4, {}), {4}: (5, {})} | custom-call | tf_op jit(solution)/shard_map/pallas_call | solution.py:501
Async XLA Ops:
  0.6 62.5 %copy-start = (s32[16]{0:T(128)S(1)}, s32[16]{0:T(128)}, u32[]{:S(2)}) copy-start(s32[16]{0:T(128)} %len_ref.1) | copy-start | bytes 196

commit v12 on v10

--- a/solution.py
+++ b/solution.py
@@ -377,12 +377,12 @@
     forward(1)
     each(middle, 0)
     partial(1)
+    each(middle, 1)
     each(finish, 0)
-    each(middle, 1)
+    each(finish, 1)
     each(relay, 0)
-    each(finish, 1)
+    each(relay, 1)
     each(last, 0)
-    each(relay, 1)
     each(last, 1)
     wo_swap.wait_send()
     for p in range(N_PARTS):

time: 71.4 us -> 69.9 us (0.979)
  Pallas kernels: 70.6 us -> 69.2 us
    pallas_call x1, Pallas kernels: 60.5 us -> 59 us  [local_block(): pl.pallas_call(block_kernel, out_shape=[pltpu.VMEM(y_shape, bf16), pltpu....]
where the time goes in v12:
time: 69.9 us; the launch traced here: 69.8 us
  Pallas kernels  69.2 us (99%)
    pallas_call x1, Pallas kernels, local_block(): pl.pallas_call(block_kernel, out_shape=[pltpu.VMEM(y_shape, bf16), pltpu....  59 us
    pallas_call x1, Pallas kernels, local_block(): pl.pallas_call(functools.partial(store_kernel, n_steps), out_shape=[jax.S...  10.1 us

profile of v12, /device:TPU:113, one launch (start us, length us, event | category | flops | bytes accessed | tf_op | source)
XLA Modules:
  0.0 69.8 jit_solution(1010981508163154841)
XLA Ops:
  0.6 0.0 copy-start
  0.6 59.0 %shard_map.139 = (bf16[3,4,2,2,8,4096]{5,4,3,2,1,0:T(8,128)(2,1)S(1)}, bf16[16,3072,128]{2,1,0:T(8,128)(2,1)S(1)}, bf16[16,3072,128]{2,1,0:T(8,128)(2,1)S(1)}, f32[256,128]{1,0:T(8,128)S(1)}, f32[256,128]{1,0:T(8,128)S(1)}) custom-call(s32[16]{0:T(128)} %len_ref.1, bf16[4096]{0:T(1024)(128)(2,1)} %g_hbm.1, bf16[4096]{0:T(1024)(128)(2,1)} %lb_hbm.1, ...), custom_call_target="tpu_custom_call" | custom-call | flops 2415919104 | bytes 25165824 | tf_op jit(solution)/shard_map/pallas_call | solution.py:450
  59.7 0.0 copy-done
  59.7 10.1 %shard_map.140 = (bf16[3,4,2,2,8,4096]{5,4,3,2,1,0:T(8,128)(2,1)}, bf16[16,3072,128]{2,1,0:T(8,128)(2,1)}, bf16[16,3072,128]{2,1,0:T(8,128)(2,1)}, bf16[16,3072,...) custom-call(s32[16]{0:T(128)S(1)} %copy-done, ...), custom_call_target="tpu_custom_call", output_to_operand_aliasing={{3}: (4, {}), {4}: (5, {})} | custom-call | tf_op jit(solution)/shard_map/pallas_call | solution.py:496
Async XLA Ops:
  0.6 59.0 %copy-start = (s32[16]{0:T(128)S(1)}, s32[16]{0:T(128)}, u32[]{:S(2)}) copy-start(s32[16]{0:T(128)} %len_ref.1) | copy-start | bytes 196
